TPU v7x, 512 devices: a whole 4x4x16 slice. The times are simulated.
512 devices in a mesh: outer: 32 (over y, z_hi, core), inner: 16 (over z_lo, x).
Axes of the slice: x: 4, y: 4, z: 16 (z_hi: 4, z_lo: 4; z = z_hi * 4 + z_lo), core: 2. Of those that a mesh axis runs over, the one named last changes fastest.
Arguments:
- group_latents: bfloat16 [65536, 1024], P(('outer', 'inner')), may hold values from -6 to 6
- slot_ids: int32 [32, 16], P('outer', 'inner'), may hold values from 0 to 15, each once within a row
- slot_embed: bfloat16 [16, 1024], replicated, may hold values from -6 to 6
- merge_latents: bfloat16 [128, 2048], replicated, may hold values from -6 to 6
- query_weight: bfloat16 [2048, 2048], P(None, 'inner'), may hold values from -0.125 to 0.125
- key_weight: bfloat16 [1024, 2048], P(None, 'inner'), may hold values from -0.1875 to 0.1875
- value_weight: bfloat16 [1024, 2048], P(None, 'inner'), may hold values from -0.1875 to 0.1875
- output_weight: bfloat16 [2048, 2048], P('inner'), may hold values from -0.125 to 0.125
- global_latents: bfloat16 [1024, 2048], P(('outer', 'inner')), may hold values from -6 to 6
- decode_query: bfloat16 [2048, 2048], P(None, 'inner'), may hold values from -0.125 to 0.125
- decode_key: bfloat16 [2048, 2048], P(None, 'inner'), may hold values from -0.125 to 0.125
- decode_value: bfloat16 [2048, 2048], P(None, 'inner'), may hold values from -0.125 to 0.125
- decode_output: bfloat16 [2048, 2048], P('inner'), may hold values from -0.125 to 0.125
Outputs:
- decoded: bfloat16 [4096, 2048], P(('outer', 'inner'))
Inputs may be any that keep to these rules, and one draw needn't show every extreme that they name: `slot_ids`: each row holds every slot once.
All inputs are finite; a program needn't handle non-finite values.
Results may differ from a plain program's by a relative error of at most 0.014.
Values may be sent and summed in bfloat16 or wider, within the bound.
No kernel may reach another device: no remote copies, remote signals or barrier semaphores. Data moves between devices by JAX's collectives and lax.ppermute only.
A program may use at most 64 MiB of HBM per device.

v0:
```python
import functools

import jax
import jax.numpy as jnp
from jax import lax
from jax.experimental import pallas as pl
from jax.experimental.pallas import tpu as pltpu
from jax.sharding import Mesh
from jax.sharding import PartitionSpec as P


HEAD = 128
AXES = ("y", "h", "c", "z", "x")
INNER = ("z", "x")
OUTER = ("y", "h", "c")
ALL = OUTER + INNER
BF16 = jnp.bfloat16
F32 = jnp.float32
SCALE = HEAD ** (-0.5)
TAIL = 16
PARAMS = pltpu.CompilerParams(vmem_limit_bytes=20 * 2**20)


VMEM = pl.BlockSpec(memory_space=pltpu.VMEM)


def dot(a, b, dims):
    return lax.dot_general(a, b, (dims, ((), ())), preferred_element_type=F32)


def partner(value, axis, step):
    pairs = [(i, i ^ step) for i in range(lax.axis_size(axis))]
    return lax.ppermute(value, axis, pairs)


def exchange(tiles, axis):
    return lax.all_to_all(tiles, axis, split_axis=0, concat_axis=0, tiled=True)


def all_from(value, axis):
    copies = jnp.broadcast_to(value, (lax.axis_size(axis), *value.shape))
    return exchange(copies, axis)


def cost(flops, size):
    return pl.CostEstimate(flops=flops, bytes_accessed=size, transcendentals=0)


def attend_kernel(*refs):
    blocks, packs, out_ref = refs[:4], refs[4:8], refs[8]
    mine = lax.axis_index("x")
    for step, pack_ref in enumerate(packs):
        place = mine ^ step
        pack = pack_ref[...]
        both = [dot(block[...], pack, ((1,), (0,))) for block in blocks]
        scores = jnp.concatenate([b[:, :HEAD] for b in both], axis=0) * SCALE
        values = jnp.concatenate([b[:, HEAD:].astype(BF16) for b in both], axis=0)
        top = jnp.max(scores, axis=0, keepdims=True)
        weights = jnp.exp(scores - top)
        total = jnp.sum(weights, axis=0, keepdims=True)
        mixed = dot(values, weights.astype(BF16), ((0,), (0,))) / total
        level = top + jnp.log(total)
        high = level.astype(BF16).astype(F32)
        middle = (level - high).astype(BF16).astype(F32)
        low = level - high - middle
        line = lax.broadcasted_iota(jnp.int32, (TAIL, mixed.shape[1]), 0)
        tail = jnp.where(line == 0, high, jnp.where(line == 1, middle, jnp.where(line == 2, low, 0.0)))
        out_ref[place] = jnp.concatenate([mixed, tail], axis=0).astype(BF16)


def attend_part(blocks, packs, length):
    many = len(packs)
    keys = sum(b.shape[0] for b in blocks)
    flops = 2 * many * keys * (blocks[0].shape[1] * 2 * HEAD + HEAD * length)
    return pl.pallas_call(
        attend_kernel,
        out_shape=jax.ShapeDtypeStruct((many, HEAD + TAIL, length), BF16),
        in_specs=[VMEM] * (len(blocks) + many),
        out_specs=VMEM,
        compiler_params=PARAMS,
        cost_estimate=cost(flops, 3 * 2**20),
        name="attend_part",
    )(*blocks, *packs)


def join_kernel(parts_ref, weight_ref, out_ref):
    many = parts_ref.shape[0]
    levels = [
        jnp.sum(parts_ref[j, HEAD:, :].astype(F32), axis=0, keepdims=True) for j in range(many)
    ]
    top = functools.reduce(jnp.maximum, levels)
    shares = [jnp.exp(level - top) for level in levels]
    total = functools.reduce(jnp.add, shares)
    mixed = functools.reduce(
        jnp.add, [parts_ref[j, :HEAD, :].astype(F32) * (shares[j] / total) for j in range(many)]
    )
    out_ref[...] = dot(mixed.astype(BF16), weight_ref[...], ((0,), (0,))).astype(BF16)


def join_and_project(parts, weight):
    length, width = parts.shape[2], weight.shape[1]
    return pl.pallas_call(
        join_kernel,
        out_shape=jax.ShapeDtypeStruct((length, width), BF16),
        in_specs=[VMEM, VMEM],
        out_specs=VMEM,
        compiler_params=PARAMS,
        cost_estimate=cost(2 * length * width * HEAD, 2**20),
        name="join_and_project",
    )(parts, weight)


def norm_kernel(parts_ref, own_ref, level_ref, copies_ref):
    many = parts_ref.shape[0]
    level = own_ref[...].astype(F32) + functools.reduce(
        jnp.add, [parts_ref[j].astype(F32) for j in range(many)]
    )
    level_ref[...] = level
    scale = lax.rsqrt(jnp.mean(level * level, axis=-1, keepdims=True) + 1e-06)
    normed = (level * scale).astype(BF16)
    for j in range(many):
        copies_ref[j] = normed


def sum_and_norm(parts, own):
    return pl.pallas_call(
        norm_kernel,
        out_shape=[
            jax.ShapeDtypeStruct(own.shape, F32),
            jax.ShapeDtypeStruct(parts.shape, BF16),
        ],
        in_specs=[VMEM, VMEM],
        out_specs=[VMEM, VMEM],
        compiler_params=PARAMS,
        cost_estimate=cost(4 * parts.size, 2**20),
        name="sum_and_norm",
    )(parts, own)


def last_kernel(parts_ref, level_ref, out_ref):
    total = functools.reduce(
        jnp.add, [parts_ref[j].astype(F32) for j in range(parts_ref.shape[0])]
    )
    out_ref[...] = (level_ref[...] + total).astype(BF16)


def last_sum(parts, level):
    return pl.pallas_call(
        last_kernel,
        out_shape=jax.ShapeDtypeStruct(level.shape, BF16),
        in_specs=[VMEM, VMEM],
        out_specs=VMEM,
        compiler_params=PARAMS,
        cost_estimate=cost(parts.size, 2**20),
        name="last_sum",
    )(parts, level)


def step(
    group_latents,
    slot_ids,
    slot_embed,
    merge_latents,
    query_weight,
    key_weight,
    value_weight,
    output_weight,
    global_latents,
    decode_query,
    decode_key,
    decode_value,
    decode_output,
):
    inner = lax.axis_size(INNER)
    length, width = merge_latents.shape
    rows = length // inner

    query_two = dot(merge_latents, query_weight, ((1,), (0,))).astype(BF16)
    folded = dot(key_weight, query_two, ((1,), (1,))).astype(BF16)
    pack = jnp.concatenate([folded, value_weight], axis=1)
    slot_row = lax.dynamic_slice_in_dim(slot_embed, slot_ids[0, 0], 1, 0)
    keyed = (group_latents.astype(F32) + slot_row.astype(F32)).astype(BF16)
    own_rows = lax.dynamic_slice_in_dim(merge_latents, lax.axis_index(INNER) * rows, rows, 0)

    pack_two = partner(pack, "x", 2)
    keyed_three = partner(keyed, "z", 3)
    outer_block = all_from(global_latents, INNER).reshape(-1, width)
    pack_three = partner(pack, "x", 3)
    keyed_two = partner(keyed, "z", 2)
    pack_one = partner(pack, "x", 1)
    keyed_one = partner(keyed, "z", 1)

    pairs = jnp.concatenate(
        [
            dot(outer_block, decode_key, ((1,), (0,))).astype(BF16),
            dot(outer_block, decode_value, ((1,), (0,))).astype(BF16),
        ],
        axis=1,
    )
    for axis, step_size in (("h", 1), ("h", 2), ("y", 1), ("y", 2)):
        if lax.axis_size(axis) > step_size:
            pairs = jnp.concatenate([pairs, partner(pairs, axis, step_size)], axis=0)
    other = partner(pairs, "c", 1)

    parts = attend_part(
        [keyed, keyed_one, keyed_two, keyed_three],
        [pack, pack_one, pack_two, pack_three],
        length,
    )
    parts = exchange(parts, "x")
    partial = join_and_project(parts, output_weight)
    arrived = exchange(partial.reshape(inner, rows, width), INNER)
    level_two, copies = sum_and_norm(arrived, own_rows)
    normed = exchange(copies, INNER).reshape(length, width)

    query_five = dot(normed, decode_query, ((1,), (0,))).astype(BF16)
    pairs = jnp.concatenate([pairs, other], axis=0)
    scores = dot(pairs[:, :HEAD], query_five, ((1,), (1,))) * SCALE
    top = jnp.max(scores, axis=0, keepdims=True)
    weights = jnp.exp(scores - top)
    total = jnp.sum(weights, axis=0, keepdims=True)
    weights = weights.astype(BF16)
    mixed_five = (dot(pairs[:, HEAD:], weights, ((0,), (0,))) / total).astype(BF16)
    partial = dot(mixed_five, decode_output, ((0,), (0,))).astype(BF16)
    arrived = exchange(partial.reshape(inner, rows, width), INNER)
    return last_sum(arrived, level_two)


def solution(mesh):
    outer, inner = mesh.shape["outer"], mesh.shape["inner"]
    finer = Mesh(mesh.devices.reshape(outer // 8, 4, 2, inner // 4, 4), AXES)
    placed = (
        P(ALL, None),
        P(OUTER, INNER),
        P(),
        P(),
        P(None, INNER),
        P(None, INNER),
        P(None, INNER),
        P(INNER, None),
        P(ALL, None),
        P(None, INNER),
        P(None, INNER),
        P(None, INNER),
        P(INNER, None),
    )
    return jax.shard_map(step, mesh=finer, in_specs=placed, out_specs=P(ALL, None), check_vma=False)
```

profile of v0, /device:TPU:24, one launch (start us, length us, event | category | flops | bytes accessed | tf_op | source)
XLA Modules:
  0.0 166.9 jit_solution(18195553193242434028)
XLA Ops:
  0.7 0.7 dynamic-slice_convert_fusion
  1.5 1.0 add_convert_fusion.refs_0_
  2.5 4.0 %collective-permute-start.5 = (bf16[128,1024]{1,0:T(8,128)(2,1)S(1)}, bf16[128,1024]{1,0:T(8,128)(2,1)S(1)}, u32[]{:S(2)}, u32[]{:S(2)}) collective-permute-start(bf16[128,1024]{1,0:T(8,128)(2,1)S(1)} %add_convert_fusion.refs_0_), channel_id=1, source_target_pairs={{0,4},{4,0},{8,12},{12,8},{1,5},{5,1},{9,13},{13,9},{2,6},{6,2},{1... | collective-permute-start | bytes 786440 | tf_op jit(solution)/shard_map/ppermute | solution.py:33
  6.5 1.6 fusion.1
  8.1 3.4 %collective-permute-start.8 = (bf16[1024,256]{1,0:T(8,128)(2,1)S(1)}, bf16[1024,256]{1,0:T(8,128)(2,1)S(1)}, u32[]{:S(2)}, u32[]{:S(2)}) collective-permute-start(bf16[1024,256]{1,0:T(8,128)(2,1)S(1)} %pad_maximum_fusion.refs_4_), channel_id=1, source_target_pairs={{0,1},{1,0},{2,3},{3,2},{4,5},{5,4},{6,7},{7,6},{8,9},{9,8},{10,11... | collective-permute-start | bytes 1572872 | tf_op jit(solution)/shard_map/ppermute | solution.py:33
  11.5 4.6 %collective-permute-start.9 = (bf16[1024,256]{1,0:T(8,128)(2,1)S(1)}, bf16[1024,256]{1,0:T(8,128)(2,1)S(1)}, u32[]{:S(2)}, u32[]{:S(2)}) collective-permute-start(bf16[1024,256]{1,0:T(8,128)(2,1)S(1)} %pad_maximum_fusion.refs_4_), channel_id=1, source_target_pairs={{0,2},{1,3},{2,0},{3,1},{4,6},{5,7},{6,4},{7,5},{8,10},{9,11},{10,... | collective-permute-start | bytes 1572872 | tf_op jit(solution)/shard_map/ppermute | solution.py:33
  16.2 2.4 %collective-permute-start.10 = (bf16[1024,256]{1,0:T(8,128)(2,1)S(1)}, bf16[1024,256]{1,0:T(8,128)(2,1)S(1)}, u32[]{:S(2)}, u32[]{:S(2)}) collective-permute-start(bf16[1024,256]{1,0:T(8,128)(2,1)S(1)} %pad_maximum_fusion.refs_4_), channel_id=1, source_target_pairs={{0,3},{1,2},{2,1},{3,0},{4,7},{5,6},{6,5},{7,4},{8,11},{9,10},{10,... | collective-permute-start | bytes 1572872 | tf_op jit(solution)/shard_map/ppermute | solution.py:33
  18.6 5.2 %collective-permute-start.6 = (bf16[128,1024]{1,0:T(8,128)(2,1)S(1)}, bf16[128,1024]{1,0:T(8,128)(2,1)S(1)}, u32[]{:S(2)}, u32[]{:S(2)}) collective-permute-start(bf16[128,1024]{1,0:T(8,128)(2,1)S(1)} %add_convert_fusion.refs_0_), channel_id=1, source_target_pairs={{0,8},{4,12},{8,0},{12,4},{1,9},{5,13},{9,1},{13,5},{2,10},{6,14},... | collective-permute-start | bytes 786440 | tf_op jit(solution)/shard_map/ppermute | solution.py:33
  23.8 1.9 %collective-permute-start.7 = (bf16[128,1024]{1,0:T(8,128)(2,1)S(1)}, bf16[128,1024]{1,0:T(8,128)(2,1)S(1)}, u32[]{:S(2)}, u32[]{:S(2)}) collective-permute-start(bf16[128,1024]{1,0:T(8,128)(2,1)S(1)} %add_convert_fusion.refs_0_), channel_id=1, source_target_pairs={{0,12},{4,8},{8,4},{12,0},{1,13},{5,9},{9,5},{13,1},{2,14},{6,10},... | collective-permute-start | bytes 786440 | tf_op jit(solution)/shard_map/ppermute | solution.py:33
  25.7 14.3 %collective-permute-done.6.refs_2_ = bf16[128,1024]{1,0:T(8,128)(2,1)S(1)} collective-permute-done((bf16[128,1024]{1,0:T(8,128)(2,1)S(1)}, bf16[128,1024]{1,0:T(8,128)(2,1)S(1)}, u32[]{:S(2)}, u32[]{:S(2)}) %collective-permute-start.6) | collective-permute-done | bytes 262176 | tf_op jit(solution)/shard_map/ppermute | solution.py:33
  40.0 3.3 %collective-permute-done.10.refs_7_ = bf16[1024,256]{1,0:T(8,128)(2,1)S(1)} collective-permute-done((bf16[1024,256]{1,0:T(8,128)(2,1)S(1)}, bf16[1024,256]{1,0:T(8,128)(2,1)S(1)}, u32[]{:S(2)}, u32[]{:S(2)}) %collective-permute-start.10) | collective-permute-done | bytes 524320 | tf_op jit(solution)/shard_map/ppermute | solution.py:33
  43.4 2.2 %attend_part.1 = bf16[4,144,128]{2,1,0:T(8,128)(2,1)S(1)} custom-call(bf16[128,1024]{1,0:T(8,128)(2,1)S(1)} %add_convert_fusion.refs_0_, bf16[128,1024]{1,0:T(8,128)(2,1)S(1)} %collective-permute-done.5.refs_1_, bf16[128,1024]{1,0:T(8,128)(2,1)S(1)} %collective-permute-done.6.refs_2_, bf16[128,1024]{1,0:T(8,128)(2,1)S(1)} %collective-permute-done.7.refs_3_, ...), custom_call_target="tpu_custom_call" | custom-call | flops 1140850688 | bytes 3145728 | tf_op jit(solution)/shard_map/attend_part/pallas_call | solution.py:75
  45.5 8.4 %all_to_all.25.parts_ref = bf16[4,144,128]{2,1,0:T(8,128)(2,1)S(1)} all-to-all(bf16[4,144,128]{2,1,0:T(8,128)(2,1)S(1)} %attend_part.1), channel_id=1, replica_groups=mesh['y'=4,'h'=4,'c'=2,'z'=4,'x'=4] {'x'}, dimensions={0} | all-to-all | bytes 294912 | tf_op jit(solution)/shard_map/all_to_all | solution.py:37
  54.3 20.5 %all_to_all.26.parts_ref = bf16[16,8,2048]{2,1,0:T(8,128)(2,1)S(1)} all-to-all(bf16[16,8,2048]{2,1,0:T(8,128)(2,1)S(1)} %bitcast.25), channel_id=1, replica_groups=mesh['y'=4,'h'=4,'c'=2,'z'=4,'x'=4] {'z','x'}, dimensions={0} | all-to-all | bytes 1048576 | tf_op jit(solution)/shard_map/all_to_all | solution.py:37
  74.8 0.7 broadcast_in_dim.2
  75.6 4.4 %all-to-all-start = ((bf16[16,2,2048]{2,1,0:T(2,128)(2,1)}), bf16[16,2,2048]{2,1,0:T(2,128)(2,1)S(1)}, u32[]{:S(2)}, u32[]{:S(2)}) async-start(bf16[16,2,2048]{2,1,0:T(2,128)(2,1)} %broadcast_in_dim.2), calls=%async_computation | async-start | bytes 262144 | tf_op jit(solution)/shard_map/all_to_all | solution.py:37
  80.0 1.0 sum_and_norm.1
  81.1 7.9 %all-to-all-done = bf16[16,2,2048]{2,1,0:T(2,128)(2,1)S(1)} async-done(((bf16[16,2,2048]{2,1,0:T(2,128)(2,1)}), bf16[16,2,2048]{2,1,0:T(2,128)(2,1)S(1)}, u32[]{:S(2)}, u32[]{:S(2)}) %all-to-all-start) | async-done | bytes 131104 | tf_op jit(solution)/shard_map/all_to_all | solution.py:37
  89.0 3.7 %all-to-all-start.3 = ((bf16[16,8,2048]{2,1,0:T(8,128)(2,1)}), bf16[16,8,2048]{2,1,0:T(8,128)(2,1)S(1)}, u32[]{:S(2)}, u32[]{:S(2)}) async-start(bf16[16,8,2048]{2,1,0:T(8,128)(2,1)} %get-tuple-element.7), calls=%async_computation.3 | async-start | bytes 1048576 | tf_op jit(solution)/shard_map/all_to_all | solution.py:37
  93.0 0.8 copy-done.4
  93.9 9.1 %collective-permute-start = (bf16[32,256]{1,0:T(8,128)(2,1)S(1)}, bf16[32,256]{1,0:T(8,128)(2,1)S(1)}, u32[]{:S(2)}, u32[]{:S(2)}) collective-permute-start(bf16[32,256]{1,0:T(8,128)(2,1)S(1)} %get-tuple-element.19), channel_id=1, source_target_pairs={{0,32},{32,0},{64,96},{96,64},{1,33},{33,1},{65,97},{97,65},{2,34}... | collective-permute-start | bytes 49160 | tf_op jit(solution)/shard_map/ppermute | solution.py:33
  103.0 1.8 %collective-permute-done = bf16[32,256]{1,0:T(8,128)(2,1)S(1)} collective-permute-done((bf16[32,256]{1,0:T(8,128)(2,1)S(1)}, bf16[32,256]{1,0:T(8,128)(2,1)S(1)}, u32[]{:S(2)}, u32[]{:S(2)}) %collective-permute-start) | collective-permute-done | bytes 16416 | tf_op jit(solution)/shard_map/ppermute | solution.py:33
  104.8 13.0 %collective-permute-start.1 = (bf16[64,256]{1,0:T(8,128)(2,1)S(1)}, bf16[64,256]{1,0:T(8,128)(2,1)S(1)}, u32[]{:S(2)}, u32[]{:S(2)}) collective-permute-start(bf16[64,256]{1,0:T(8,128)(2,1)S(1)} %pad_maximum_fusion.3), channel_id=1, source_target_pairs={{0,64},{32,96},{64,0},{96,32},{1,65},{33,97},{65,1},{97,33},{2,66}... | collective-permute-start | bytes 98312 | tf_op jit(solution)/shard_map/ppermute | solution.py:33
  117.8 1.9 %collective-permute-done.1 = bf16[64,256]{1,0:T(8,128)(2,1)S(1)} collective-permute-done((bf16[64,256]{1,0:T(8,128)(2,1)S(1)}, bf16[64,256]{1,0:T(8,128)(2,1)S(1)}, u32[]{:S(2)}, u32[]{:S(2)}) %collective-permute-start.1) | collective-permute-done | bytes 32800 | tf_op jit(solution)/shard_map/ppermute | solution.py:33
  119.8 2.6 %collective-permute-start.2 = (bf16[128,256]{1,0:T(8,128)(2,1)S(1)}, bf16[128,256]{1,0:T(8,128)(2,1)S(1)}, u32[]{:S(2)}, u32[]{:S(2)}) collective-permute-start(bf16[128,256]{1,0:T(8,128)(2,1)S(1)} %pad_maximum_fusion.2), channel_id=1, source_target_pairs={{0,128},{128,0},{256,384},{384,256},{1,129},{129,1},{257,385},{385... | collective-permute-start | bytes 196616 | tf_op jit(solution)/shard_map/ppermute | solution.py:33
  122.4 3.5 %collective-permute-done.2 = bf16[128,256]{1,0:T(8,128)(2,1)S(1)} collective-permute-done((bf16[128,256]{1,0:T(8,128)(2,1)S(1)}, bf16[128,256]{1,0:T(8,128)(2,1)S(1)}, u32[]{:S(2)}, u32[]{:S(2)}) %collective-permute-start.2) | collective-permute-done | bytes 65568 | tf_op jit(solution)/shard_map/ppermute | solution.py:33
  125.9 3.1 %collective-permute-start.3 = (bf16[256,256]{1,0:T(8,128)(2,1)S(1)}, bf16[256,256]{1,0:T(8,128)(2,1)S(1)}, u32[]{:S(2)}, u32[]{:S(2)}) collective-permute-start(bf16[256,256]{1,0:T(8,128)(2,1)S(1)} %pad_maximum_fusion.1), channel_id=1, source_target_pairs={{0,256},{128,384},{256,0},{384,128},{1,257},{129,385},{257,1},{385... | collective-permute-start | bytes 393224 | tf_op jit(solution)/shard_map/ppermute | solution.py:33
  129.1 5.2 %collective-permute-done.3 = bf16[256,256]{1,0:T(8,128)(2,1)S(1)} collective-permute-done((bf16[256,256]{1,0:T(8,128)(2,1)S(1)}, bf16[256,256]{1,0:T(8,128)(2,1)S(1)}, u32[]{:S(2)}, u32[]{:S(2)}) %collective-permute-start.3) | collective-permute-done | bytes 131104 | tf_op jit(solution)/shard_map/ppermute | solution.py:33
  134.3 1.9 %collective-permute-start.4 = (bf16[512,256]{1,0:T(8,128)(2,1)S(1)}, bf16[512,256]{1,0:T(8,128)(2,1)S(1)}, u32[]{:S(2)}, u32[]{:S(2)}) collective-permute-start(bf16[512,256]{1,0:T(8,128)(2,1)S(1)} %get-tuple-element.9), channel_id=1, source_target_pairs={{0,16},{16,0},{1,17},{17,1},{2,18},{18,2},{3,19},{19,3},{4,20},{20... | collective-permute-start | bytes 786440 | tf_op jit(solution)/shard_map/ppermute | solution.py:33
  136.3 1.5 collective-permute-done.4
  139.1 27.1 %all_to_all.27.parts_ref = bf16[16,8,2048]{2,1,0:T(8,128)(2,1)S(1)} all-to-all(bf16[16,8,2048]{2,1,0:T(8,128)(2,1)S(1)} %fusion), channel_id=1, replica_groups=mesh['y'=4,'h'=4,'c'=2,'z'=4,'x'=4] {'z','x'}, dimensions={0} | all-to-all | bytes 1048576 | tf_op jit(solution)/shard_map/all_to_all | solution.py:37
  166.2 0.7 last_sum.1
  (38 shorter events, 2.3 us)
Async XLA Ops:
  0.0 138.5 %copy-start = (bf16[128,2048]{1,0:T(8,128)(2,1)S(1)}, bf16[128,2048]{1,0:T(8,128)(2,1)}, u32[]{:S(2)}) copy-start(bf16[128,2048]{1,0:T(8,128)(2,1)} %param.25) | copy-start | bytes 1572868
  0.0 6.5 %copy-start.2 = (bf16[128,2048]{1,0:T(8,128)(2,1)S(1)}, bf16[128,2048]{1,0:T(8,128)(2,1)}, u32[]{:S(2)}) copy-start(bf16[128,2048]{1,0:T(8,128)(2,1)} %param.16) | copy-start | bytes 1572868
  2.5 5.6 %copy-start.6 = (bf16[1024,128]{1,0:T(8,128)(2,1)S(1)}, bf16[1024,128]{1,0:T(8,128)(2,1)}, u32[]{:S(2)}) copy-start(bf16[1024,128]{1,0:T(8,128)(2,1)} %param.19) | copy-start | bytes 786436
  2.5 21.3 %collective-permute-start.5 = (bf16[128,1024]{1,0:T(8,128)(2,1)S(1)}, bf16[128,1024]{1,0:T(8,128)(2,1)S(1)}, u32[]{:S(2)}, u32[]{:S(2)}) collective-permute-start(bf16[128,1024]{1,0:T(8,128)(2,1)S(1)} %add_convert_fusion.refs_0_), channel_id=1, source_target_pairs={{0,4},{4,0},{8,12},{12,8},{1,5},{5,1},{9,13},{13,9},{2,6},{6,2},{1... | collective-permute-start | bytes 786440 | tf_op jit(solution)/shard_map/ppermute | solution.py:33
  8.1 31.9 %collective-permute-start.8 = (bf16[1024,256]{1,0:T(8,128)(2,1)S(1)}, bf16[1024,256]{1,0:T(8,128)(2,1)S(1)}, u32[]{:S(2)}, u32[]{:S(2)}) collective-permute-start(bf16[1024,256]{1,0:T(8,128)(2,1)S(1)} %pad_maximum_fusion.refs_4_), channel_id=1, source_target_pairs={{0,1},{1,0},{2,3},{3,2},{4,5},{5,4},{6,7},{7,6},{8,9},{9,8},{10,11... | collective-permute-start | bytes 1572872 | tf_op jit(solution)/shard_map/ppermute | solution.py:33
  11.5 28.5 %collective-permute-start.9 = (bf16[1024,256]{1,0:T(8,128)(2,1)S(1)}, bf16[1024,256]{1,0:T(8,128)(2,1)S(1)}, u32[]{:S(2)}, u32[]{:S(2)}) collective-permute-start(bf16[1024,256]{1,0:T(8,128)(2,1)S(1)} %pad_maximum_fusion.refs_4_), channel_id=1, source_target_pairs={{0,2},{1,3},{2,0},{3,1},{4,6},{5,7},{6,4},{7,5},{8,10},{9,11},{10,... | collective-permute-start | bytes 1572872 | tf_op jit(solution)/shard_map/ppermute | solution.py:33
  16.2 27.2 %collective-permute-start.10 = (bf16[1024,256]{1,0:T(8,128)(2,1)S(1)}, bf16[1024,256]{1,0:T(8,128)(2,1)S(1)}, u32[]{:S(2)}, u32[]{:S(2)}) collective-permute-start(bf16[1024,256]{1,0:T(8,128)(2,1)S(1)} %pad_maximum_fusion.refs_4_), channel_id=1, source_target_pairs={{0,3},{1,2},{2,1},{3,0},{4,7},{5,6},{6,5},{7,4},{8,11},{9,10},{10,... | collective-permute-start | bytes 1572872 | tf_op jit(solution)/shard_map/ppermute | solution.py:33
  18.6 21.4 %collective-permute-start.6 = (bf16[128,1024]{1,0:T(8,128)(2,1)S(1)}, bf16[128,1024]{1,0:T(8,128)(2,1)S(1)}, u32[]{:S(2)}, u32[]{:S(2)}) collective-permute-start(bf16[128,1024]{1,0:T(8,128)(2,1)S(1)} %add_convert_fusion.refs_0_), channel_id=1, source_target_pairs={{0,8},{4,12},{8,0},{12,4},{1,9},{5,13},{9,1},{13,5},{2,10},{6,14},... | collective-permute-start | bytes 786440 | tf_op jit(solution)/shard_map/ppermute | solution.py:33
  23.8 16.2 %collective-permute-start.7 = (bf16[128,1024]{1,0:T(8,128)(2,1)S(1)}, bf16[128,1024]{1,0:T(8,128)(2,1)S(1)}, u32[]{:S(2)}, u32[]{:S(2)}) collective-permute-start(bf16[128,1024]{1,0:T(8,128)(2,1)S(1)} %add_convert_fusion.refs_0_), channel_id=1, source_target_pairs={{0,12},{4,8},{8,4},{12,0},{1,13},{5,9},{9,5},{13,1},{2,14},{6,10},... | collective-permute-start | bytes 786440 | tf_op jit(solution)/shard_map/ppermute | solution.py:33
  43.4 10.6 %copy-start.1 = (bf16[128,2048]{1,0:T(8,128)(2,1)S(1)}, bf16[128,2048]{1,0:T(8,128)(2,1)}, u32[]{:S(2)}) copy-start(bf16[128,2048]{1,0:T(8,128)(2,1)} %weight_ref.1) | copy-start | bytes 1572868
  54.3 20.5 %copy-start.7 = (bf16[2,2048]{1,0:T(2,128)(2,1)S(1)}, bf16[2,2048]{1,0:T(2,128)(2,1)}, u32[]{:S(2)}) copy-start(bf16[2,2048]{1,0:T(2,128)(2,1)} %param.21) | copy-start | bytes 24580
  75.6 13.4 %all-to-all-start = ((bf16[16,2,2048]{2,1,0:T(2,128)(2,1)}), bf16[16,2,2048]{2,1,0:T(2,128)(2,1)S(1)}, u32[]{:S(2)}, u32[]{:S(2)}) async-start(bf16[16,2,2048]{2,1,0:T(2,128)(2,1)} %broadcast_in_dim.2), calls=%async_computation | async-start | bytes 262144 | tf_op jit(solution)/shard_map/all_to_all | solution.py:37
  89.0 3.8 %copy-start.3 = (bf16[2048,128]{1,0:T(8,128)(2,1)S(1)}, bf16[2048,128]{1,0:T(8,128)(2,1)}, u32[]{:S(2)}) copy-start(bf16[2048,128]{1,0:T(8,128)(2,1)} %param.24) | copy-start | bytes 1572868
  89.0 48.8 %all-to-all-start.3 = ((bf16[16,8,2048]{2,1,0:T(8,128)(2,1)}), bf16[16,8,2048]{2,1,0:T(8,128)(2,1)S(1)}, u32[]{:S(2)}, u32[]{:S(2)}) async-start(bf16[16,8,2048]{2,1,0:T(8,128)(2,1)} %get-tuple-element.7), calls=%async_computation.3 | async-start | bytes 1048576 | tf_op jit(solution)/shard_map/all_to_all | solution.py:37
  92.7 1.0 copy-start.4
  93.9 10.9 %collective-permute-start = (bf16[32,256]{1,0:T(8,128)(2,1)S(1)}, bf16[32,256]{1,0:T(8,128)(2,1)S(1)}, u32[]{:S(2)}, u32[]{:S(2)}) collective-permute-start(bf16[32,256]{1,0:T(8,128)(2,1)S(1)} %get-tuple-element.19), channel_id=1, source_target_pairs={{0,32},{32,0},{64,96},{96,64},{1,33},{33,1},{65,97},{97,65},{2,34}... | collective-permute-start | bytes 49160 | tf_op jit(solution)/shard_map/ppermute | solution.py:33
  104.8 14.9 %collective-permute-start.1 = (bf16[64,256]{1,0:T(8,128)(2,1)S(1)}, bf16[64,256]{1,0:T(8,128)(2,1)S(1)}, u32[]{:S(2)}, u32[]{:S(2)}) collective-permute-start(bf16[64,256]{1,0:T(8,128)(2,1)S(1)} %pad_maximum_fusion.3), channel_id=1, source_target_pairs={{0,64},{32,96},{64,0},{96,32},{1,65},{33,97},{65,1},{97,33},{2,66}... | collective-permute-start | bytes 98312 | tf_op jit(solution)/shard_map/ppermute | solution.py:33
  119.8 6.1 %collective-permute-start.2 = (bf16[128,256]{1,0:T(8,128)(2,1)S(1)}, bf16[128,256]{1,0:T(8,128)(2,1)S(1)}, u32[]{:S(2)}, u32[]{:S(2)}) collective-permute-start(bf16[128,256]{1,0:T(8,128)(2,1)S(1)} %pad_maximum_fusion.2), channel_id=1, source_target_pairs={{0,128},{128,0},{256,384},{384,256},{1,129},{129,1},{257,385},{385... | collective-permute-start | bytes 196616 | tf_op jit(solution)/shard_map/ppermute | solution.py:33
  125.9 8.4 %collective-permute-start.3 = (bf16[256,256]{1,0:T(8,128)(2,1)S(1)}, bf16[256,256]{1,0:T(8,128)(2,1)S(1)}, u32[]{:S(2)}, u32[]{:S(2)}) collective-permute-start(bf16[256,256]{1,0:T(8,128)(2,1)S(1)} %pad_maximum_fusion.1), channel_id=1, source_target_pairs={{0,256},{128,384},{256,0},{384,128},{1,257},{129,385},{257,1},{385... | collective-permute-start | bytes 393224 | tf_op jit(solution)/shard_map/ppermute | solution.py:33
  129.1 8.7 %copy-start.5 = (bf16[2048,128]{1,0:T(8,128)(2,1)S(1)}, bf16[2048,128]{1,0:T(8,128)(2,1)}, u32[]{:S(2)}) copy-start(bf16[2048,128]{1,0:T(8,128)(2,1)} %param.22) | copy-start | bytes 1572868
  134.3 3.4 %collective-permute-start.4 = (bf16[512,256]{1,0:T(8,128)(2,1)S(1)}, bf16[512,256]{1,0:T(8,128)(2,1)S(1)}, u32[]{:S(2)}, u32[]{:S(2)}) collective-permute-start(bf16[512,256]{1,0:T(8,128)(2,1)S(1)} %get-tuple-element.9), channel_id=1, source_target_pairs={{0,16},{16,0},{1,17},{17,1},{2,18},{18,2},{3,19},{19,3},{4,20},{20... | collective-permute-start | bytes 786440 | tf_op jit(solution)/shard_map/ppermute | solution.py:33
where the time goes:
time: 168 us; the launch traced here: 167 us
  starting transfers between devices  59.4 us (35%)
  blocking collectives  56 us (33%)
  waiting for transfers between devices  39.4 us (23%)
  Pallas kernels  4.25 us (3%)
  matrix products  3.13 us (2%)
  other arithmetic  1.97 us (1%)
    all_to_all x3, blocking collectives, exchange(): return lax.all_to_all(tiles, axis, split_axis=0, concat_axis=0, tiled=True)  56 us
    ppermute x11, starting transfers between devices, partner(): return lax.ppermute(value, axis, pairs)  51.2 us
    ppermute x11, waiting for transfers between devices, partner(): return lax.ppermute(value, axis, pairs)  31.6 us
    all_to_all x2, starting transfers between devices, exchange(): return lax.all_to_all(tiles, axis, split_axis=0, concat_axis=0, tiled=True)  8.15 us
    all_to_all x2, waiting for transfers between devices, exchange(): return lax.all_to_all(tiles, axis, split_axis=0, concat_axis=0, tiled=True)  7.86 us
  transfers between devices with their start and end apart: 13, of which 8 were waited for; matrix products, arithmetic and copies ran while one was open for 1% of the time, Pallas kernels for 1%

commit v1 on v0

--- a/solution.py
+++ b/solution.py
@@ -18,7 +18,9 @@
 F32 = jnp.float32
 SCALE = HEAD ** (-0.5)
 TAIL = 16
+EXTRA = 8
 PARAMS = pltpu.CompilerParams(vmem_limit_bytes=20 * 2**20)
+WIDE = pltpu.CompilerParams(vmem_limit_bytes=62 * 2**20)
 
 
 VMEM = pl.BlockSpec(memory_space=pltpu.VMEM)
@@ -37,24 +39,55 @@
     return lax.all_to_all(tiles, axis, split_axis=0, concat_axis=0, tiled=True)
 
 
-def all_from(value, axis):
-    copies = jnp.broadcast_to(value, (lax.axis_size(axis), *value.shape))
-    return exchange(copies, axis)
-
-
 def cost(flops, size):
     return pl.CostEstimate(flops=flops, bytes_accessed=size, transcendentals=0)
 
 
+def key_kernel(slot_ref, group_ref, embed_ref, global_ref, out_ref):
+    lines = lax.broadcasted_iota(jnp.int32, embed_ref.shape, 0)
+    chosen = jnp.where(lines == slot_ref[0, 0], embed_ref[...].astype(F32), 0.0)
+    keyed = group_ref[...].astype(F32) + jnp.sum(chosen, axis=0, keepdims=True)
+    length, width = group_ref.shape
+    latents = global_ref[...].astype(F32)
+    rest = jnp.zeros((out_ref.shape[1] - length - 4, width), F32)
+    tail = jnp.concatenate([latents[:, :width], latents[:, width:], rest], axis=0)
+    block = jnp.concatenate([keyed, tail], axis=0).astype(BF16)
+    for j in range(out_ref.shape[0]):
+        out_ref[j] = block
+
+
+def key_copies(slot_ids, group_latents, slot_embed, global_latents, many):
+    length, width = group_latents.shape
+    return pl.pallas_call(
+        key_kernel,
+        out_shape=jax.ShapeDtypeStruct((many, length + EXTRA, width), BF16),
+        in_specs=[pl.BlockSpec(memory_space=pltpu.SMEM), VMEM, VMEM, VMEM],
+        out_specs=VMEM,
+        compiler_params=WIDE,
+        cost_estimate=cost(4 * group_latents.size, 2**20),
+        name="key_copies",
+    )(slot_ids, group_latents, slot_embed, global_latents)
+
+
 def attend_kernel(*refs):
-    blocks, packs, out_ref = refs[:4], refs[4:8], refs[8]
+    blocks_ref, packs, out_ref = refs[0], refs[1:-1], refs[-1]
     mine = lax.axis_index("x")
+    many, length = blocks_ref.shape[0], blocks_ref.shape[1] - EXTRA
+    tails = [blocks_ref[j, length:, :].astype(F32) for j in range(many)]
+    latents = jnp.concatenate(
+        [
+            jnp.concatenate([tail[:2] for tail in tails], axis=0),
+            jnp.concatenate([tail[2:4] for tail in tails], axis=0),
+        ],
+        axis=1,
+    )
+    pieces = [latents[:, k : k + HEAD] for k in range(0, latents.shape[1], HEAD)]
     for step, pack_ref in enumerate(packs):
         place = mine ^ step
         pack = pack_ref[...]
-        both = [dot(block[...], pack, ((1,), (0,))) for block in blocks]
-        scores = jnp.concatenate([b[:, :HEAD] for b in both], axis=0) * SCALE
-        values = jnp.concatenate([b[:, HEAD:].astype(BF16) for b in both], axis=0)
+        both = [dot(blocks_ref[j, :length, :], pack, ((1,), (0,))) for j in range(many)]
+        scores = jnp.concatenate([b[:, :-HEAD] for b in both], axis=0) * SCALE
+        values = jnp.concatenate([b[:, -HEAD:].astype(BF16) for b in both], axis=0)
         top = jnp.max(scores, axis=0, keepdims=True)
         weights = jnp.exp(scores - top)
         total = jnp.sum(weights, axis=0, keepdims=True)
@@ -65,28 +98,57 @@
         low = level - high - middle
         line = lax.broadcasted_iota(jnp.int32, (TAIL, mixed.shape[1]), 0)
         tail = jnp.where(line == 0, high, jnp.where(line == 1, middle, jnp.where(line == 2, low, 0.0)))
-        out_ref[place] = jnp.concatenate([mixed, tail], axis=0).astype(BF16)
-
-
-def attend_part(blocks, packs, length):
-    many = len(packs)
-    keys = sum(b.shape[0] for b in blocks)
-    flops = 2 * many * keys * (blocks[0].shape[1] * 2 * HEAD + HEAD * length)
+        out_ref[place] = jnp.concatenate([mixed, tail, *pieces], axis=0).astype(BF16)
+
+
+def attend_part(blocks, packs):
+    many, length = len(packs), packs[0].shape[1] - HEAD
+    keys = blocks.shape[0] * blocks.shape[1]
+    flops = 2 * many * keys * (blocks.shape[2] * 2 * HEAD + HEAD * length)
+    height = HEAD + TAIL + 2 * blocks.shape[0] * 2 * blocks.shape[2] // HEAD
     return pl.pallas_call(
         attend_kernel,
-        out_shape=jax.ShapeDtypeStruct((many, HEAD + TAIL, length), BF16),
-        in_specs=[VMEM] * (len(blocks) + many),
-        out_specs=VMEM,
-        compiler_params=PARAMS,
+        out_shape=jax.ShapeDtypeStruct((many, height, length), BF16),
+        in_specs=[VMEM] * (1 + many),
+        out_specs=VMEM,
+        compiler_params=WIDE,
         cost_estimate=cost(flops, 3 * 2**20),
         name="attend_part",
-    )(*blocks, *packs)
+    )(blocks, *packs)
+
+
+def pair_kernel(parts_ref, key_ref, value_ref, out_ref):
+    many, height, _ = parts_ref.shape
+    lines = []
+    for j in range(many):
+        pieces = [
+            parts_ref[j, k : k + 8, :].astype(F32) for k in range(HEAD + TAIL, height, 8)
+        ]
+        lines.append(jnp.concatenate(pieces, axis=1))
+    latents = jnp.concatenate(lines, axis=0).astype(BF16)
+    out_ref[:, :HEAD] = dot(latents, key_ref[...], ((1,), (0,))).astype(BF16)
+    out_ref[:, HEAD:] = dot(latents, value_ref[...], ((1,), (0,))).astype(BF16)
+
+
+def decode_pairs(parts, key_weight, value_weight):
+    many, height, length = parts.shape
+    size = many * (height - HEAD - TAIL) * length
+    rows = size // key_weight.shape[0]
+    return pl.pallas_call(
+        pair_kernel,
+        out_shape=jax.ShapeDtypeStruct((rows, 2 * HEAD), BF16),
+        in_specs=[VMEM, VMEM, VMEM],
+        out_specs=VMEM,
+        compiler_params=PARAMS,
+        cost_estimate=cost(4 * size * HEAD, 2**20),
+        name="decode_pairs",
+    )(parts, key_weight, value_weight)
 
 
 def join_kernel(parts_ref, weight_ref, out_ref):
     many = parts_ref.shape[0]
     levels = [
-        jnp.sum(parts_ref[j, HEAD:, :].astype(F32), axis=0, keepdims=True) for j in range(many)
+        jnp.sum(parts_ref[j, HEAD : HEAD + TAIL, :].astype(F32), axis=0, keepdims=True) for j in range(many)
     ]
     top = functools.reduce(jnp.maximum, levels)
     shares = [jnp.exp(level - top) for level in levels]
@@ -178,36 +240,22 @@
     query_two = dot(merge_latents, query_weight, ((1,), (0,))).astype(BF16)
     folded = dot(key_weight, query_two, ((1,), (1,))).astype(BF16)
     pack = jnp.concatenate([folded, value_weight], axis=1)
-    slot_row = lax.dynamic_slice_in_dim(slot_embed, slot_ids[0, 0], 1, 0)
-    keyed = (group_latents.astype(F32) + slot_row.astype(F32)).astype(BF16)
     own_rows = lax.dynamic_slice_in_dim(merge_latents, lax.axis_index(INNER) * rows, rows, 0)
 
+    copies = key_copies(slot_ids, group_latents, slot_embed, global_latents, lax.axis_size("z"))
+    blocks = exchange(copies, "z")
     pack_two = partner(pack, "x", 2)
-    keyed_three = partner(keyed, "z", 3)
-    outer_block = all_from(global_latents, INNER).reshape(-1, width)
     pack_three = partner(pack, "x", 3)
-    keyed_two = partner(keyed, "z", 2)
     pack_one = partner(pack, "x", 1)
-    keyed_one = partner(keyed, "z", 1)
-
-    pairs = jnp.concatenate(
-        [
-            dot(outer_block, decode_key, ((1,), (0,))).astype(BF16),
-            dot(outer_block, decode_value, ((1,), (0,))).astype(BF16),
-        ],
-        axis=1,
-    )
+    parts = attend_part(blocks, [pack, pack_one, pack_two, pack_three])
+    parts = exchange(parts, "x")
+
+    pairs = decode_pairs(parts, decode_key, decode_value)
     for axis, step_size in (("h", 1), ("h", 2), ("y", 1), ("y", 2)):
         if lax.axis_size(axis) > step_size:
             pairs = jnp.concatenate([pairs, partner(pairs, axis, step_size)], axis=0)
     other = partner(pairs, "c", 1)
 
-    parts = attend_part(
-        [keyed, keyed_one, keyed_two, keyed_three],
-        [pack, pack_one, pack_two, pack_three],
-        length,
-    )
-    parts = exchange(parts, "x")
     partial = join_and_project(parts, output_weight)
     arrived = exchange(partial.reshape(inner, rows, width), INNER)
     level_two, copies = sum_and_norm(arrived, own_rows)

time: 168 us -> 161 us (0.958)
  blocking collectives: 56 us -> 37.8 us
  waiting for transfers between devices: 39.4 us -> 51.8 us
  Pallas kernels: 4.25 us -> 9.93 us
  starting transfers between devices: 59.4 us -> 56.3 us
  other arithmetic: 1.97 us -> 0.24 us
    all_to_all x3 -> x2, blocking collectives: 56 us -> 37.8 us  [exchange(): return lax.all_to_all(tiles, axis, split_axis=0, concat_axis=0, tiled=True)]
    ppermute x11 -> x8, starting transfers between devices: 51.2 us -> 40.4 us  [partner(): return lax.ppermute(value, axis, pairs)]
    all_to_all x2 -> x3, starting transfers between devices: 8.15 us -> 15.9 us  [exchange(): return lax.all_to_all(tiles, axis, split_axis=0, concat_axis=0, tiled=True)]
    ppermute x11 -> x8, waiting for transfers between devices: 31.6 us -> 39.2 us  [partner(): return lax.ppermute(value, axis, pairs)]
    pallas_call x1 -> x3, Pallas kernels: 2.16 us -> 7.02 us  [the longest x1 4.71 us: attend_part(): pl.pallas_call(attend_kernel, out_shape=jax.ShapeDtypeStruct((many, heigh...]
    all_to_all x2 -> x3, waiting for transfers between devices: 7.86 us -> 12.6 us  [exchange(): return lax.all_to_all(tiles, axis, split_axis=0, concat_axis=0, tiled=True)]
  transfers between devices with their start and end apart: 13 -> 11, of which waited for: 8 -> 9; matrix products, arithmetic and copies ran while one was open for 1% -> 0% of each run, Pallas kernels for 1% -> 0%
where the time goes in v1:
time: 161 us; the launch traced here: 160 us
  starting transfers between devices  56.3 us (35%)
  waiting for transfers between devices  51.8 us (32%)
  blocking collectives  37.8 us (23%)
  Pallas kernels  9.93 us (6%)
  matrix products  1.62 us (1%)
    ppermute x8, starting transfers between devices, partner(): return lax.ppermute(value, axis, pairs)  40.4 us
    ppermute x8, waiting for transfers between devices, partner(): return lax.ppermute(value, axis, pairs)  39.2 us
    all_to_all x2, blocking collectives, exchange(): return lax.all_to_all(tiles, axis, split_axis=0, concat_axis=0, tiled=True)  37.8 us
    all_to_all x3, starting transfers between devices, exchange(): return lax.all_to_all(tiles, axis, split_axis=0, concat_axis=0, tiled=True)  15.9 us
    all_to_all x3, waiting for transfers between devices, exchange(): return lax.all_to_all(tiles, axis, split_axis=0, concat_axis=0, tiled=True)  12.6 us
    pallas_call x1, Pallas kernels, attend_part(): pl.pallas_call(attend_kernel, out_shape=jax.ShapeDtypeStruct((many, heigh...  4.71 us
  transfers between devices with their start and end apart: 11, of which 9 were waited for; matrix products, arithmetic and copies ran while one was open for 0% of the time, Pallas kernels for 0%

profile of v1, /device:TPU:24, one launch (start us, length us, event | category | flops | bytes accessed | tf_op | source)
XLA Modules:
  0.0 160.0 jit_solution(6253054657198932110)
XLA Ops:
  0.7 2.0 %key_copies.1 = bf16[4,136,1024]{2,1,0:T(8,128)(2,1)} custom-call(s32[1,1]{1,0:T(1,128)S(6)} %copy.25.slot_ref, bf16[128,1024]{1,0:T(8,128)(2,1)} %group_ref.1, bf16[16,1024]{1,0:T(8,128)(2,1)} %embed_ref.1, bf16[2,2048]{1,0:T(2,128)(2,1)} %global_ref.1), custom_call_target="tpu_custom_call" | custom-call | flops 524288 | bytes 1048576 | tf_op jit(solution)/shard_map/key_copies/pallas_call | solution.py:61
  2.8 6.0 %all-to-all-start = ((bf16[4,136,1024]{2,1,0:T(8,128)(2,1)}), bf16[4,136,1024]{2,1,0:T(8,128)(2,1)}, u32[]{:S(2)}, u32[]{:S(2)}) async-start(bf16[4,136,1024]{2,1,0:T(8,128)(2,1)} %key_copies.1), calls=%async_computation | async-start | bytes 2228224 | tf_op jit(solution)/shard_map/all_to_all | solution.py:39
  8.8 0.5 fusion.1
  9.3 0.5 copy-done.9
  9.8 3.5 %collective-permute-start = (bf16[1024,256]{1,0:T(8,128)(2,1)S(1)}, bf16[1024,256]{1,0:T(8,128)(2,1)S(1)}, u32[]{:S(2)}, u32[]{:S(2)}) collective-permute-start(bf16[1024,256]{1,0:T(8,128)(2,1)S(1)} %pad_maximum_fusion.refs_1_), channel_id=1, source_target_pairs={{0,1},{1,0},{2,3},{3,2},{4,5},{5,4},{6,7},{7,6},{8,9},{9,8},{10,11... | collective-permute-start | bytes 1572872 | tf_op jit(solution)/shard_map/ppermute | solution.py:35
  13.4 4.6 %collective-permute-start.1 = (bf16[1024,256]{1,0:T(8,128)(2,1)S(1)}, bf16[1024,256]{1,0:T(8,128)(2,1)S(1)}, u32[]{:S(2)}, u32[]{:S(2)}) collective-permute-start(bf16[1024,256]{1,0:T(8,128)(2,1)S(1)} %pad_maximum_fusion.refs_1_), channel_id=1, source_target_pairs={{0,2},{1,3},{2,0},{3,1},{4,6},{5,7},{6,4},{7,5},{8,10},{9,11},{10,... | collective-permute-start | bytes 1572872 | tf_op jit(solution)/shard_map/ppermute | solution.py:35
  18.0 2.4 %collective-permute-start.2 = (bf16[1024,256]{1,0:T(8,128)(2,1)S(1)}, bf16[1024,256]{1,0:T(8,128)(2,1)}, u32[]{:S(2)}, u32[]{:S(2)}) collective-permute-start(bf16[1024,256]{1,0:T(8,128)(2,1)S(1)} %pad_maximum_fusion.refs_1_), channel_id=1, source_target_pairs={{0,3},{1,2},{2,1},{3,0},{4,7},{5,6},{6,5},{7,4},{8,11},{9,10},{10,... | collective-permute-start | bytes 1572872 | tf_op jit(solution)/shard_map/ppermute | solution.py:35
  20.4 6.2 %collective-permute-done.refs_2_ = bf16[1024,256]{1,0:T(8,128)(2,1)S(1)} collective-permute-done((bf16[1024,256]{1,0:T(8,128)(2,1)S(1)}, bf16[1024,256]{1,0:T(8,128)(2,1)S(1)}, u32[]{:S(2)}, u32[]{:S(2)}) %collective-permute-start) | collective-permute-done | bytes 524320 | tf_op jit(solution)/shard_map/ppermute | solution.py:35
  26.7 12.1 %collective-permute-done.1.refs_3_ = bf16[1024,256]{1,0:T(8,128)(2,1)S(1)} collective-permute-done((bf16[1024,256]{1,0:T(8,128)(2,1)S(1)}, bf16[1024,256]{1,0:T(8,128)(2,1)S(1)}, u32[]{:S(2)}, u32[]{:S(2)}) %collective-permute-start.1) | collective-permute-done | bytes 524320 | tf_op jit(solution)/shard_map/ppermute | solution.py:35
  38.8 0.8 copy-done.11
  39.6 5.7 %collective-permute-done.2.refs_4_ = bf16[1024,256]{1,0:T(8,128)(2,1)} collective-permute-done((bf16[1024,256]{1,0:T(8,128)(2,1)S(1)}, bf16[1024,256]{1,0:T(8,128)(2,1)}, u32[]{:S(2)}, u32[]{:S(2)}) %collective-permute-start.2) | collective-permute-done | bytes 524320 | tf_op jit(solution)/shard_map/ppermute | solution.py:35
  45.3 4.7 %attend_part.1 = bf16[4,272,128]{2,1,0:T(8,128)(2,1)} custom-call(bf16[4,136,1024]{2,1,0:T(8,128)(2,1)} %all-to-all-done.refs_0_, bf16[1024,256]{1,0:T(8,128)(2,1)} %copy-done.6, bf16[1024,256]{1,0:T(8,128)(2,1)} %copy-done.10, bf16[1024,256]{1,0:T(8,128)(2,1)} %copy-done.11, bf16[1024,256]{1,0:T(8,128)(2,1)} %collective-permute-done.2.refs_4_), custom_call_target="tpu_custom_call" | custom-call | flops 1212153856 | bytes 3145728 | tf_op jit(solution)/shard_map/attend_part/pallas_call | solution.py:109
  50.0 10.2 %all_to_all.25.parts_ref = bf16[4,272,128]{2,1,0:T(8,128)(2,1)S(1)} all-to-all(bf16[4,272,128]{2,1,0:T(8,128)(2,1)} %attend_part.1), channel_id=1, replica_groups=mesh['y'=4,'h'=4,'c'=2,'z'=4,'x'=4] {'x'}, dimensions={0} | all-to-all | bytes 557056 | tf_op jit(solution)/shard_map/all_to_all | solution.py:39
  60.2 1.2 join_and_project.1
  61.4 5.7 %all-to-all-start.2 = ((bf16[16,8,2048]{2,1,0:T(8,128)(2,1)}), bf16[16,8,2048]{2,1,0:T(8,128)(2,1)S(1)}, u32[]{:S(2)}, u32[]{:S(2)}) async-start(bf16[16,8,2048]{2,1,0:T(8,128)(2,1)} %bitcast.1), calls=%async_computation.2 | async-start | bytes 1048576 | tf_op jit(solution)/shard_map/all_to_all | solution.py:39
  67.1 12.6 %all-to-all-done.2.parts_ref = bf16[16,8,2048]{2,1,0:T(8,128)(2,1)S(1)} async-done(((bf16[16,8,2048]{2,1,0:T(8,128)(2,1)}), bf16[16,8,2048]{2,1,0:T(8,128)(2,1)S(1)}, u32[]{:S(2)}, u32[]{:S(2)}) %all-to-all-start.2) | async-done | bytes 524320 | tf_op jit(solution)/shard_map/all_to_all | solution.py:39
  79.6 1.0 sum_and_norm.1
  80.7 4.2 %all-to-all-start.3 = ((bf16[16,8,2048]{2,1,0:T(8,128)(2,1)}), bf16[16,8,2048]{2,1,0:T(8,128)(2,1)S(1)}, u32[]{:S(2)}, u32[]{:S(2)}) async-start(bf16[16,8,2048]{2,1,0:T(8,128)(2,1)} %get-tuple-element.7), calls=%async_computation.3 | async-start | bytes 1048576 | tf_op jit(solution)/shard_map/all_to_all | solution.py:39
  85.2 9.2 %collective-permute-start.3 = (bf16[32,256]{1,0:T(8,128)(2,1)S(1)}, bf16[32,256]{1,0:T(8,128)(2,1)S(1)}, u32[]{:S(2)}, u32[]{:S(2)}) collective-permute-start(bf16[32,256]{1,0:T(8,128)(2,1)S(1)} %decode_pairs.1), channel_id=1, source_target_pairs={{0,32},{32,0},{64,96},{96,64},{1,33},{33,1},{65,97},{97,65},{2,34}... | collective-permute-start | bytes 49160 | tf_op jit(solution)/shard_map/ppermute | solution.py:35
  94.5 1.8 %collective-permute-done.3 = bf16[32,256]{1,0:T(8,128)(2,1)S(1)} collective-permute-done((bf16[32,256]{1,0:T(8,128)(2,1)S(1)}, bf16[32,256]{1,0:T(8,128)(2,1)S(1)}, u32[]{:S(2)}, u32[]{:S(2)}) %collective-permute-start.3) | collective-permute-done | bytes 16416 | tf_op jit(solution)/shard_map/ppermute | solution.py:35
  96.3 13.5 %collective-permute-start.4 = (bf16[64,256]{1,0:T(8,128)(2,1)S(1)}, bf16[64,256]{1,0:T(8,128)(2,1)S(1)}, u32[]{:S(2)}, u32[]{:S(2)}) collective-permute-start(bf16[64,256]{1,0:T(8,128)(2,1)S(1)} %pad_maximum_fusion.3), channel_id=1, source_target_pairs={{0,64},{32,96},{64,0},{96,32},{1,65},{33,97},{65,1},{97,33},{2,66}... | collective-permute-start | bytes 98312 | tf_op jit(solution)/shard_map/ppermute | solution.py:35
  109.8 1.9 %collective-permute-done.4 = bf16[64,256]{1,0:T(8,128)(2,1)S(1)} collective-permute-done((bf16[64,256]{1,0:T(8,128)(2,1)S(1)}, bf16[64,256]{1,0:T(8,128)(2,1)S(1)}, u32[]{:S(2)}, u32[]{:S(2)}) %collective-permute-start.4) | collective-permute-done | bytes 32800 | tf_op jit(solution)/shard_map/ppermute | solution.py:35
  111.7 2.6 %collective-permute-start.5 = (bf16[128,256]{1,0:T(8,128)(2,1)S(1)}, bf16[128,256]{1,0:T(8,128)(2,1)S(1)}, u32[]{:S(2)}, u32[]{:S(2)}) collective-permute-start(bf16[128,256]{1,0:T(8,128)(2,1)S(1)} %pad_maximum_fusion.2), channel_id=1, source_target_pairs={{0,128},{128,0},{256,384},{384,256},{1,129},{129,1},{257,385},{385... | collective-permute-start | bytes 196616 | tf_op jit(solution)/shard_map/ppermute | solution.py:35
  114.3 4.1 %collective-permute-done.5 = bf16[128,256]{1,0:T(8,128)(2,1)S(1)} collective-permute-done((bf16[128,256]{1,0:T(8,128)(2,1)S(1)}, bf16[128,256]{1,0:T(8,128)(2,1)S(1)}, u32[]{:S(2)}, u32[]{:S(2)}) %collective-permute-start.5) | collective-permute-done | bytes 65568 | tf_op jit(solution)/shard_map/ppermute | solution.py:35
  118.5 2.5 %collective-permute-start.6 = (bf16[256,256]{1,0:T(8,128)(2,1)S(1)}, bf16[256,256]{1,0:T(8,128)(2,1)S(1)}, u32[]{:S(2)}, u32[]{:S(2)}) collective-permute-start(bf16[256,256]{1,0:T(8,128)(2,1)S(1)} %pad_maximum_fusion.1), channel_id=1, source_target_pairs={{0,256},{128,384},{256,0},{384,128},{1,257},{129,385},{257,1},{385... | collective-permute-start | bytes 393224 | tf_op jit(solution)/shard_map/ppermute | solution.py:35
  121.0 5.8 %collective-permute-done.6 = bf16[256,256]{1,0:T(8,128)(2,1)S(1)} collective-permute-done((bf16[256,256]{1,0:T(8,128)(2,1)S(1)}, bf16[256,256]{1,0:T(8,128)(2,1)S(1)}, u32[]{:S(2)}, u32[]{:S(2)}) %collective-permute-start.6) | collective-permute-done | bytes 131104 | tf_op jit(solution)/shard_map/ppermute | solution.py:35
  126.9 1.9 %collective-permute-start.7 = (bf16[512,256]{1,0:T(8,128)(2,1)S(1)}, bf16[512,256]{1,0:T(8,128)(2,1)S(1)}, u32[]{:S(2)}, u32[]{:S(2)}) collective-permute-start(bf16[512,256]{1,0:T(8,128)(2,1)S(1)} %get-tuple-element.9), channel_id=1, source_target_pairs={{0,16},{16,0},{1,17},{17,1},{2,18},{18,2},{3,19},{19,3},{4,20},{20... | collective-permute-start | bytes 786440 | tf_op jit(solution)/shard_map/ppermute | solution.py:35
  128.8 1.5 collective-permute-done.7
  130.3 0.6 fusion.15
  131.1 0.6 fusion
  131.7 27.7 %all_to_all.26.parts_ref = bf16[16,8,2048]{2,1,0:T(8,128)(2,1)S(1)} all-to-all(bf16[16,8,2048]{2,1,0:T(8,128)(2,1)S(1)} %fusion), channel_id=1, replica_groups=mesh['y'=4,'h'=4,'c'=2,'z'=4,'x'=4] {'z','x'}, dimensions={0} | all-to-all | bytes 1048576 | tf_op jit(solution)/shard_map/all_to_all | solution.py:39
  159.3 0.7 last_sum.1
  (37 shorter events, 0.6 us)
Async XLA Ops:
  0.0 131.1 %copy-start = (bf16[128,2048]{1,0:T(8,128)(2,1)S(1)}, bf16[128,2048]{1,0:T(8,128)(2,1)}, u32[]{:S(2)}) copy-start(bf16[128,2048]{1,0:T(8,128)(2,1)} %param.25) | copy-start | bytes 1572868
  2.8 6.0 %copy-start.4 = (bf16[128,2048]{1,0:T(8,128)(2,1)S(1)}, bf16[128,2048]{1,0:T(8,128)(2,1)}, u32[]{:S(2)}) copy-start(bf16[128,2048]{1,0:T(8,128)(2,1)} %param.16) | copy-start | bytes 1572868
  2.8 6.0 %copy-start.5 = (bf16[2048,128]{1,0:T(8,128)(2,1)S(1)}, bf16[2048,128]{1,0:T(8,128)(2,1)}, u32[]{:S(2)}) copy-start(bf16[2048,128]{1,0:T(8,128)(2,1)} %param.17) | copy-start | bytes 1572868
  2.8 6.0 %copy-start.8 = (bf16[1024,128]{1,0:T(8,128)(2,1)S(1)}, bf16[1024,128]{1,0:T(8,128)(2,1)}, u32[]{:S(2)}) copy-start(bf16[1024,128]{1,0:T(8,128)(2,1)} %param.18) | copy-start | bytes 786436
  2.8 42.5 %all-to-all-start = ((bf16[4,136,1024]{2,1,0:T(8,128)(2,1)}), bf16[4,136,1024]{2,1,0:T(8,128)(2,1)}, u32[]{:S(2)}, u32[]{:S(2)}) async-start(bf16[4,136,1024]{2,1,0:T(8,128)(2,1)} %key_copies.1), calls=%async_computation | async-start | bytes 2228224 | tf_op jit(solution)/shard_map/all_to_all | solution.py:39
  8.8 1.0 copy-start.9
  9.8 8.2 %copy-start.6 = (bf16[1024,256]{1,0:T(8,128)(2,1)}, bf16[1024,256]{1,0:T(8,128)(2,1)S(1)}, u32[]{:S(2)}) copy-start(bf16[1024,256]{1,0:T(8,128)(2,1)S(1)} %pad_maximum_fusion.refs_1_) | copy-start | bytes 1572868
  9.8 50.4 %copy-start.1 = (bf16[128,2048]{1,0:T(8,128)(2,1)S(1)}, bf16[128,2048]{1,0:T(8,128)(2,1)}, u32[]{:S(2)}) copy-start(bf16[128,2048]{1,0:T(8,128)(2,1)} %weight_ref.1) | copy-start | bytes 1572868
  9.8 16.8 %collective-permute-start = (bf16[1024,256]{1,0:T(8,128)(2,1)S(1)}, bf16[1024,256]{1,0:T(8,128)(2,1)S(1)}, u32[]{:S(2)}, u32[]{:S(2)}) collective-permute-start(bf16[1024,256]{1,0:T(8,128)(2,1)S(1)} %pad_maximum_fusion.refs_1_), channel_id=1, source_target_pairs={{0,1},{1,0},{2,3},{3,2},{4,5},{5,4},{6,7},{7,6},{8,9},{9,8},{10,11... | collective-permute-start | bytes 1572872 | tf_op jit(solution)/shard_map/ppermute | solution.py:35
  13.4 25.4 %collective-permute-start.1 = (bf16[1024,256]{1,0:T(8,128)(2,1)S(1)}, bf16[1024,256]{1,0:T(8,128)(2,1)S(1)}, u32[]{:S(2)}, u32[]{:S(2)}) collective-permute-start(bf16[1024,256]{1,0:T(8,128)(2,1)S(1)} %pad_maximum_fusion.refs_1_), channel_id=1, source_target_pairs={{0,2},{1,3},{2,0},{3,1},{4,6},{5,7},{6,4},{7,5},{8,10},{9,11},{10,... | collective-permute-start | bytes 1572872 | tf_op jit(solution)/shard_map/ppermute | solution.py:35
  18.0 27.3 %collective-permute-start.2 = (bf16[1024,256]{1,0:T(8,128)(2,1)S(1)}, bf16[1024,256]{1,0:T(8,128)(2,1)}, u32[]{:S(2)}, u32[]{:S(2)}) collective-permute-start(bf16[1024,256]{1,0:T(8,128)(2,1)S(1)} %pad_maximum_fusion.refs_1_), channel_id=1, source_target_pairs={{0,3},{1,2},{2,1},{3,0},{4,7},{5,6},{6,5},{7,4},{8,11},{9,10},{10,... | collective-permute-start | bytes 1572872 | tf_op jit(solution)/shard_map/ppermute | solution.py:35
  26.7 12.1 %copy-start.10 = (bf16[1024,256]{1,0:T(8,128)(2,1)}, bf16[1024,256]{1,0:T(8,128)(2,1)S(1)}, u32[]{:S(2)}) copy-start(bf16[1024,256]{1,0:T(8,128)(2,1)S(1)} %collective-permute-done.refs_2_) | copy-start | bytes 1572868
  38.8 0.8 copy-start.11
  61.4 23.5 %copy-start.2 = (bf16[2048,128]{1,0:T(8,128)(2,1)S(1)}, bf16[2048,128]{1,0:T(8,128)(2,1)}, u32[]{:S(2)}) copy-start(bf16[2048,128]{1,0:T(8,128)(2,1)} %key_ref.1) | copy-start | bytes 1572868
  61.4 23.5 %copy-start.3 = (bf16[2048,128]{1,0:T(8,128)(2,1)S(1)}, bf16[2048,128]{1,0:T(8,128)(2,1)}, u32[]{:S(2)}) copy-start(bf16[2048,128]{1,0:T(8,128)(2,1)} %value_ref.1) | copy-start | bytes 1572868
  61.4 18.3 %all-to-all-start.2 = ((bf16[16,8,2048]{2,1,0:T(8,128)(2,1)}), bf16[16,8,2048]{2,1,0:T(8,128)(2,1)S(1)}, u32[]{:S(2)}, u32[]{:S(2)}) async-start(bf16[16,8,2048]{2,1,0:T(8,128)(2,1)} %bitcast.1), calls=%async_computation.2 | async-start | bytes 1048576 | tf_op jit(solution)/shard_map/all_to_all | solution.py:39
  80.7 49.6 %all-to-all-start.3 = ((bf16[16,8,2048]{2,1,0:T(8,128)(2,1)}), bf16[16,8,2048]{2,1,0:T(8,128)(2,1)S(1)}, u32[]{:S(2)}, u32[]{:S(2)}) async-start(bf16[16,8,2048]{2,1,0:T(8,128)(2,1)} %get-tuple-element.7), calls=%async_computation.3 | async-start | bytes 1048576 | tf_op jit(solution)/shard_map/all_to_all | solution.py:39
  85.2 45.1 %copy-start.7 = (bf16[2048,128]{1,0:T(8,128)(2,1)S(1)}, bf16[2048,128]{1,0:T(8,128)(2,1)}, u32[]{:S(2)}) copy-start(bf16[2048,128]{1,0:T(8,128)(2,1)} %param.22) | copy-start | bytes 1572868
  85.2 11.1 %collective-permute-start.3 = (bf16[32,256]{1,0:T(8,128)(2,1)S(1)}, bf16[32,256]{1,0:T(8,128)(2,1)S(1)}, u32[]{:S(2)}, u32[]{:S(2)}) collective-permute-start(bf16[32,256]{1,0:T(8,128)(2,1)S(1)} %decode_pairs.1), channel_id=1, source_target_pairs={{0,32},{32,0},{64,96},{96,64},{1,33},{33,1},{65,97},{97,65},{2,34}... | collective-permute-start | bytes 49160 | tf_op jit(solution)/shard_map/ppermute | solution.py:35
  96.3 15.4 %collective-permute-start.4 = (bf16[64,256]{1,0:T(8,128)(2,1)S(1)}, bf16[64,256]{1,0:T(8,128)(2,1)S(1)}, u32[]{:S(2)}, u32[]{:S(2)}) collective-permute-start(bf16[64,256]{1,0:T(8,128)(2,1)S(1)} %pad_maximum_fusion.3), channel_id=1, source_target_pairs={{0,64},{32,96},{64,0},{96,32},{1,65},{33,97},{65,1},{97,33},{2,66}... | collective-permute-start | bytes 98312 | tf_op jit(solution)/shard_map/ppermute | solution.py:35
  111.7 6.8 %collective-permute-start.5 = (bf16[128,256]{1,0:T(8,128)(2,1)S(1)}, bf16[128,256]{1,0:T(8,128)(2,1)S(1)}, u32[]{:S(2)}, u32[]{:S(2)}) collective-permute-start(bf16[128,256]{1,0:T(8,128)(2,1)S(1)} %pad_maximum_fusion.2), channel_id=1, source_target_pairs={{0,128},{128,0},{256,384},{384,256},{1,129},{129,1},{257,385},{385... | collective-permute-start | bytes 196616 | tf_op jit(solution)/shard_map/ppermute | solution.py:35
  118.5 8.4 %collective-permute-start.6 = (bf16[256,256]{1,0:T(8,128)(2,1)S(1)}, bf16[256,256]{1,0:T(8,128)(2,1)S(1)}, u32[]{:S(2)}, u32[]{:S(2)}) collective-permute-start(bf16[256,256]{1,0:T(8,128)(2,1)S(1)} %pad_maximum_fusion.1), channel_id=1, source_target_pairs={{0,256},{128,384},{256,0},{384,128},{1,257},{129,385},{257,1},{385... | collective-permute-start | bytes 393224 | tf_op jit(solution)/shard_map/ppermute | solution.py:35
  126.9 3.4 %collective-permute-start.7 = (bf16[512,256]{1,0:T(8,128)(2,1)S(1)}, bf16[512,256]{1,0:T(8,128)(2,1)S(1)}, u32[]{:S(2)}, u32[]{:S(2)}) collective-permute-start(bf16[512,256]{1,0:T(8,128)(2,1)S(1)} %get-tuple-element.9), channel_id=1, source_target_pairs={{0,16},{16,0},{1,17},{17,1},{2,18},{18,2},{3,19},{19,3},{4,20},{20... | collective-permute-start | bytes 786440 | tf_op jit(solution)/shard_map/ppermute | solution.py:35

commit v2 on v1

--- a/solution.py
+++ b/solution.py
@@ -18,7 +18,6 @@
 F32 = jnp.float32
 SCALE = HEAD ** (-0.5)
 TAIL = 16
-EXTRA = 8
 PARAMS = pltpu.CompilerParams(vmem_limit_bytes=20 * 2**20)
 WIDE = pltpu.CompilerParams(vmem_limit_bytes=62 * 2**20)
 
@@ -39,108 +38,102 @@
     return lax.all_to_all(tiles, axis, split_axis=0, concat_axis=0, tiled=True)
 
 
+def all_from(value, axis):
+    copies = jnp.broadcast_to(value, (lax.axis_size(axis), *value.shape))
+    return exchange(copies, axis)
+
+
 def cost(flops, size):
     return pl.CostEstimate(flops=flops, bytes_accessed=size, transcendentals=0)
 
 
-def key_kernel(slot_ref, group_ref, embed_ref, global_ref, out_ref):
+def key_kernel(slot_ref, group_ref, embed_ref, out_ref):
     lines = lax.broadcasted_iota(jnp.int32, embed_ref.shape, 0)
     chosen = jnp.where(lines == slot_ref[0, 0], embed_ref[...].astype(F32), 0.0)
     keyed = group_ref[...].astype(F32) + jnp.sum(chosen, axis=0, keepdims=True)
-    length, width = group_ref.shape
-    latents = global_ref[...].astype(F32)
-    rest = jnp.zeros((out_ref.shape[1] - length - 4, width), F32)
-    tail = jnp.concatenate([latents[:, :width], latents[:, width:], rest], axis=0)
-    block = jnp.concatenate([keyed, tail], axis=0).astype(BF16)
+    block = keyed.astype(BF16)
     for j in range(out_ref.shape[0]):
         out_ref[j] = block
 
 
-def key_copies(slot_ids, group_latents, slot_embed, global_latents, many):
-    length, width = group_latents.shape
+def key_copies(slot_ids, group_latents, slot_embed, many):
     return pl.pallas_call(
         key_kernel,
-        out_shape=jax.ShapeDtypeStruct((many, length + EXTRA, width), BF16),
-        in_specs=[pl.BlockSpec(memory_space=pltpu.SMEM), VMEM, VMEM, VMEM],
+        out_shape=jax.ShapeDtypeStruct((many, *group_latents.shape), BF16),
+        in_specs=[pl.BlockSpec(memory_space=pltpu.SMEM), VMEM, VMEM],
         out_specs=VMEM,
         compiler_params=WIDE,
         cost_estimate=cost(4 * group_latents.size, 2**20),
         name="key_copies",
-    )(slot_ids, group_latents, slot_embed, global_latents)
-
-
-def attend_kernel(*refs):
-    blocks_ref, packs, out_ref = refs[0], refs[1:-1], refs[-1]
+    )(slot_ids, group_latents, slot_embed)
+
+
+def attend_one(blocks_ref, pack):
+    many = blocks_ref.shape[0]
+    both = [dot(blocks_ref[j], pack, ((1,), (0,))) for j in range(many)]
+    scores = jnp.concatenate([b[:, :-HEAD] for b in both], axis=0) * SCALE
+    values = jnp.concatenate([b[:, -HEAD:].astype(BF16) for b in both], axis=0)
+    top = jnp.max(scores, axis=0, keepdims=True)
+    weights = jnp.exp(scores - top)
+    total = jnp.sum(weights, axis=0, keepdims=True)
+    mixed = dot(values, weights.astype(BF16), ((0,), (0,))) / total
+    level = top + jnp.log(total)
+    high = level.astype(BF16).astype(F32)
+    middle = (level - high).astype(BF16).astype(F32)
+    low = level - high - middle
+    line = lax.broadcasted_iota(jnp.int32, (TAIL, mixed.shape[1]), 0)
+    tail = jnp.where(line == 0, high, jnp.where(line == 1, middle, jnp.where(line == 2, low, 0.0)))
+    return jnp.concatenate([mixed, tail], axis=0).astype(BF16)
+
+
+def first_kernel(blocks_ref, *refs):
+    out_ref = refs[-1]
+    for k, pack_ref in enumerate(refs[:-1]):
+        out_ref[k] = attend_one(blocks_ref, pack_ref[...])
+
+
+def second_kernel(steps, blocks_ref, done_ref, *refs):
+    out_ref = refs[-1]
     mine = lax.axis_index("x")
-    many, length = blocks_ref.shape[0], blocks_ref.shape[1] - EXTRA
-    tails = [blocks_ref[j, length:, :].astype(F32) for j in range(many)]
-    latents = jnp.concatenate(
-        [
-            jnp.concatenate([tail[:2] for tail in tails], axis=0),
-            jnp.concatenate([tail[2:4] for tail in tails], axis=0),
-        ],
-        axis=1,
-    )
-    pieces = [latents[:, k : k + HEAD] for k in range(0, latents.shape[1], HEAD)]
-    for step, pack_ref in enumerate(packs):
-        place = mine ^ step
-        pack = pack_ref[...]
-        both = [dot(blocks_ref[j, :length, :], pack, ((1,), (0,))) for j in range(many)]
-        scores = jnp.concatenate([b[:, :-HEAD] for b in both], axis=0) * SCALE
-        values = jnp.concatenate([b[:, -HEAD:].astype(BF16) for b in both], axis=0)
-        top = jnp.max(scores, axis=0, keepdims=True)
-        weights = jnp.exp(scores - top)
-        total = jnp.sum(weights, axis=0, keepdims=True)
-        mixed = dot(values, weights.astype(BF16), ((0,), (0,))) / total
-        level = top + jnp.log(total)
-        high = level.astype(BF16).astype(F32)
-        middle = (level - high).astype(BF16).astype(F32)
-        low = level - high - middle
-        line = lax.broadcasted_iota(jnp.int32, (TAIL, mixed.shape[1]), 0)
-        tail = jnp.where(line == 0, high, jnp.where(line == 1, middle, jnp.where(line == 2, low, 0.0)))
-        out_ref[place] = jnp.concatenate([mixed, tail, *pieces], axis=0).astype(BF16)
-
-
-def attend_part(blocks, packs):
-    many, length = len(packs), packs[0].shape[1] - HEAD
+    for k in range(done_ref.shape[0]):
+        out_ref[mine ^ steps[k]] = done_ref[k]
+    for k, pack_ref in enumerate(refs[:-1]):
+        out_ref[mine ^ steps[done_ref.shape[0] + k]] = attend_one(blocks_ref, pack_ref[...])
+
+
+def attend_part(blocks, packs, done=None, steps=None):
+    length = packs[0].shape[1] - HEAD
+    many = len(packs) + (0 if done is None else done.shape[0])
     keys = blocks.shape[0] * blocks.shape[1]
-    flops = 2 * many * keys * (blocks.shape[2] * 2 * HEAD + HEAD * length)
-    height = HEAD + TAIL + 2 * blocks.shape[0] * 2 * blocks.shape[2] // HEAD
-    return pl.pallas_call(
-        attend_kernel,
-        out_shape=jax.ShapeDtypeStruct((many, height, length), BF16),
-        in_specs=[VMEM] * (1 + many),
+    flops = 2 * len(packs) * keys * (blocks.shape[2] * 2 * HEAD + HEAD * length)
+    given = [blocks] if done is None else [blocks, done]
+    return pl.pallas_call(
+        first_kernel if done is None else functools.partial(second_kernel, steps),
+        out_shape=jax.ShapeDtypeStruct((many, HEAD + TAIL, length), BF16),
+        in_specs=[VMEM] * (len(given) + len(packs)),
         out_specs=VMEM,
         compiler_params=WIDE,
         cost_estimate=cost(flops, 3 * 2**20),
-        name="attend_part",
-    )(blocks, *packs)
+        name="attend_first" if done is None else "attend_second",
+    )(*given, *packs)
 
 
 def pair_kernel(parts_ref, key_ref, value_ref, out_ref):
-    many, height, _ = parts_ref.shape
-    lines = []
-    for j in range(many):
-        pieces = [
-            parts_ref[j, k : k + 8, :].astype(F32) for k in range(HEAD + TAIL, height, 8)
-        ]
-        lines.append(jnp.concatenate(pieces, axis=1))
+    lines = [parts_ref[j].astype(F32) for j in range(parts_ref.shape[0])]
     latents = jnp.concatenate(lines, axis=0).astype(BF16)
     out_ref[:, :HEAD] = dot(latents, key_ref[...], ((1,), (0,))).astype(BF16)
     out_ref[:, HEAD:] = dot(latents, value_ref[...], ((1,), (0,))).astype(BF16)
 
 
 def decode_pairs(parts, key_weight, value_weight):
-    many, height, length = parts.shape
-    size = many * (height - HEAD - TAIL) * length
-    rows = size // key_weight.shape[0]
+    rows = parts.shape[0] * parts.shape[1]
     return pl.pallas_call(
         pair_kernel,
         out_shape=jax.ShapeDtypeStruct((rows, 2 * HEAD), BF16),
         in_specs=[VMEM, VMEM, VMEM],
         out_specs=VMEM,
         compiler_params=PARAMS,
-        cost_estimate=cost(4 * size * HEAD, 2**20),
+        cost_estimate=cost(4 * parts.size * HEAD, 2**20),
         name="decode_pairs",
     )(parts, key_weight, value_weight)
 
@@ -242,16 +235,18 @@
     pack = jnp.concatenate([folded, value_weight], axis=1)
     own_rows = lax.dynamic_slice_in_dim(merge_latents, lax.axis_index(INNER) * rows, rows, 0)
 
-    copies = key_copies(slot_ids, group_latents, slot_embed, global_latents, lax.axis_size("z"))
+    copies = key_copies(slot_ids, group_latents, slot_embed, lax.axis_size("z"))
     blocks = exchange(copies, "z")
     pack_two = partner(pack, "x", 2)
     pack_three = partner(pack, "x", 3)
     pack_one = partner(pack, "x", 1)
-    parts = attend_part(blocks, [pack, pack_one, pack_two, pack_three])
+    done = attend_part(blocks, [pack, pack_two])
+    outer_block = all_from(global_latents, INNER)
+    parts = attend_part(blocks, [pack_three, pack_one], done, (0, 2, 3, 1))
     parts = exchange(parts, "x")
 
-    pairs = decode_pairs(parts, decode_key, decode_value)
-    for axis, step_size in (("h", 1), ("h", 2), ("y", 1), ("y", 2)):
+    pairs = decode_pairs(outer_block, decode_key, decode_value)
+    for axis, step_size in (("h", 1), ("h", 3), ("y", 1), ("y", 3)):
         if lax.axis_size(axis) > step_size:
             pairs = jnp.concatenate([pairs, partner(pairs, axis, step_size)], axis=0)
     other = partner(pairs, "c", 1)

time: 161 us -> 161 us (level)
  blocking collectives: 37.8 us -> 55.8 us
  waiting for transfers between devices: 51.8 us -> 35.9 us
  starting transfers between devices: 56.3 us -> 49.9 us
  other arithmetic: 0.24 us -> 1.99 us
    all_to_all x2 -> x3, blocking collectives: 37.8 us -> 55.8 us  [exchange(): return lax.all_to_all(tiles, axis, split_axis=0, concat_axis=0, tiled=True)]
    ppermute x8, waiting for transfers between devices: 39.2 us -> 23.9 us  [partner(): return lax.ppermute(value, axis, pairs)]
    ppermute x8, starting transfers between devices: 40.4 us -> 35.7 us  [partner(): return lax.ppermute(value, axis, pairs)]
    pallas_call x2 -> x3, Pallas kernels: 6.75 us -> 8.76 us  [the longest x2 6.72 us: attend_part(): pl.pallas_call(first_kernel if done is None else functools.partial(second...]
    all_to_all x3, starting transfers between devices: 15.9 us -> 14.1 us  [exchange(): return lax.all_to_all(tiles, axis, split_axis=0, concat_axis=0, tiled=True)]
    concatenate x1, other arithmetic: 0.06 us -> 1.81 us  [step(): pack = jnp.concatenate([folded, value_weight], axis=1)]
  transfers between devices with their start and end apart: 11 -> 11, of which waited for: 9 -> 10; matrix products, arithmetic and copies ran while one was open for 0% -> 2% of each run, Pallas kernels for 0% -> 3%
where the time goes in v2:
time: 161 us; the launch traced here: 160 us
  blocking collectives  55.8 us (35%)
  starting transfers between devices  49.9 us (31%)
  waiting for transfers between devices  35.9 us (22%)
  Pallas kernels  11.1 us (7%)
  local copies, waits for them, and re-layouts  2.59 us (2%)
  other arithmetic  1.99 us (1%)
  matrix products  1.62 us (1%)
    all_to_all x3, blocking collectives, exchange(): return lax.all_to_all(tiles, axis, split_axis=0, concat_axis=0, tiled=True)  55.8 us
    ppermute x8, starting transfers between devices, partner(): return lax.ppermute(value, axis, pairs)  35.7 us
    ppermute x8, waiting for transfers between devices, partner(): return lax.ppermute(value, axis, pairs)  23.9 us
    all_to_all x3, starting transfers between devices, exchange(): return lax.all_to_all(tiles, axis, split_axis=0, concat_axis=0, tiled=True)  14.1 us
    all_to_all x3, waiting for transfers between devices, exchange(): return lax.all_to_all(tiles, axis, split_axis=0, concat_axis=0, tiled=True)  12 us
    pallas_call x2, Pallas kernels, attend_part(): pl.pallas_call(first_kernel if done is None else functools.partial(second...  6.72 us
  transfers between devices with their start and end apart: 11, of which 10 were waited for; matrix products, arithmetic and copies ran while one was open for 2% of the time, Pallas kernels for 3%

profile of v2, /device:TPU:24, one launch (start us, length us, event | category | flops | bytes accessed | tf_op | source)
XLA Modules:
  0.0 159.8 jit_solution(723807682482799779)
XLA Ops:
  0.7 2.0 %key_copies.1 = bf16[4,128,1024]{2,1,0:T(8,128)(2,1)} custom-call(s32[1,1]{1,0:T(1,128)S(6)} %copy.25.slot_ref, bf16[128,1024]{1,0:T(8,128)(2,1)} %group_ref.1, bf16[16,1024]{1,0:T(8,128)(2,1)} %embed_ref.1), custom_call_target="tpu_custom_call" | custom-call | flops 524288 | bytes 1048576 | tf_op jit(solution)/shard_map/key_copies/pallas_call | solution.py:60
  2.8 6.0 %all-to-all-start.1 = ((bf16[4,128,1024]{2,1,0:T(8,128)(2,1)}), bf16[4,128,1024]{2,1,0:T(8,128)(2,1)S(1)}, u32[]{:S(2)}, u32[]{:S(2)}) async-start(bf16[4,128,1024]{2,1,0:T(8,128)(2,1)} %key_copies.1), calls=%async_computation.1 | async-start | bytes 2097152 | tf_op jit(solution)/shard_map/all_to_all | solution.py:38
  9.3 1.8 %pad_maximum_fusion.refs_0_ = bf16[1024,256]{1,0:T(8,128)(2,1)} fusion(bf16[1024,128]{1,0:T(8,128)(2,1)} %param.19, bf16[1024,128]{1,0:T(8,128)(2,1)S(1)} %fusion.1), kind=kLoop, calls=%fused_computation.9 | loop fusion | flops 1048576 | bytes 1048576 | tf_op jit(solution)/shard_map/concatenate | solution.py:235
  11.1 4.9 %collective-permute-start.5 = (bf16[1024,256]{1,0:T(8,128)(2,1)}, bf16[1024,256]{1,0:T(8,128)(2,1)}, u32[]{:S(2)}, u32[]{:S(2)}) collective-permute-start(bf16[1024,256]{1,0:T(8,128)(2,1)} %pad_maximum_fusion.refs_0_), channel_id=1, source_target_pairs={{0,2},{1,3},{2,0},{3,1},{4,6},{5,7},{6,4},{7,5},{8,10},{9,11},{10,... | collective-permute-start | bytes 1572872 | tf_op jit(solution)/shard_map/ppermute | solution.py:34
  16.0 3.0 %collective-permute-start.6 = (bf16[1024,256]{1,0:T(8,128)(2,1)}, bf16[1024,256]{1,0:T(8,128)(2,1)}, u32[]{:S(2)}, u32[]{:S(2)}) collective-permute-start(bf16[1024,256]{1,0:T(8,128)(2,1)} %pad_maximum_fusion.refs_0_), channel_id=1, source_target_pairs={{0,3},{1,2},{2,1},{3,0},{4,7},{5,6},{6,5},{7,4},{8,11},{9,10},{10,... | collective-permute-start | bytes 1572872 | tf_op jit(solution)/shard_map/ppermute | solution.py:34
  19.1 1.9 %collective-permute-start.7 = (bf16[1024,256]{1,0:T(8,128)(2,1)}, bf16[1024,256]{1,0:T(8,128)(2,1)}, u32[]{:S(2)}, u32[]{:S(2)}) collective-permute-start(bf16[1024,256]{1,0:T(8,128)(2,1)} %pad_maximum_fusion.refs_0_), channel_id=1, source_target_pairs={{0,1},{1,0},{2,3},{3,2},{4,5},{5,4},{6,7},{7,6},{8,9},{9,8},{10,11... | collective-permute-start | bytes 1572872 | tf_op jit(solution)/shard_map/ppermute | solution.py:34
  21.0 8.6 %collective-permute-done.5.refs_1_ = bf16[1024,256]{1,0:T(8,128)(2,1)} collective-permute-done((bf16[1024,256]{1,0:T(8,128)(2,1)}, bf16[1024,256]{1,0:T(8,128)(2,1)}, u32[]{:S(2)}, u32[]{:S(2)}) %collective-permute-start.5) | collective-permute-done | bytes 524320 | tf_op jit(solution)/shard_map/ppermute | solution.py:34
  29.6 4.9 %all-to-all-done.1.blocks_ref = bf16[4,128,1024]{2,1,0:T(8,128)(2,1)S(1)} async-done(((bf16[4,128,1024]{2,1,0:T(8,128)(2,1)}), bf16[4,128,1024]{2,1,0:T(8,128)(2,1)S(1)}, u32[]{:S(2)}, u32[]{:S(2)}) %all-to-all-start.1) | async-done | bytes 1048608 | tf_op jit(solution)/shard_map/all_to_all | solution.py:38
  34.5 1.0 copy-done.4
  35.5 3.3 %attend_first.1.done_ref = bf16[2,144,128]{2,1,0:T(8,128)(2,1)} custom-call(bf16[4,128,1024]{2,1,0:T(8,128)(2,1)} %copy-done.4, bf16[1024,256]{1,0:T(8,128)(2,1)} %pad_maximum_fusion.refs_0_, bf16[1024,256]{1,0:T(8,128)(2,1)} %collective-permute-done.5.refs_1_), custom_call_target="tpu_custom_call" | custom-call | flops 570425344 | bytes 3145728 | tf_op jit(solution)/shard_map/attend_first/pallas_call | solution.py:110
  38.8 0.6 collective-permute-done.6.refs_0_
  39.5 3.4 %attend_second.1 = bf16[4,144,128]{2,1,0:T(8,128)(2,1)} custom-call(bf16[4,128,1024]{2,1,0:T(8,128)(2,1)} %copy-done.4, bf16[2,144,128]{2,1,0:T(8,128)(2,1)} %attend_first.1.done_ref, bf16[1024,256]{1,0:T(8,128)(2,1)} %collective-permute-done.6.refs_0_, bf16[1024,256]{1,0:T(8,128)(2,1)} %collective-permute-done.7.refs_1_), custom_call_target="tpu_custom_call" | custom-call | flops 570425344 | bytes 3145728 | tf_op jit(solution)/shard_map/attend_second/pallas_call | solution.py:110
  43.0 10.2 %all_to_all.30.parts_ref = bf16[4,144,128]{2,1,0:T(8,128)(2,1)S(1)} all-to-all(bf16[4,144,128]{2,1,0:T(8,128)(2,1)} %attend_second.1), channel_id=1, replica_groups=mesh['y'=4,'h'=4,'c'=2,'z'=4,'x'=4] {'x'}, dimensions={0} | all-to-all | bytes 294912 | tf_op jit(solution)/shard_map/all_to_all | solution.py:38
  53.6 19.9 %all_to_all.31.parts_ref = bf16[16,8,2048]{2,1,0:T(8,128)(2,1)S(1)} all-to-all(bf16[16,8,2048]{2,1,0:T(8,128)(2,1)S(1)} %bitcast.16), channel_id=1, replica_groups=mesh['y'=4,'h'=4,'c'=2,'z'=4,'x'=4] {'z','x'}, dimensions={0} | all-to-all | bytes 1048576 | tf_op jit(solution)/shard_map/all_to_all | solution.py:38
  73.4 0.7 broadcast_in_dim.2
  74.2 4.4 %all-to-all-start = ((bf16[16,2,2048]{2,1,0:T(2,128)(2,1)}), bf16[16,2,2048]{2,1,0:T(2,128)(2,1)S(1)}, u32[]{:S(2)}, u32[]{:S(2)}) async-start(bf16[16,2,2048]{2,1,0:T(2,128)(2,1)} %broadcast_in_dim.2), calls=%async_computation | async-start | bytes 262144 | tf_op jit(solution)/shard_map/all_to_all | solution.py:38
  78.6 0.8 constant_dynamic-slice_fusion.own_ref
  79.4 1.0 sum_and_norm.1
  80.4 7.1 %all-to-all-done.parts_ref = bf16[16,2,2048]{2,1,0:T(2,128)(2,1)S(1)} async-done(((bf16[16,2,2048]{2,1,0:T(2,128)(2,1)}), bf16[16,2,2048]{2,1,0:T(2,128)(2,1)S(1)}, u32[]{:S(2)}, u32[]{:S(2)}) %all-to-all-start) | async-done | bytes 131104 | tf_op jit(solution)/shard_map/all_to_all | solution.py:38
  87.5 3.7 %all-to-all-start.4 = ((bf16[16,8,2048]{2,1,0:T(8,128)(2,1)}), bf16[16,8,2048]{2,1,0:T(8,128)(2,1)S(1)}, u32[]{:S(2)}, u32[]{:S(2)}) async-start(bf16[16,8,2048]{2,1,0:T(8,128)(2,1)} %get-tuple-element.7), calls=%async_computation.4 | async-start | bytes 1048576 | tf_op jit(solution)/shard_map/all_to_all | solution.py:38
  91.5 9.1 %collective-permute-start = (bf16[32,256]{1,0:T(8,128)(2,1)S(1)}, bf16[32,256]{1,0:T(8,128)(2,1)S(1)}, u32[]{:S(2)}, u32[]{:S(2)}) collective-permute-start(bf16[32,256]{1,0:T(8,128)(2,1)S(1)} %decode_pairs.1), channel_id=1, source_target_pairs={{0,32},{32,0},{64,96},{96,64},{1,33},{33,1},{65,97},{97,65},{2,34}... | collective-permute-start | bytes 49160 | tf_op jit(solution)/shard_map/ppermute | solution.py:34
  100.6 1.8 %collective-permute-done = bf16[32,256]{1,0:T(8,128)(2,1)S(1)} collective-permute-done((bf16[32,256]{1,0:T(8,128)(2,1)S(1)}, bf16[32,256]{1,0:T(8,128)(2,1)S(1)}, u32[]{:S(2)}, u32[]{:S(2)}) %collective-permute-start) | collective-permute-done | bytes 16416 | tf_op jit(solution)/shard_map/ppermute | solution.py:34
  102.4 10.1 %collective-permute-start.1 = (bf16[64,256]{1,0:T(8,128)(2,1)S(1)}, bf16[64,256]{1,0:T(8,128)(2,1)S(1)}, u32[]{:S(2)}, u32[]{:S(2)}) collective-permute-start(bf16[64,256]{1,0:T(8,128)(2,1)S(1)} %pad_maximum_fusion.3), channel_id=1, source_target_pairs={{0,96},{32,64},{64,32},{96,0},{1,97},{33,65},{65,33},{97,1},{2,98}... | collective-permute-start | bytes 98312 | tf_op jit(solution)/shard_map/ppermute | solution.py:34
  112.5 1.9 %collective-permute-done.1 = bf16[64,256]{1,0:T(8,128)(2,1)S(1)} collective-permute-done((bf16[64,256]{1,0:T(8,128)(2,1)S(1)}, bf16[64,256]{1,0:T(8,128)(2,1)S(1)}, u32[]{:S(2)}, u32[]{:S(2)}) %collective-permute-start.1) | collective-permute-done | bytes 32800 | tf_op jit(solution)/shard_map/ppermute | solution.py:34
  114.4 2.6 %collective-permute-start.2 = (bf16[128,256]{1,0:T(8,128)(2,1)S(1)}, bf16[128,256]{1,0:T(8,128)(2,1)S(1)}, u32[]{:S(2)}, u32[]{:S(2)}) collective-permute-start(bf16[128,256]{1,0:T(8,128)(2,1)S(1)} %pad_maximum_fusion.2), channel_id=1, source_target_pairs={{0,128},{128,0},{256,384},{384,256},{1,129},{129,1},{257,385},{385... | collective-permute-start | bytes 196616 | tf_op jit(solution)/shard_map/ppermute | solution.py:34
  117.1 3.5 %collective-permute-done.2 = bf16[128,256]{1,0:T(8,128)(2,1)S(1)} collective-permute-done((bf16[128,256]{1,0:T(8,128)(2,1)S(1)}, bf16[128,256]{1,0:T(8,128)(2,1)S(1)}, u32[]{:S(2)}, u32[]{:S(2)}) %collective-permute-start.2) | collective-permute-done | bytes 65568 | tf_op jit(solution)/shard_map/ppermute | solution.py:34
  120.6 2.1 %collective-permute-start.3 = (bf16[256,256]{1,0:T(8,128)(2,1)S(1)}, bf16[256,256]{1,0:T(8,128)(2,1)S(1)}, u32[]{:S(2)}, u32[]{:S(2)}) collective-permute-start(bf16[256,256]{1,0:T(8,128)(2,1)S(1)} %pad_maximum_fusion.1), channel_id=1, source_target_pairs={{0,384},{128,256},{256,128},{384,0},{1,385},{129,257},{257,129},{3... | collective-permute-start | bytes 393224 | tf_op jit(solution)/shard_map/ppermute | solution.py:34
  122.7 5.9 %collective-permute-done.3 = bf16[256,256]{1,0:T(8,128)(2,1)S(1)} collective-permute-done((bf16[256,256]{1,0:T(8,128)(2,1)S(1)}, bf16[256,256]{1,0:T(8,128)(2,1)S(1)}, u32[]{:S(2)}, u32[]{:S(2)}) %collective-permute-start.3) | collective-permute-done | bytes 131104 | tf_op jit(solution)/shard_map/ppermute | solution.py:34
  128.7 1.9 %collective-permute-start.4 = (bf16[512,256]{1,0:T(8,128)(2,1)S(1)}, bf16[512,256]{1,0:T(8,128)(2,1)S(1)}, u32[]{:S(2)}, u32[]{:S(2)}) collective-permute-start(bf16[512,256]{1,0:T(8,128)(2,1)S(1)} %get-tuple-element.9), channel_id=1, source_target_pairs={{0,16},{16,0},{1,17},{17,1},{2,18},{18,2},{3,19},{19,3},{4,20},{20... | collective-permute-start | bytes 786440 | tf_op jit(solution)/shard_map/ppermute | solution.py:34
  130.6 1.5 collective-permute-done.4
  133.4 25.7 %all_to_all.32.parts_ref = bf16[16,8,2048]{2,1,0:T(8,128)(2,1)S(1)} all-to-all(bf16[16,8,2048]{2,1,0:T(8,128)(2,1)S(1)} %fusion), channel_id=1, replica_groups=mesh['y'=4,'h'=4,'c'=2,'z'=4,'x'=4] {'z','x'}, dimensions={0} | all-to-all | bytes 1048576 | tf_op jit(solution)/shard_map/all_to_all | solution.py:38
  159.2 0.7 last_sum.1
  (36 shorter events, 2.7 us)
Async XLA Ops:
  0.0 132.9 %copy-start = (bf16[128,2048]{1,0:T(8,128)(2,1)S(1)}, bf16[128,2048]{1,0:T(8,128)(2,1)}, u32[]{:S(2)}) copy-start(bf16[128,2048]{1,0:T(8,128)(2,1)} %param.25) | copy-start | bytes 1572868
  2.8 6.0 %copy-start.5 = (bf16[128,2048]{1,0:T(8,128)(2,1)S(1)}, bf16[128,2048]{1,0:T(8,128)(2,1)}, u32[]{:S(2)}) copy-start(bf16[128,2048]{1,0:T(8,128)(2,1)} %param.16) | copy-start | bytes 1572868
  2.8 6.0 %copy-start.6 = (bf16[2048,128]{1,0:T(8,128)(2,1)S(1)}, bf16[2048,128]{1,0:T(8,128)(2,1)}, u32[]{:S(2)}) copy-start(bf16[2048,128]{1,0:T(8,128)(2,1)} %param.17) | copy-start | bytes 1572868
  2.8 6.0 %copy-start.8 = (bf16[1024,128]{1,0:T(8,128)(2,1)S(1)}, bf16[1024,128]{1,0:T(8,128)(2,1)}, u32[]{:S(2)}) copy-start(bf16[1024,128]{1,0:T(8,128)(2,1)} %param.18) | copy-start | bytes 786436
  2.8 31.8 %all-to-all-start.1 = ((bf16[4,128,1024]{2,1,0:T(8,128)(2,1)}), bf16[4,128,1024]{2,1,0:T(8,128)(2,1)S(1)}, u32[]{:S(2)}, u32[]{:S(2)}) async-start(bf16[4,128,1024]{2,1,0:T(8,128)(2,1)} %key_copies.1), calls=%async_computation.1 | async-start | bytes 2097152 | tf_op jit(solution)/shard_map/all_to_all | solution.py:38
  11.1 18.5 %collective-permute-start.5 = (bf16[1024,256]{1,0:T(8,128)(2,1)}, bf16[1024,256]{1,0:T(8,128)(2,1)}, u32[]{:S(2)}, u32[]{:S(2)}) collective-permute-start(bf16[1024,256]{1,0:T(8,128)(2,1)} %pad_maximum_fusion.refs_0_), channel_id=1, source_target_pairs={{0,2},{1,3},{2,0},{3,1},{4,6},{5,7},{6,4},{7,5},{8,10},{9,11},{10,... | collective-permute-start | bytes 1572872 | tf_op jit(solution)/shard_map/ppermute | solution.py:34
  16.0 23.4 %collective-permute-start.6 = (bf16[1024,256]{1,0:T(8,128)(2,1)}, bf16[1024,256]{1,0:T(8,128)(2,1)}, u32[]{:S(2)}, u32[]{:S(2)}) collective-permute-start(bf16[1024,256]{1,0:T(8,128)(2,1)} %pad_maximum_fusion.refs_0_), channel_id=1, source_target_pairs={{0,3},{1,2},{2,1},{3,0},{4,7},{5,6},{6,5},{7,4},{8,11},{9,10},{10,... | collective-permute-start | bytes 1572872 | tf_op jit(solution)/shard_map/ppermute | solution.py:34
  19.1 20.5 %collective-permute-start.7 = (bf16[1024,256]{1,0:T(8,128)(2,1)}, bf16[1024,256]{1,0:T(8,128)(2,1)}, u32[]{:S(2)}, u32[]{:S(2)}) collective-permute-start(bf16[1024,256]{1,0:T(8,128)(2,1)} %pad_maximum_fusion.refs_0_), channel_id=1, source_target_pairs={{0,1},{1,0},{2,3},{3,2},{4,5},{5,4},{6,7},{7,6},{8,9},{9,8},{10,11... | collective-permute-start | bytes 1572872 | tf_op jit(solution)/shard_map/ppermute | solution.py:34
  34.5 1.0 copy-start.4
  39.5 13.7 %copy-start.1 = (bf16[128,2048]{1,0:T(8,128)(2,1)S(1)}, bf16[128,2048]{1,0:T(8,128)(2,1)}, u32[]{:S(2)}) copy-start(bf16[128,2048]{1,0:T(8,128)(2,1)} %weight_ref.1) | copy-start | bytes 1572868
  53.6 19.9 %copy-start.9 = (bf16[2,2048]{1,0:T(2,128)(2,1)S(1)}, bf16[2,2048]{1,0:T(2,128)(2,1)}, u32[]{:S(2)}) copy-start(bf16[2,2048]{1,0:T(2,128)(2,1)} %param.21) | copy-start | bytes 24580
  74.2 13.3 %all-to-all-start = ((bf16[16,2,2048]{2,1,0:T(2,128)(2,1)}), bf16[16,2,2048]{2,1,0:T(2,128)(2,1)S(1)}, u32[]{:S(2)}, u32[]{:S(2)}) async-start(bf16[16,2,2048]{2,1,0:T(2,128)(2,1)} %broadcast_in_dim.2), calls=%async_computation | async-start | bytes 262144 | tf_op jit(solution)/shard_map/all_to_all | solution.py:38
  87.5 3.7 %copy-start.2 = (bf16[2048,128]{1,0:T(8,128)(2,1)S(1)}, bf16[2048,128]{1,0:T(8,128)(2,1)}, u32[]{:S(2)}) copy-start(bf16[2048,128]{1,0:T(8,128)(2,1)} %key_ref.1) | copy-start | bytes 1572868
  87.5 3.7 %copy-start.3 = (bf16[2048,128]{1,0:T(8,128)(2,1)S(1)}, bf16[2048,128]{1,0:T(8,128)(2,1)}, u32[]{:S(2)}) copy-start(bf16[2048,128]{1,0:T(8,128)(2,1)} %value_ref.1) | copy-start | bytes 1572868
  87.5 44.6 %all-to-all-start.4 = ((bf16[16,8,2048]{2,1,0:T(8,128)(2,1)}), bf16[16,8,2048]{2,1,0:T(8,128)(2,1)S(1)}, u32[]{:S(2)}, u32[]{:S(2)}) async-start(bf16[16,8,2048]{2,1,0:T(8,128)(2,1)} %get-tuple-element.7), calls=%async_computation.4 | async-start | bytes 1048576 | tf_op jit(solution)/shard_map/all_to_all | solution.py:38
  91.5 10.9 %collective-permute-start = (bf16[32,256]{1,0:T(8,128)(2,1)S(1)}, bf16[32,256]{1,0:T(8,128)(2,1)S(1)}, u32[]{:S(2)}, u32[]{:S(2)}) collective-permute-start(bf16[32,256]{1,0:T(8,128)(2,1)S(1)} %decode_pairs.1), channel_id=1, source_target_pairs={{0,32},{32,0},{64,96},{96,64},{1,33},{33,1},{65,97},{97,65},{2,34}... | collective-permute-start | bytes 49160 | tf_op jit(solution)/shard_map/ppermute | solution.py:34
  102.4 12.0 %collective-permute-start.1 = (bf16[64,256]{1,0:T(8,128)(2,1)S(1)}, bf16[64,256]{1,0:T(8,128)(2,1)S(1)}, u32[]{:S(2)}, u32[]{:S(2)}) collective-permute-start(bf16[64,256]{1,0:T(8,128)(2,1)S(1)} %pad_maximum_fusion.3), channel_id=1, source_target_pairs={{0,96},{32,64},{64,32},{96,0},{1,97},{33,65},{65,33},{97,1},{2,98}... | collective-permute-start | bytes 98312 | tf_op jit(solution)/shard_map/ppermute | solution.py:34
  114.4 6.1 %collective-permute-start.2 = (bf16[128,256]{1,0:T(8,128)(2,1)S(1)}, bf16[128,256]{1,0:T(8,128)(2,1)S(1)}, u32[]{:S(2)}, u32[]{:S(2)}) collective-permute-start(bf16[128,256]{1,0:T(8,128)(2,1)S(1)} %pad_maximum_fusion.2), channel_id=1, source_target_pairs={{0,128},{128,0},{256,384},{384,256},{1,129},{129,1},{257,385},{385... | collective-permute-start | bytes 196616 | tf_op jit(solution)/shard_map/ppermute | solution.py:34
  120.6 8.1 %collective-permute-start.3 = (bf16[256,256]{1,0:T(8,128)(2,1)S(1)}, bf16[256,256]{1,0:T(8,128)(2,1)S(1)}, u32[]{:S(2)}, u32[]{:S(2)}) collective-permute-start(bf16[256,256]{1,0:T(8,128)(2,1)S(1)} %pad_maximum_fusion.1), channel_id=1, source_target_pairs={{0,384},{128,256},{256,128},{384,0},{1,385},{129,257},{257,129},{3... | collective-permute-start | bytes 393224 | tf_op jit(solution)/shard_map/ppermute | solution.py:34
  122.7 9.4 %copy-start.7 = (bf16[2048,128]{1,0:T(8,128)(2,1)S(1)}, bf16[2048,128]{1,0:T(8,128)(2,1)}, u32[]{:S(2)}) copy-start(bf16[2048,128]{1,0:T(8,128)(2,1)} %param.22) | copy-start | bytes 1572868
  128.7 3.4 %collective-permute-start.4 = (bf16[512,256]{1,0:T(8,128)(2,1)S(1)}, bf16[512,256]{1,0:T(8,128)(2,1)S(1)}, u32[]{:S(2)}, u32[]{:S(2)}) collective-permute-start(bf16[512,256]{1,0:T(8,128)(2,1)S(1)} %get-tuple-element.9), channel_id=1, source_target_pairs={{0,16},{16,0},{1,17},{17,1},{2,18},{18,2},{3,19},{19,3},{4,20},{20... | collective-permute-start | bytes 786440 | tf_op jit(solution)/shard_map/ppermute | solution.py:34

commit v3 on v2

--- a/solution.py
+++ b/solution.py
@@ -86,36 +86,26 @@
     return jnp.concatenate([mixed, tail], axis=0).astype(BF16)
 
 
-def first_kernel(blocks_ref, *refs):
-    out_ref = refs[-1]
-    for k, pack_ref in enumerate(refs[:-1]):
-        out_ref[k] = attend_one(blocks_ref, pack_ref[...])
-
-
-def second_kernel(steps, blocks_ref, done_ref, *refs):
+def attend_kernel(blocks_ref, *refs):
     out_ref = refs[-1]
     mine = lax.axis_index("x")
-    for k in range(done_ref.shape[0]):
-        out_ref[mine ^ steps[k]] = done_ref[k]
     for k, pack_ref in enumerate(refs[:-1]):
-        out_ref[mine ^ steps[done_ref.shape[0] + k]] = attend_one(blocks_ref, pack_ref[...])
-
-
-def attend_part(blocks, packs, done=None, steps=None):
-    length = packs[0].shape[1] - HEAD
-    many = len(packs) + (0 if done is None else done.shape[0])
+        out_ref[mine ^ k] = attend_one(blocks_ref, pack_ref[...])
+
+
+def attend_part(blocks, packs):
+    many, length = len(packs), packs[0].shape[1] - HEAD
     keys = blocks.shape[0] * blocks.shape[1]
-    flops = 2 * len(packs) * keys * (blocks.shape[2] * 2 * HEAD + HEAD * length)
-    given = [blocks] if done is None else [blocks, done]
-    return pl.pallas_call(
-        first_kernel if done is None else functools.partial(second_kernel, steps),
+    flops = 2 * many * keys * (blocks.shape[2] * 2 * HEAD + HEAD * length)
+    return pl.pallas_call(
+        attend_kernel,
         out_shape=jax.ShapeDtypeStruct((many, HEAD + TAIL, length), BF16),
-        in_specs=[VMEM] * (len(given) + len(packs)),
+        in_specs=[VMEM] * (1 + many),
         out_specs=VMEM,
         compiler_params=WIDE,
         cost_estimate=cost(flops, 3 * 2**20),
-        name="attend_first" if done is None else "attend_second",
-    )(*given, *packs)
+        name="attend_part",
+    )(blocks, *packs)
 
 
 def pair_kernel(parts_ref, key_ref, value_ref, out_ref):
@@ -240,9 +230,8 @@
     pack_two = partner(pack, "x", 2)
     pack_three = partner(pack, "x", 3)
     pack_one = partner(pack, "x", 1)
-    done = attend_part(blocks, [pack, pack_two])
     outer_block = all_from(global_latents, INNER)
-    parts = attend_part(blocks, [pack_three, pack_one], done, (0, 2, 3, 1))
+    parts = attend_part(blocks, [pack, pack_one, pack_two, pack_three])
     parts = exchange(parts, "x")
 
     pairs = decode_pairs(outer_block, decode_key, decode_value)

time: 161 us -> 164 us (1.019)
  waiting for transfers between devices: 35.9 us -> 46.6 us
  blocking collectives: 55.8 us -> 51.5 us
  Pallas kernels: 11.1 us -> 9.04 us
  other arithmetic: 1.99 us -> 0.24 us
    ppermute x8, waiting for transfers between devices: 23.9 us -> 38.8 us  [partner(): return lax.ppermute(value, axis, pairs)]
    all_to_all x3, blocking collectives: 55.8 us -> 51.5 us  [exchange(): return lax.all_to_all(tiles, axis, split_axis=0, concat_axis=0, tiled=True)]
    all_to_all x3, waiting for transfers between devices: 12 us -> 7.86 us  [exchange(): return lax.all_to_all(tiles, axis, split_axis=0, concat_axis=0, tiled=True)]
    pallas_call x2 -> x1, Pallas kernels: 6.72 us -> 4.69 us  [attend_part(): pl.pallas_call(attend_kernel, out_shape=jax.ShapeDtypeStruct((many, HEAD...]
    concatenate x1, other arithmetic: 1.81 us -> 0.06 us  [step(): pack = jnp.concatenate([folded, value_weight], axis=1)]
  transfers between devices with their start and end apart: 11 -> 11, of which waited for: 10 -> 9; matrix products, arithmetic and copies ran while one was open for 2% -> 0% of each run, Pallas kernels for 3% -> 1%
where the time goes in v3:
time: 164 us; the launch traced here: 163 us
  blocking collectives  51.5 us (31%)
  starting transfers between devices  51 us (31%)
  waiting for transfers between devices  46.6 us (28%)
  Pallas kernels  9.04 us (6%)
  local copies, waits for them, and re-layouts  2.12 us (1%)
    all_to_all x3, blocking collectives, exchange(): return lax.all_to_all(tiles, axis, split_axis=0, concat_axis=0, tiled=True)  51.5 us
    ppermute x8, waiting for transfers between devices, partner(): return lax.ppermute(value, axis, pairs)  38.8 us
    ppermute x8, starting transfers between devices, partner(): return lax.ppermute(value, axis, pairs)  37.1 us
    all_to_all x3, starting transfers between devices, exchange(): return lax.all_to_all(tiles, axis, split_axis=0, concat_axis=0, tiled=True)  13.9 us
    all_to_all x3, waiting for transfers between devices, exchange(): return lax.all_to_all(tiles, axis, split_axis=0, concat_axis=0, tiled=True)  7.86 us
    pallas_call x1, Pallas kernels, attend_part(): pl.pallas_call(attend_kernel, out_shape=jax.ShapeDtypeStruct((many, HEAD...  4.69 us
  transfers between devices with their start and end apart: 11, of which 9 were waited for; matrix products, arithmetic and copies ran while one was open for 0% of the time, Pallas kernels for 1%

profile of v3, /device:TPU:24, one launch (start us, length us, event | category | flops | bytes accessed | tf_op | source)
XLA Modules:
  0.0 163.1 jit_solution(14371402010441955835)
XLA Ops:
  0.7 2.0 %key_copies.1 = bf16[4,128,1024]{2,1,0:T(8,128)(2,1)} custom-call(s32[1,1]{1,0:T(1,128)S(6)} %copy.25.slot_ref, bf16[128,1024]{1,0:T(8,128)(2,1)} %group_ref.1, bf16[16,1024]{1,0:T(8,128)(2,1)} %embed_ref.1), custom_call_target="tpu_custom_call" | custom-call | flops 524288 | bytes 1048576 | tf_op jit(solution)/shard_map/key_copies/pallas_call | solution.py:60
  2.7 6.0 %all-to-all-start.1 = ((bf16[4,128,1024]{2,1,0:T(8,128)(2,1)}), bf16[4,128,1024]{2,1,0:T(8,128)(2,1)}, u32[]{:S(2)}, u32[]{:S(2)}) async-start(bf16[4,128,1024]{2,1,0:T(8,128)(2,1)} %key_copies.1), calls=%async_computation.1 | async-start | bytes 2097152 | tf_op jit(solution)/shard_map/all_to_all | solution.py:38
  8.8 0.5 fusion.1
  9.8 3.4 %collective-permute-start.5 = (bf16[1024,256]{1,0:T(8,128)(2,1)S(1)}, bf16[1024,256]{1,0:T(8,128)(2,1)S(1)}, u32[]{:S(2)}, u32[]{:S(2)}) collective-permute-start(bf16[1024,256]{1,0:T(8,128)(2,1)S(1)} %pad_maximum_fusion.refs_0_), channel_id=1, source_target_pairs={{0,1},{1,0},{2,3},{3,2},{4,5},{5,4},{6,7},{7,6},{8,9},{9,8},{10,11... | collective-permute-start | bytes 1572872 | tf_op jit(solution)/shard_map/ppermute | solution.py:34
  13.2 4.6 %collective-permute-start.6 = (bf16[1024,256]{1,0:T(8,128)(2,1)S(1)}, bf16[1024,256]{1,0:T(8,128)(2,1)S(1)}, u32[]{:S(2)}, u32[]{:S(2)}) collective-permute-start(bf16[1024,256]{1,0:T(8,128)(2,1)S(1)} %pad_maximum_fusion.refs_0_), channel_id=1, source_target_pairs={{0,2},{1,3},{2,0},{3,1},{4,6},{5,7},{6,4},{7,5},{8,10},{9,11},{10,... | collective-permute-start | bytes 1572872 | tf_op jit(solution)/shard_map/ppermute | solution.py:34
  17.8 2.4 %collective-permute-start.7 = (bf16[1024,256]{1,0:T(8,128)(2,1)S(1)}, bf16[1024,256]{1,0:T(8,128)(2,1)}, u32[]{:S(2)}, u32[]{:S(2)}) collective-permute-start(bf16[1024,256]{1,0:T(8,128)(2,1)S(1)} %pad_maximum_fusion.refs_0_), channel_id=1, source_target_pairs={{0,3},{1,2},{2,1},{3,0},{4,7},{5,6},{6,5},{7,4},{8,11},{9,10},{10,... | collective-permute-start | bytes 1572872 | tf_op jit(solution)/shard_map/ppermute | solution.py:34
  20.2 6.2 %collective-permute-done.5.refs_1_ = bf16[1024,256]{1,0:T(8,128)(2,1)S(1)} collective-permute-done((bf16[1024,256]{1,0:T(8,128)(2,1)S(1)}, bf16[1024,256]{1,0:T(8,128)(2,1)S(1)}, u32[]{:S(2)}, u32[]{:S(2)}) %collective-permute-start.5) | collective-permute-done | bytes 524320 | tf_op jit(solution)/shard_map/ppermute | solution.py:34
  26.5 12.1 %collective-permute-done.6.refs_2_ = bf16[1024,256]{1,0:T(8,128)(2,1)S(1)} collective-permute-done((bf16[1024,256]{1,0:T(8,128)(2,1)S(1)}, bf16[1024,256]{1,0:T(8,128)(2,1)S(1)}, u32[]{:S(2)}, u32[]{:S(2)}) %collective-permute-start.6) | collective-permute-done | bytes 524320 | tf_op jit(solution)/shard_map/ppermute | solution.py:34
  38.6 0.8 copy-done.12
  39.4 5.7 %collective-permute-done.7.refs_3_ = bf16[1024,256]{1,0:T(8,128)(2,1)} collective-permute-done((bf16[1024,256]{1,0:T(8,128)(2,1)S(1)}, bf16[1024,256]{1,0:T(8,128)(2,1)}, u32[]{:S(2)}, u32[]{:S(2)}) %collective-permute-start.7) | collective-permute-done | bytes 524320 | tf_op jit(solution)/shard_map/ppermute | solution.py:34
  45.1 4.7 %attend_part.1 = bf16[4,144,128]{2,1,0:T(8,128)(2,1)} custom-call(bf16[4,128,1024]{2,1,0:T(8,128)(2,1)} %all-to-all-done.1.blocks_ref, bf16[1024,256]{1,0:T(8,128)(2,1)} %copy-done.6, bf16[1024,256]{1,0:T(8,128)(2,1)} %copy-done.11, bf16[1024,256]{1,0:T(8,128)(2,1)} %copy-done.12, bf16[1024,256]{1,0:T(8,128)(2,1)} %collective-permute-done.7.refs_3_), custom_call_target="tpu_custom_call" | custom-call | flops 1140850688 | bytes 3145728 | tf_op jit(solution)/shard_map/attend_part/pallas_call | solution.py:100
  49.8 9.4 %all_to_all.30.parts_ref = bf16[4,144,128]{2,1,0:T(8,128)(2,1)S(1)} all-to-all(bf16[4,144,128]{2,1,0:T(8,128)(2,1)} %attend_part.1), channel_id=1, replica_groups=mesh['y'=4,'h'=4,'c'=2,'z'=4,'x'=4] {'x'}, dimensions={0} | all-to-all | bytes 294912 | tf_op jit(solution)/shard_map/all_to_all | solution.py:38
  59.6 17.9 %all_to_all.31.parts_ref = bf16[16,8,2048]{2,1,0:T(8,128)(2,1)S(1)} all-to-all(bf16[16,8,2048]{2,1,0:T(8,128)(2,1)S(1)} %bitcast.16), channel_id=1, replica_groups=mesh['y'=4,'h'=4,'c'=2,'z'=4,'x'=4] {'z','x'}, dimensions={0} | all-to-all | bytes 1048576 | tf_op jit(solution)/shard_map/all_to_all | solution.py:38
  77.5 0.7 broadcast_in_dim.2
  78.2 4.2 %all-to-all-start = ((bf16[16,2,2048]{2,1,0:T(2,128)(2,1)}), bf16[16,2,2048]{2,1,0:T(2,128)(2,1)S(1)}, u32[]{:S(2)}, u32[]{:S(2)}) async-start(bf16[16,2,2048]{2,1,0:T(2,128)(2,1)} %broadcast_in_dim.2), calls=%async_computation | async-start | bytes 262144 | tf_op jit(solution)/shard_map/all_to_all | solution.py:38
  82.5 1.0 sum_and_norm.1
  83.5 7.9 %all-to-all-done.parts_ref = bf16[16,2,2048]{2,1,0:T(2,128)(2,1)S(1)} async-done(((bf16[16,2,2048]{2,1,0:T(2,128)(2,1)}), bf16[16,2,2048]{2,1,0:T(2,128)(2,1)S(1)}, u32[]{:S(2)}, u32[]{:S(2)}) %all-to-all-start) | async-done | bytes 131104 | tf_op jit(solution)/shard_map/all_to_all | solution.py:38
  91.4 3.7 %all-to-all-start.4 = ((bf16[16,8,2048]{2,1,0:T(8,128)(2,1)}), bf16[16,8,2048]{2,1,0:T(8,128)(2,1)S(1)}, u32[]{:S(2)}, u32[]{:S(2)}) async-start(bf16[16,8,2048]{2,1,0:T(8,128)(2,1)} %get-tuple-element.7), calls=%async_computation.4 | async-start | bytes 1048576 | tf_op jit(solution)/shard_map/all_to_all | solution.py:38
  95.4 9.1 %collective-permute-start = (bf16[32,256]{1,0:T(8,128)(2,1)S(1)}, bf16[32,256]{1,0:T(8,128)(2,1)S(1)}, u32[]{:S(2)}, u32[]{:S(2)}) collective-permute-start(bf16[32,256]{1,0:T(8,128)(2,1)S(1)} %decode_pairs.1), channel_id=1, source_target_pairs={{0,32},{32,0},{64,96},{96,64},{1,33},{33,1},{65,97},{97,65},{2,34}... | collective-permute-start | bytes 49160 | tf_op jit(solution)/shard_map/ppermute | solution.py:34
  104.5 1.8 %collective-permute-done = bf16[32,256]{1,0:T(8,128)(2,1)S(1)} collective-permute-done((bf16[32,256]{1,0:T(8,128)(2,1)S(1)}, bf16[32,256]{1,0:T(8,128)(2,1)S(1)}, u32[]{:S(2)}, u32[]{:S(2)}) %collective-permute-start) | collective-permute-done | bytes 16416 | tf_op jit(solution)/shard_map/ppermute | solution.py:34
  106.3 10.9 %collective-permute-start.1 = (bf16[64,256]{1,0:T(8,128)(2,1)S(1)}, bf16[64,256]{1,0:T(8,128)(2,1)S(1)}, u32[]{:S(2)}, u32[]{:S(2)}) collective-permute-start(bf16[64,256]{1,0:T(8,128)(2,1)S(1)} %pad_maximum_fusion.3), channel_id=1, source_target_pairs={{0,96},{32,64},{64,32},{96,0},{1,97},{33,65},{65,33},{97,1},{2,98}... | collective-permute-start | bytes 98312 | tf_op jit(solution)/shard_map/ppermute | solution.py:34
  117.2 2.0 %collective-permute-done.1 = bf16[64,256]{1,0:T(8,128)(2,1)S(1)} collective-permute-done((bf16[64,256]{1,0:T(8,128)(2,1)S(1)}, bf16[64,256]{1,0:T(8,128)(2,1)S(1)}, u32[]{:S(2)}, u32[]{:S(2)}) %collective-permute-start.1) | collective-permute-done | bytes 32800 | tf_op jit(solution)/shard_map/ppermute | solution.py:34
  119.2 2.6 %collective-permute-start.2 = (bf16[128,256]{1,0:T(8,128)(2,1)S(1)}, bf16[128,256]{1,0:T(8,128)(2,1)S(1)}, u32[]{:S(2)}, u32[]{:S(2)}) collective-permute-start(bf16[128,256]{1,0:T(8,128)(2,1)S(1)} %pad_maximum_fusion.2), channel_id=1, source_target_pairs={{0,128},{128,0},{256,384},{384,256},{1,129},{129,1},{257,385},{385... | collective-permute-start | bytes 196616 | tf_op jit(solution)/shard_map/ppermute | solution.py:34
  121.8 3.5 %collective-permute-done.2 = bf16[128,256]{1,0:T(8,128)(2,1)S(1)} collective-permute-done((bf16[128,256]{1,0:T(8,128)(2,1)S(1)}, bf16[128,256]{1,0:T(8,128)(2,1)S(1)}, u32[]{:S(2)}, u32[]{:S(2)}) %collective-permute-start.2) | collective-permute-done | bytes 65568 | tf_op jit(solution)/shard_map/ppermute | solution.py:34
  125.3 2.1 %collective-permute-start.3 = (bf16[256,256]{1,0:T(8,128)(2,1)S(1)}, bf16[256,256]{1,0:T(8,128)(2,1)S(1)}, u32[]{:S(2)}, u32[]{:S(2)}) collective-permute-start(bf16[256,256]{1,0:T(8,128)(2,1)S(1)} %pad_maximum_fusion.1), channel_id=1, source_target_pairs={{0,384},{128,256},{256,128},{384,0},{1,385},{129,257},{257,129},{3... | collective-permute-start | bytes 393224 | tf_op jit(solution)/shard_map/ppermute | solution.py:34
  127.5 5.9 %collective-permute-done.3 = bf16[256,256]{1,0:T(8,128)(2,1)S(1)} collective-permute-done((bf16[256,256]{1,0:T(8,128)(2,1)S(1)}, bf16[256,256]{1,0:T(8,128)(2,1)S(1)}, u32[]{:S(2)}, u32[]{:S(2)}) %collective-permute-start.3) | collective-permute-done | bytes 131104 | tf_op jit(solution)/shard_map/ppermute | solution.py:34
  133.4 1.9 %collective-permute-start.4 = (bf16[512,256]{1,0:T(8,128)(2,1)S(1)}, bf16[512,256]{1,0:T(8,128)(2,1)S(1)}, u32[]{:S(2)}, u32[]{:S(2)}) collective-permute-start(bf16[512,256]{1,0:T(8,128)(2,1)S(1)} %get-tuple-element.9), channel_id=1, source_target_pairs={{0,16},{16,0},{1,17},{17,1},{2,18},{18,2},{3,19},{19,3},{4,20},{20... | collective-permute-start | bytes 786440 | tf_op jit(solution)/shard_map/ppermute | solution.py:34
  135.4 1.5 collective-permute-done.4
  136.9 0.6 fusion.15
  137.6 0.6 fusion
  138.2 24.2 %all_to_all.32.parts_ref = bf16[16,8,2048]{2,1,0:T(8,128)(2,1)S(1)} all-to-all(bf16[16,8,2048]{2,1,0:T(8,128)(2,1)S(1)} %fusion), channel_id=1, replica_groups=mesh['y'=4,'h'=4,'c'=2,'z'=4,'x'=4] {'z','x'}, dimensions={0} | all-to-all | bytes 1048576 | tf_op jit(solution)/shard_map/all_to_all | solution.py:38
  162.4 0.7 last_sum.1
  (41 shorter events, 1.5 us)
Async XLA Ops:
  0.0 137.6 %copy-start = (bf16[128,2048]{1,0:T(8,128)(2,1)S(1)}, bf16[128,2048]{1,0:T(8,128)(2,1)}, u32[]{:S(2)}) copy-start(bf16[128,2048]{1,0:T(8,128)(2,1)} %param.25) | copy-start | bytes 1572868
  2.7 6.0 %copy-start.4 = (bf16[128,2048]{1,0:T(8,128)(2,1)S(1)}, bf16[128,2048]{1,0:T(8,128)(2,1)}, u32[]{:S(2)}) copy-start(bf16[128,2048]{1,0:T(8,128)(2,1)} %param.16) | copy-start | bytes 1572868
  2.7 6.0 %copy-start.5 = (bf16[2048,128]{1,0:T(8,128)(2,1)S(1)}, bf16[2048,128]{1,0:T(8,128)(2,1)}, u32[]{:S(2)}) copy-start(bf16[2048,128]{1,0:T(8,128)(2,1)} %param.17) | copy-start | bytes 1572868
  2.7 6.0 %copy-start.8 = (bf16[1024,128]{1,0:T(8,128)(2,1)S(1)}, bf16[1024,128]{1,0:T(8,128)(2,1)}, u32[]{:S(2)}) copy-start(bf16[1024,128]{1,0:T(8,128)(2,1)} %param.18) | copy-start | bytes 786436
  2.7 42.4 %all-to-all-start.1 = ((bf16[4,128,1024]{2,1,0:T(8,128)(2,1)}), bf16[4,128,1024]{2,1,0:T(8,128)(2,1)}, u32[]{:S(2)}, u32[]{:S(2)}) async-start(bf16[4,128,1024]{2,1,0:T(8,128)(2,1)} %key_copies.1), calls=%async_computation.1 | async-start | bytes 2097152 | tf_op jit(solution)/shard_map/all_to_all | solution.py:38
  8.8 1.0 copy-start.9
  9.8 35.3 %copy-start.6 = (bf16[1024,256]{1,0:T(8,128)(2,1)}, bf16[1024,256]{1,0:T(8,128)(2,1)S(1)}, u32[]{:S(2)}) copy-start(bf16[1024,256]{1,0:T(8,128)(2,1)S(1)} %pad_maximum_fusion.refs_0_) | copy-start | bytes 1572868
  9.8 16.7 %collective-permute-start.5 = (bf16[1024,256]{1,0:T(8,128)(2,1)S(1)}, bf16[1024,256]{1,0:T(8,128)(2,1)S(1)}, u32[]{:S(2)}, u32[]{:S(2)}) collective-permute-start(bf16[1024,256]{1,0:T(8,128)(2,1)S(1)} %pad_maximum_fusion.refs_0_), channel_id=1, source_target_pairs={{0,1},{1,0},{2,3},{3,2},{4,5},{5,4},{6,7},{7,6},{8,9},{9,8},{10,11... | collective-permute-start | bytes 1572872 | tf_op jit(solution)/shard_map/ppermute | solution.py:34
  13.2 25.4 %collective-permute-start.6 = (bf16[1024,256]{1,0:T(8,128)(2,1)S(1)}, bf16[1024,256]{1,0:T(8,128)(2,1)S(1)}, u32[]{:S(2)}, u32[]{:S(2)}) collective-permute-start(bf16[1024,256]{1,0:T(8,128)(2,1)S(1)} %pad_maximum_fusion.refs_0_), channel_id=1, source_target_pairs={{0,2},{1,3},{2,0},{3,1},{4,6},{5,7},{6,4},{7,5},{8,10},{9,11},{10,... | collective-permute-start | bytes 1572872 | tf_op jit(solution)/shard_map/ppermute | solution.py:34
  17.8 27.3 %collective-permute-start.7 = (bf16[1024,256]{1,0:T(8,128)(2,1)S(1)}, bf16[1024,256]{1,0:T(8,128)(2,1)}, u32[]{:S(2)}, u32[]{:S(2)}) collective-permute-start(bf16[1024,256]{1,0:T(8,128)(2,1)S(1)} %pad_maximum_fusion.refs_0_), channel_id=1, source_target_pairs={{0,3},{1,2},{2,1},{3,0},{4,7},{5,6},{6,5},{7,4},{8,11},{9,10},{10,... | collective-permute-start | bytes 1572872 | tf_op jit(solution)/shard_map/ppermute | solution.py:34
  26.5 18.6 %copy-start.11 = (bf16[1024,256]{1,0:T(8,128)(2,1)}, bf16[1024,256]{1,0:T(8,128)(2,1)S(1)}, u32[]{:S(2)}) copy-start(bf16[1024,256]{1,0:T(8,128)(2,1)S(1)} %collective-permute-done.5.refs_1_) | copy-start | bytes 1572868
  38.6 0.8 copy-start.12
  45.1 14.1 %copy-start.1 = (bf16[128,2048]{1,0:T(8,128)(2,1)S(1)}, bf16[128,2048]{1,0:T(8,128)(2,1)}, u32[]{:S(2)}) copy-start(bf16[128,2048]{1,0:T(8,128)(2,1)} %weight_ref.1) | copy-start | bytes 1572868
  59.5 17.9 %copy-start.10 = (bf16[2,2048]{1,0:T(2,128)(2,1)S(1)}, bf16[2,2048]{1,0:T(2,128)(2,1)}, u32[]{:S(2)}) copy-start(bf16[2,2048]{1,0:T(2,128)(2,1)} %param.21) | copy-start | bytes 24580
  78.2 13.2 %all-to-all-start = ((bf16[16,2,2048]{2,1,0:T(2,128)(2,1)}), bf16[16,2,2048]{2,1,0:T(2,128)(2,1)S(1)}, u32[]{:S(2)}, u32[]{:S(2)}) async-start(bf16[16,2,2048]{2,1,0:T(2,128)(2,1)} %broadcast_in_dim.2), calls=%async_computation | async-start | bytes 262144 | tf_op jit(solution)/shard_map/all_to_all | solution.py:38
  91.4 3.7 %copy-start.2 = (bf16[2048,128]{1,0:T(8,128)(2,1)S(1)}, bf16[2048,128]{1,0:T(8,128)(2,1)}, u32[]{:S(2)}) copy-start(bf16[2048,128]{1,0:T(8,128)(2,1)} %key_ref.1) | copy-start | bytes 1572868
  91.4 3.7 %copy-start.3 = (bf16[2048,128]{1,0:T(8,128)(2,1)S(1)}, bf16[2048,128]{1,0:T(8,128)(2,1)}, u32[]{:S(2)}) copy-start(bf16[2048,128]{1,0:T(8,128)(2,1)} %value_ref.1) | copy-start | bytes 1572868
  91.4 45.5 %all-to-all-start.4 = ((bf16[16,8,2048]{2,1,0:T(8,128)(2,1)}), bf16[16,8,2048]{2,1,0:T(8,128)(2,1)S(1)}, u32[]{:S(2)}, u32[]{:S(2)}) async-start(bf16[16,8,2048]{2,1,0:T(8,128)(2,1)} %get-tuple-element.7), calls=%async_computation.4 | async-start | bytes 1048576 | tf_op jit(solution)/shard_map/all_to_all | solution.py:38
  95.4 10.9 %collective-permute-start = (bf16[32,256]{1,0:T(8,128)(2,1)S(1)}, bf16[32,256]{1,0:T(8,128)(2,1)S(1)}, u32[]{:S(2)}, u32[]{:S(2)}) collective-permute-start(bf16[32,256]{1,0:T(8,128)(2,1)S(1)} %decode_pairs.1), channel_id=1, source_target_pairs={{0,32},{32,0},{64,96},{96,64},{1,33},{33,1},{65,97},{97,65},{2,34}... | collective-permute-start | bytes 49160 | tf_op jit(solution)/shard_map/ppermute | solution.py:34
  106.3 12.9 %collective-permute-start.1 = (bf16[64,256]{1,0:T(8,128)(2,1)S(1)}, bf16[64,256]{1,0:T(8,128)(2,1)S(1)}, u32[]{:S(2)}, u32[]{:S(2)}) collective-permute-start(bf16[64,256]{1,0:T(8,128)(2,1)S(1)} %pad_maximum_fusion.3), channel_id=1, source_target_pairs={{0,96},{32,64},{64,32},{96,0},{1,97},{33,65},{65,33},{97,1},{2,98}... | collective-permute-start | bytes 98312 | tf_op jit(solution)/shard_map/ppermute | solution.py:34
  119.2 6.1 %collective-permute-start.2 = (bf16[128,256]{1,0:T(8,128)(2,1)S(1)}, bf16[128,256]{1,0:T(8,128)(2,1)S(1)}, u32[]{:S(2)}, u32[]{:S(2)}) collective-permute-start(bf16[128,256]{1,0:T(8,128)(2,1)S(1)} %pad_maximum_fusion.2), channel_id=1, source_target_pairs={{0,128},{128,0},{256,384},{384,256},{1,129},{129,1},{257,385},{385... | collective-permute-start | bytes 196616 | tf_op jit(solution)/shard_map/ppermute | solution.py:34
  125.3 8.1 %collective-permute-start.3 = (bf16[256,256]{1,0:T(8,128)(2,1)S(1)}, bf16[256,256]{1,0:T(8,128)(2,1)S(1)}, u32[]{:S(2)}, u32[]{:S(2)}) collective-permute-start(bf16[256,256]{1,0:T(8,128)(2,1)S(1)} %pad_maximum_fusion.1), channel_id=1, source_target_pairs={{0,384},{128,256},{256,128},{384,0},{1,385},{129,257},{257,129},{3... | collective-permute-start | bytes 393224 | tf_op jit(solution)/shard_map/ppermute | solution.py:34
  127.5 9.4 %copy-start.7 = (bf16[2048,128]{1,0:T(8,128)(2,1)S(1)}, bf16[2048,128]{1,0:T(8,128)(2,1)}, u32[]{:S(2)}) copy-start(bf16[2048,128]{1,0:T(8,128)(2,1)} %param.22) | copy-start | bytes 1572868
  133.4 3.4 %collective-permute-start.4 = (bf16[512,256]{1,0:T(8,128)(2,1)S(1)}, bf16[512,256]{1,0:T(8,128)(2,1)S(1)}, u32[]{:S(2)}, u32[]{:S(2)}) collective-permute-start(bf16[512,256]{1,0:T(8,128)(2,1)S(1)} %get-tuple-element.9), channel_id=1, source_target_pairs={{0,16},{16,0},{1,17},{17,1},{2,18},{18,2},{3,19},{19,3},{4,20},{20... | collective-permute-start | bytes 786440 | tf_op jit(solution)/shard_map/ppermute | solution.py:34

commit v4 on v3

--- a/solution.py
+++ b/solution.py
@@ -51,20 +51,18 @@
     lines = lax.broadcasted_iota(jnp.int32, embed_ref.shape, 0)
     chosen = jnp.where(lines == slot_ref[0, 0], embed_ref[...].astype(F32), 0.0)
     keyed = group_ref[...].astype(F32) + jnp.sum(chosen, axis=0, keepdims=True)
-    block = keyed.astype(BF16)
-    for j in range(out_ref.shape[0]):
-        out_ref[j] = block
-
-
-def key_copies(slot_ids, group_latents, slot_embed, many):
+    out_ref[...] = keyed.astype(BF16)
+
+
+def key_rows(slot_ids, group_latents, slot_embed):
     return pl.pallas_call(
         key_kernel,
-        out_shape=jax.ShapeDtypeStruct((many, *group_latents.shape), BF16),
+        out_shape=jax.ShapeDtypeStruct(group_latents.shape, BF16),
         in_specs=[pl.BlockSpec(memory_space=pltpu.SMEM), VMEM, VMEM],
         out_specs=VMEM,
         compiler_params=WIDE,
         cost_estimate=cost(4 * group_latents.size, 2**20),
-        name="key_copies",
+        name="key_rows",
     )(slot_ids, group_latents, slot_embed)
 
 
@@ -86,26 +84,40 @@
     return jnp.concatenate([mixed, tail], axis=0).astype(BF16)
 
 
-def attend_kernel(blocks_ref, *refs):
-    out_ref = refs[-1]
+def attend_kernel(count, *refs):
+    given, (out_ref, blocks_ref, packs_ref, sems) = refs[:-4], refs[-4:]
+    copies = []
+    for k, ref in enumerate(given):
+        target = blocks_ref.at[k] if k < count else packs_ref.at[k - count]
+        copies.append(pltpu.make_async_copy(ref, target, sems.at[k]))
+        copies[-1].start()
+    for copy in copies[:count]:
+        copy.wait()
     mine = lax.axis_index("x")
-    for k, pack_ref in enumerate(refs[:-1]):
-        out_ref[mine ^ k] = attend_one(blocks_ref, pack_ref[...])
+    for k, copy in enumerate(copies[count:]):
+        copy.wait()
+        out_ref[mine ^ k] = attend_one(blocks_ref, packs_ref[k])
 
 
 def attend_part(blocks, packs):
     many, length = len(packs), packs[0].shape[1] - HEAD
-    keys = blocks.shape[0] * blocks.shape[1]
-    flops = 2 * many * keys * (blocks.shape[2] * 2 * HEAD + HEAD * length)
-    return pl.pallas_call(
-        attend_kernel,
+    count = len(blocks)
+    keys = count * blocks[0].shape[0]
+    flops = 2 * many * keys * (blocks[0].shape[1] * 2 * HEAD + HEAD * length)
+    return pl.pallas_call(
+        functools.partial(attend_kernel, count),
         out_shape=jax.ShapeDtypeStruct((many, HEAD + TAIL, length), BF16),
-        in_specs=[VMEM] * (1 + many),
-        out_specs=VMEM,
+        in_specs=[pl.BlockSpec(memory_space=pl.ANY)] * (count + many),
+        out_specs=VMEM,
+        scratch_shapes=[
+            pltpu.VMEM((count, *blocks[0].shape), BF16),
+            pltpu.VMEM((many, *packs[0].shape), BF16),
+            pltpu.SemaphoreType.DMA((count + many,)),
+        ],
         compiler_params=WIDE,
         cost_estimate=cost(flops, 3 * 2**20),
         name="attend_part",
-    )(blocks, *packs)
+    )(*blocks, *packs)
 
 
 def pair_kernel(parts_ref, key_ref, value_ref, out_ref):
@@ -225,13 +237,18 @@
     pack = jnp.concatenate([folded, value_weight], axis=1)
     own_rows = lax.dynamic_slice_in_dim(merge_latents, lax.axis_index(INNER) * rows, rows, 0)
 
-    copies = key_copies(slot_ids, group_latents, slot_embed, lax.axis_size("z"))
-    blocks = exchange(copies, "z")
+    keyed = key_rows(slot_ids, group_latents, slot_embed)
     pack_two = partner(pack, "x", 2)
+    keyed_three = partner(keyed, "z", 3)
+    outer_block = all_from(global_latents, INNER)
     pack_three = partner(pack, "x", 3)
+    keyed_two = partner(keyed, "z", 2)
     pack_one = partner(pack, "x", 1)
-    outer_block = all_from(global_latents, INNER)
-    parts = attend_part(blocks, [pack, pack_one, pack_two, pack_three])
+    keyed_one = partner(keyed, "z", 1)
+    parts = attend_part(
+        [keyed, keyed_one, keyed_two, keyed_three],
+        [pack, pack_one, pack_two, pack_three],
+    )
     parts = exchange(parts, "x")
 
     pairs = decode_pairs(outer_block, decode_key, decode_value)

time: 164 us -> 167 us (1.018)
  waiting for transfers between devices: 46.6 us -> 38.3 us
  starting transfers between devices: 51 us -> 56 us
  blocking collectives: 51.5 us -> 56 us
    ppermute x8 -> x11, starting transfers between devices: 37.1 us -> 47.8 us  [partner(): return lax.ppermute(value, axis, pairs)]
    ppermute x8 -> x11, waiting for transfers between devices: 38.8 us -> 30.5 us  [partner(): return lax.ppermute(value, axis, pairs)]
    all_to_all x3 -> x2, starting transfers between devices: 13.9 us -> 8.15 us  [exchange(): return lax.all_to_all(tiles, axis, split_axis=0, concat_axis=0, tiled=True)]
    all_to_all x3, blocking collectives: 51.5 us -> 56 us  [exchange(): return lax.all_to_all(tiles, axis, split_axis=0, concat_axis=0, tiled=True)]
    all_to_all x3 -> x2, waiting for transfers between devices: 7.86 us -> 7.86 us  [exchange(): return lax.all_to_all(tiles, axis, split_axis=0, concat_axis=0, tiled=True)]
  transfers between devices with their start and end apart: 11 -> 13, of which waited for: 9 -> 8; matrix products, arithmetic and copies ran while one was open for 0% -> 1% of each run, Pallas kernels for 1% -> 1%
where the time goes in v4:
time: 167 us; the launch traced here: 166 us
  starting transfers between devices  56 us (34%)
  blocking collectives  56 us (34%)
  waiting for transfers between devices  38.3 us (23%)
  Pallas kernels  8.91 us (5%)
  matrix products  2.74 us (2%)
  local copies, waits for them, and re-layouts  2.59 us (2%)
    all_to_all x3, blocking collectives, exchange(): return lax.all_to_all(tiles, axis, split_axis=0, concat_axis=0, tiled=True)  56 us
    ppermute x11, starting transfers between devices, partner(): return lax.ppermute(value, axis, pairs)  47.8 us
    ppermute x11, waiting for transfers between devices, partner(): return lax.ppermute(value, axis, pairs)  30.5 us
    all_to_all x2, starting transfers between devices, exchange(): return lax.all_to_all(tiles, axis, split_axis=0, concat_axis=0, tiled=True)  8.15 us
    all_to_all x2, waiting for transfers between devices, exchange(): return lax.all_to_all(tiles, axis, split_axis=0, concat_axis=0, tiled=True)  7.86 us
    pallas_call x1, Pallas kernels, attend_part(): pl.pallas_call(functools.partial(attend_kernel, count), out_shape=jax.Sha...  4.84 us
  transfers between devices with their start and end apart: 13, of which 8 were waited for; matrix products, arithmetic and copies ran while one was open for 1% of the time, Pallas kernels for 1%

profile of v4, /device:TPU:24, one launch (start us, length us, event | category | flops | bytes accessed | tf_op | source)
XLA Modules:
  0.0 165.8 jit_solution(15387786243524746110)
XLA Ops:
  0.7 1.7 %key_rows.1.refs_0_ = bf16[128,1024]{1,0:T(8,128)(2,1)} custom-call(s32[1,1]{1,0:T(1,128)S(6)} %copy.25.slot_ref, bf16[128,1024]{1,0:T(8,128)(2,1)} %group_ref.1, bf16[16,1024]{1,0:T(8,128)(2,1)} %embed_ref.1), custom_call_target="tpu_custom_call" | custom-call | flops 524288 | bytes 1048576 | tf_op jit(solution)/shard_map/key_rows/pallas_call | solution.py:58
  2.5 3.9 %collective-permute-start.5 = (bf16[128,1024]{1,0:T(8,128)(2,1)}, bf16[128,1024]{1,0:T(8,128)(2,1)S(1)}, u32[]{:S(2)}, u32[]{:S(2)}) collective-permute-start(bf16[128,1024]{1,0:T(8,128)(2,1)} %key_rows.1.refs_0_), channel_id=1, source_target_pairs={{0,4},{4,0},{8,12},{12,8},{1,5},{5,1},{9,13},{13,9},{2,6},{6,2},{1... | collective-permute-start | bytes 786440 | tf_op jit(solution)/shard_map/ppermute | solution.py:34
  6.4 1.6 fusion.1
  8.1 3.4 %collective-permute-start.8 = (bf16[1024,256]{1,0:T(8,128)(2,1)S(1)}, bf16[1024,256]{1,0:T(8,128)(2,1)S(1)}, u32[]{:S(2)}, u32[]{:S(2)}) collective-permute-start(bf16[1024,256]{1,0:T(8,128)(2,1)S(1)} %pad_maximum_fusion.refs_4_), channel_id=1, source_target_pairs={{0,1},{1,0},{2,3},{3,2},{4,5},{5,4},{6,7},{7,6},{8,9},{9,8},{10,11... | collective-permute-start | bytes 1572872 | tf_op jit(solution)/shard_map/ppermute | solution.py:34
  11.5 4.6 %collective-permute-start.9 = (bf16[1024,256]{1,0:T(8,128)(2,1)S(1)}, bf16[1024,256]{1,0:T(8,128)(2,1)S(1)}, u32[]{:S(2)}, u32[]{:S(2)}) collective-permute-start(bf16[1024,256]{1,0:T(8,128)(2,1)S(1)} %pad_maximum_fusion.refs_4_), channel_id=1, source_target_pairs={{0,2},{1,3},{2,0},{3,1},{4,6},{5,7},{6,4},{7,5},{8,10},{9,11},{10,... | collective-permute-start | bytes 1572872 | tf_op jit(solution)/shard_map/ppermute | solution.py:34
  16.2 2.4 %collective-permute-start.10 = (bf16[1024,256]{1,0:T(8,128)(2,1)S(1)}, bf16[1024,256]{1,0:T(8,128)(2,1)}, u32[]{:S(2)}, u32[]{:S(2)}) collective-permute-start(bf16[1024,256]{1,0:T(8,128)(2,1)S(1)} %pad_maximum_fusion.refs_4_), channel_id=1, source_target_pairs={{0,3},{1,2},{2,1},{3,0},{4,7},{5,6},{6,5},{7,4},{8,11},{9,10},{10,... | collective-permute-start | bytes 1572872 | tf_op jit(solution)/shard_map/ppermute | solution.py:34
  18.6 5.2 %collective-permute-start.6 = (bf16[128,1024]{1,0:T(8,128)(2,1)S(1)}, bf16[128,1024]{1,0:T(8,128)(2,1)S(1)}, u32[]{:S(2)}, u32[]{:S(2)}) collective-permute-start(bf16[128,1024]{1,0:T(8,128)(2,1)S(1)} %copy-done.7), channel_id=1, source_target_pairs={{0,8},{4,12},{8,0},{12,4},{1,9},{5,13},{9,1},{13,5},{2,10},{6,14},... | collective-permute-start | bytes 786440 | tf_op jit(solution)/shard_map/ppermute | solution.py:34
  23.8 1.9 %collective-permute-start.7 = (bf16[128,1024]{1,0:T(8,128)(2,1)S(1)}, bf16[128,1024]{1,0:T(8,128)(2,1)S(1)}, u32[]{:S(2)}, u32[]{:S(2)}) collective-permute-start(bf16[128,1024]{1,0:T(8,128)(2,1)S(1)} %copy-done.7), channel_id=1, source_target_pairs={{0,12},{4,8},{8,4},{12,0},{1,13},{5,9},{9,5},{13,1},{2,14},{6,10},... | collective-permute-start | bytes 786440 | tf_op jit(solution)/shard_map/ppermute | solution.py:34
  25.7 14.3 %collective-permute-done.6.refs_2_ = bf16[128,1024]{1,0:T(8,128)(2,1)S(1)} collective-permute-done((bf16[128,1024]{1,0:T(8,128)(2,1)S(1)}, bf16[128,1024]{1,0:T(8,128)(2,1)S(1)}, u32[]{:S(2)}, u32[]{:S(2)}) %collective-permute-start.6) | collective-permute-done | bytes 262176 | tf_op jit(solution)/shard_map/ppermute | solution.py:34
  40.0 0.7 copy-done.13
  41.0 0.8 copy-done.11
  41.8 1.7 %collective-permute-done.10.refs_7_ = bf16[1024,256]{1,0:T(8,128)(2,1)} collective-permute-done((bf16[1024,256]{1,0:T(8,128)(2,1)S(1)}, bf16[1024,256]{1,0:T(8,128)(2,1)}, u32[]{:S(2)}, u32[]{:S(2)}) %collective-permute-start.10) | collective-permute-done | bytes 524320 | tf_op jit(solution)/shard_map/ppermute | solution.py:34
  43.4 4.8 %attend_part.1 = bf16[4,144,128]{2,1,0:T(8,128)(2,1)} custom-call(bf16[128,1024]{1,0:T(8,128)(2,1)} %key_rows.1.refs_0_, bf16[128,1024]{1,0:T(8,128)(2,1)} %copy-done.12, bf16[128,1024]{1,0:T(8,128)(2,1)} %copy-done.13, bf16[128,1024]{1,0:T(8,128)(2,1)} %copy-done.14, bf16[1024,256]{1,0:T(8,128)(2,1)} %copy-done.5, bf16[1024,256]{1,0:T(8,128)(2,1)} %copy-done.10, ...), custom_call_target="tpu_custom_call" | custom-call | flops 1140850688 | bytes 3145728 | tf_op jit(solution)/shard_map/attend_part/pallas_call | solution.py:107
  48.3 9.4 %all_to_all.25.parts_ref = bf16[4,144,128]{2,1,0:T(8,128)(2,1)S(1)} all-to-all(bf16[4,144,128]{2,1,0:T(8,128)(2,1)} %attend_part.1), channel_id=1, replica_groups=mesh['y'=4,'h'=4,'c'=2,'z'=4,'x'=4] {'x'}, dimensions={0} | all-to-all | bytes 294912 | tf_op jit(solution)/shard_map/all_to_all | solution.py:38
  58.0 21.4 %all_to_all.26.parts_ref = bf16[16,8,2048]{2,1,0:T(8,128)(2,1)S(1)} all-to-all(bf16[16,8,2048]{2,1,0:T(8,128)(2,1)S(1)} %bitcast.16), channel_id=1, replica_groups=mesh['y'=4,'h'=4,'c'=2,'z'=4,'x'=4] {'z','x'}, dimensions={0} | all-to-all | bytes 1048576 | tf_op jit(solution)/shard_map/all_to_all | solution.py:38
  79.4 0.7 broadcast_in_dim.2
  80.1 4.4 %all-to-all-start = ((bf16[16,2,2048]{2,1,0:T(2,128)(2,1)}), bf16[16,2,2048]{2,1,0:T(2,128)(2,1)S(1)}, u32[]{:S(2)}, u32[]{:S(2)}) async-start(bf16[16,2,2048]{2,1,0:T(2,128)(2,1)} %broadcast_in_dim.2), calls=%async_computation | async-start | bytes 262144 | tf_op jit(solution)/shard_map/all_to_all | solution.py:38
  84.6 1.0 sum_and_norm.1
  85.6 7.9 %all-to-all-done.parts_ref = bf16[16,2,2048]{2,1,0:T(2,128)(2,1)S(1)} async-done(((bf16[16,2,2048]{2,1,0:T(2,128)(2,1)}), bf16[16,2,2048]{2,1,0:T(2,128)(2,1)S(1)}, u32[]{:S(2)}, u32[]{:S(2)}) %all-to-all-start) | async-done | bytes 131104 | tf_op jit(solution)/shard_map/all_to_all | solution.py:38
  93.5 3.7 %all-to-all-start.3 = ((bf16[16,8,2048]{2,1,0:T(8,128)(2,1)}), bf16[16,8,2048]{2,1,0:T(8,128)(2,1)S(1)}, u32[]{:S(2)}, u32[]{:S(2)}) async-start(bf16[16,8,2048]{2,1,0:T(8,128)(2,1)} %get-tuple-element.7), calls=%async_computation.3 | async-start | bytes 1048576 | tf_op jit(solution)/shard_map/all_to_all | solution.py:38
  97.5 9.1 %collective-permute-start = (bf16[32,256]{1,0:T(8,128)(2,1)S(1)}, bf16[32,256]{1,0:T(8,128)(2,1)S(1)}, u32[]{:S(2)}, u32[]{:S(2)}) collective-permute-start(bf16[32,256]{1,0:T(8,128)(2,1)S(1)} %decode_pairs.1), channel_id=1, source_target_pairs={{0,32},{32,0},{64,96},{96,64},{1,33},{33,1},{65,97},{97,65},{2,34}... | collective-permute-start | bytes 49160 | tf_op jit(solution)/shard_map/ppermute | solution.py:34
  106.6 1.8 %collective-permute-done = bf16[32,256]{1,0:T(8,128)(2,1)S(1)} collective-permute-done((bf16[32,256]{1,0:T(8,128)(2,1)S(1)}, bf16[32,256]{1,0:T(8,128)(2,1)S(1)}, u32[]{:S(2)}, u32[]{:S(2)}) %collective-permute-start) | collective-permute-done | bytes 16416 | tf_op jit(solution)/shard_map/ppermute | solution.py:34
  108.4 10.6 %collective-permute-start.1 = (bf16[64,256]{1,0:T(8,128)(2,1)S(1)}, bf16[64,256]{1,0:T(8,128)(2,1)S(1)}, u32[]{:S(2)}, u32[]{:S(2)}) collective-permute-start(bf16[64,256]{1,0:T(8,128)(2,1)S(1)} %pad_maximum_fusion.3), channel_id=1, source_target_pairs={{0,96},{32,64},{64,32},{96,0},{1,97},{33,65},{65,33},{97,1},{2,98}... | collective-permute-start | bytes 98312 | tf_op jit(solution)/shard_map/ppermute | solution.py:34
  119.0 1.9 %collective-permute-done.1 = bf16[64,256]{1,0:T(8,128)(2,1)S(1)} collective-permute-done((bf16[64,256]{1,0:T(8,128)(2,1)S(1)}, bf16[64,256]{1,0:T(8,128)(2,1)S(1)}, u32[]{:S(2)}, u32[]{:S(2)}) %collective-permute-start.1) | collective-permute-done | bytes 32800 | tf_op jit(solution)/shard_map/ppermute | solution.py:34
  120.9 2.6 %collective-permute-start.2 = (bf16[128,256]{1,0:T(8,128)(2,1)S(1)}, bf16[128,256]{1,0:T(8,128)(2,1)S(1)}, u32[]{:S(2)}, u32[]{:S(2)}) collective-permute-start(bf16[128,256]{1,0:T(8,128)(2,1)S(1)} %pad_maximum_fusion.2), channel_id=1, source_target_pairs={{0,128},{128,0},{256,384},{384,256},{1,129},{129,1},{257,385},{385... | collective-permute-start | bytes 196616 | tf_op jit(solution)/shard_map/ppermute | solution.py:34
  123.5 3.5 %collective-permute-done.2 = bf16[128,256]{1,0:T(8,128)(2,1)S(1)} collective-permute-done((bf16[128,256]{1,0:T(8,128)(2,1)S(1)}, bf16[128,256]{1,0:T(8,128)(2,1)S(1)}, u32[]{:S(2)}, u32[]{:S(2)}) %collective-permute-start.2) | collective-permute-done | bytes 65568 | tf_op jit(solution)/shard_map/ppermute | solution.py:34
  127.0 2.1 %collective-permute-start.3 = (bf16[256,256]{1,0:T(8,128)(2,1)S(1)}, bf16[256,256]{1,0:T(8,128)(2,1)S(1)}, u32[]{:S(2)}, u32[]{:S(2)}) collective-permute-start(bf16[256,256]{1,0:T(8,128)(2,1)S(1)} %pad_maximum_fusion.1), channel_id=1, source_target_pairs={{0,384},{128,256},{256,128},{384,0},{1,385},{129,257},{257,129},{3... | collective-permute-start | bytes 393224 | tf_op jit(solution)/shard_map/ppermute | solution.py:34
  129.2 5.9 %collective-permute-done.3 = bf16[256,256]{1,0:T(8,128)(2,1)S(1)} collective-permute-done((bf16[256,256]{1,0:T(8,128)(2,1)S(1)}, bf16[256,256]{1,0:T(8,128)(2,1)S(1)}, u32[]{:S(2)}, u32[]{:S(2)}) %collective-permute-start.3) | collective-permute-done | bytes 131104 | tf_op jit(solution)/shard_map/ppermute | solution.py:34
  135.1 1.9 %collective-permute-start.4 = (bf16[512,256]{1,0:T(8,128)(2,1)S(1)}, bf16[512,256]{1,0:T(8,128)(2,1)S(1)}, u32[]{:S(2)}, u32[]{:S(2)}) collective-permute-start(bf16[512,256]{1,0:T(8,128)(2,1)S(1)} %get-tuple-element.9), channel_id=1, source_target_pairs={{0,16},{16,0},{1,17},{17,1},{2,18},{18,2},{3,19},{19,3},{4,20},{20... | collective-permute-start | bytes 786440 | tf_op jit(solution)/shard_map/ppermute | solution.py:34
  137.1 1.5 collective-permute-done.4
  139.9 25.2 %all_to_all.27.parts_ref = bf16[16,8,2048]{2,1,0:T(8,128)(2,1)S(1)} all-to-all(bf16[16,8,2048]{2,1,0:T(8,128)(2,1)S(1)} %fusion), channel_id=1, replica_groups=mesh['y'=4,'h'=4,'c'=2,'z'=4,'x'=4] {'z','x'}, dimensions={0} | all-to-all | bytes 1048576 | tf_op jit(solution)/shard_map/all_to_all | solution.py:38
  165.1 0.7 last_sum.1
  (49 shorter events, 2.4 us)
Async XLA Ops:
  0.0 139.3 %copy-start = (bf16[128,2048]{1,0:T(8,128)(2,1)S(1)}, bf16[128,2048]{1,0:T(8,128)(2,1)}, u32[]{:S(2)}) copy-start(bf16[128,2048]{1,0:T(8,128)(2,1)} %param.25) | copy-start | bytes 1572868
  0.0 6.4 %copy-start.4 = (bf16[128,2048]{1,0:T(8,128)(2,1)S(1)}, bf16[128,2048]{1,0:T(8,128)(2,1)}, u32[]{:S(2)}) copy-start(bf16[128,2048]{1,0:T(8,128)(2,1)} %param.16) | copy-start | bytes 1572868
  2.5 5.6 %copy-start.8 = (bf16[1024,128]{1,0:T(8,128)(2,1)S(1)}, bf16[1024,128]{1,0:T(8,128)(2,1)}, u32[]{:S(2)}) copy-start(bf16[1024,128]{1,0:T(8,128)(2,1)} %param.19) | copy-start | bytes 786436
  2.5 21.3 %collective-permute-start.5 = (bf16[128,1024]{1,0:T(8,128)(2,1)}, bf16[128,1024]{1,0:T(8,128)(2,1)S(1)}, u32[]{:S(2)}, u32[]{:S(2)}) collective-permute-start(bf16[128,1024]{1,0:T(8,128)(2,1)} %key_rows.1.refs_0_), channel_id=1, source_target_pairs={{0,4},{4,0},{8,12},{12,8},{1,5},{5,1},{9,13},{13,9},{2,6},{6,2},{1... | collective-permute-start | bytes 786440 | tf_op jit(solution)/shard_map/ppermute | solution.py:34
  8.0 10.5 %copy-start.7 = (bf16[128,1024]{1,0:T(8,128)(2,1)S(1)}, bf16[128,1024]{1,0:T(8,128)(2,1)}, u32[]{:S(2)}) copy-start(bf16[128,1024]{1,0:T(8,128)(2,1)} %key_rows.1.refs_0_) | copy-start | bytes 786436
  8.1 31.9 %copy-start.5 = (bf16[1024,256]{1,0:T(8,128)(2,1)}, bf16[1024,256]{1,0:T(8,128)(2,1)S(1)}, u32[]{:S(2)}) copy-start(bf16[1024,256]{1,0:T(8,128)(2,1)S(1)} %pad_maximum_fusion.refs_4_) | copy-start | bytes 1572868
  8.1 31.9 %collective-permute-start.8 = (bf16[1024,256]{1,0:T(8,128)(2,1)S(1)}, bf16[1024,256]{1,0:T(8,128)(2,1)S(1)}, u32[]{:S(2)}, u32[]{:S(2)}) collective-permute-start(bf16[1024,256]{1,0:T(8,128)(2,1)S(1)} %pad_maximum_fusion.refs_4_), channel_id=1, source_target_pairs={{0,1},{1,0},{2,3},{3,2},{4,5},{5,4},{6,7},{7,6},{8,9},{9,8},{10,11... | collective-permute-start | bytes 1572872 | tf_op jit(solution)/shard_map/ppermute | solution.py:34
  11.5 28.5 %collective-permute-start.9 = (bf16[1024,256]{1,0:T(8,128)(2,1)S(1)}, bf16[1024,256]{1,0:T(8,128)(2,1)S(1)}, u32[]{:S(2)}, u32[]{:S(2)}) collective-permute-start(bf16[1024,256]{1,0:T(8,128)(2,1)S(1)} %pad_maximum_fusion.refs_4_), channel_id=1, source_target_pairs={{0,2},{1,3},{2,0},{3,1},{4,6},{5,7},{6,4},{7,5},{8,10},{9,11},{10,... | collective-permute-start | bytes 1572872 | tf_op jit(solution)/shard_map/ppermute | solution.py:34
  16.2 27.3 %collective-permute-start.10 = (bf16[1024,256]{1,0:T(8,128)(2,1)S(1)}, bf16[1024,256]{1,0:T(8,128)(2,1)}, u32[]{:S(2)}, u32[]{:S(2)}) collective-permute-start(bf16[1024,256]{1,0:T(8,128)(2,1)S(1)} %pad_maximum_fusion.refs_4_), channel_id=1, source_target_pairs={{0,3},{1,2},{2,1},{3,0},{4,7},{5,6},{6,5},{7,4},{8,11},{9,10},{10,... | collective-permute-start | bytes 1572872 | tf_op jit(solution)/shard_map/ppermute | solution.py:34
  18.6 21.4 %collective-permute-start.6 = (bf16[128,1024]{1,0:T(8,128)(2,1)S(1)}, bf16[128,1024]{1,0:T(8,128)(2,1)S(1)}, u32[]{:S(2)}, u32[]{:S(2)}) collective-permute-start(bf16[128,1024]{1,0:T(8,128)(2,1)S(1)} %copy-done.7), channel_id=1, source_target_pairs={{0,8},{4,12},{8,0},{12,4},{1,9},{5,13},{9,1},{13,5},{2,10},{6,14},... | collective-permute-start | bytes 786440 | tf_op jit(solution)/shard_map/ppermute | solution.py:34
  23.8 19.7 %copy-start.12 = (bf16[128,1024]{1,0:T(8,128)(2,1)}, bf16[128,1024]{1,0:T(8,128)(2,1)S(1)}, u32[]{:S(2)}) copy-start(bf16[128,1024]{1,0:T(8,128)(2,1)S(1)} %collective-permute-done.5.refs_1_) | copy-start | bytes 786436
  23.8 16.2 %collective-permute-start.7 = (bf16[128,1024]{1,0:T(8,128)(2,1)S(1)}, bf16[128,1024]{1,0:T(8,128)(2,1)S(1)}, u32[]{:S(2)}, u32[]{:S(2)}) collective-permute-start(bf16[128,1024]{1,0:T(8,128)(2,1)S(1)} %copy-done.7), channel_id=1, source_target_pairs={{0,12},{4,8},{8,4},{12,0},{1,13},{5,9},{9,5},{13,1},{2,14},{6,10},... | collective-permute-start | bytes 786440 | tf_op jit(solution)/shard_map/ppermute | solution.py:34
  40.0 0.7 copy-start.13
  40.0 0.8 copy-start.14
  40.0 1.0 copy-start.10
  41.0 0.8 copy-start.11
  43.4 14.2 %copy-start.1 = (bf16[128,2048]{1,0:T(8,128)(2,1)S(1)}, bf16[128,2048]{1,0:T(8,128)(2,1)}, u32[]{:S(2)}) copy-start(bf16[128,2048]{1,0:T(8,128)(2,1)} %weight_ref.1) | copy-start | bytes 1572868
  58.0 21.4 %copy-start.9 = (bf16[2,2048]{1,0:T(2,128)(2,1)S(1)}, bf16[2,2048]{1,0:T(2,128)(2,1)}, u32[]{:S(2)}) copy-start(bf16[2,2048]{1,0:T(2,128)(2,1)} %param.21) | copy-start | bytes 24580
  80.1 13.4 %all-to-all-start = ((bf16[16,2,2048]{2,1,0:T(2,128)(2,1)}), bf16[16,2,2048]{2,1,0:T(2,128)(2,1)S(1)}, u32[]{:S(2)}, u32[]{:S(2)}) async-start(bf16[16,2,2048]{2,1,0:T(2,128)(2,1)} %broadcast_in_dim.2), calls=%async_computation | async-start | bytes 262144 | tf_op jit(solution)/shard_map/all_to_all | solution.py:38
  93.5 3.7 %copy-start.2 = (bf16[2048,128]{1,0:T(8,128)(2,1)S(1)}, bf16[2048,128]{1,0:T(8,128)(2,1)}, u32[]{:S(2)}) copy-start(bf16[2048,128]{1,0:T(8,128)(2,1)} %key_ref.1) | copy-start | bytes 1572868
  93.5 3.7 %copy-start.3 = (bf16[2048,128]{1,0:T(8,128)(2,1)S(1)}, bf16[2048,128]{1,0:T(8,128)(2,1)}, u32[]{:S(2)}) copy-start(bf16[2048,128]{1,0:T(8,128)(2,1)} %value_ref.1) | copy-start | bytes 1572868
  93.5 45.1 %all-to-all-start.3 = ((bf16[16,8,2048]{2,1,0:T(8,128)(2,1)}), bf16[16,8,2048]{2,1,0:T(8,128)(2,1)S(1)}, u32[]{:S(2)}, u32[]{:S(2)}) async-start(bf16[16,8,2048]{2,1,0:T(8,128)(2,1)} %get-tuple-element.7), calls=%async_computation.3 | async-start | bytes 1048576 | tf_op jit(solution)/shard_map/all_to_all | solution.py:38
  97.5 10.9 %collective-permute-start = (bf16[32,256]{1,0:T(8,128)(2,1)S(1)}, bf16[32,256]{1,0:T(8,128)(2,1)S(1)}, u32[]{:S(2)}, u32[]{:S(2)}) collective-permute-start(bf16[32,256]{1,0:T(8,128)(2,1)S(1)} %decode_pairs.1), channel_id=1, source_target_pairs={{0,32},{32,0},{64,96},{96,64},{1,33},{33,1},{65,97},{97,65},{2,34}... | collective-permute-start | bytes 49160 | tf_op jit(solution)/shard_map/ppermute | solution.py:34
  108.4 12.5 %collective-permute-start.1 = (bf16[64,256]{1,0:T(8,128)(2,1)S(1)}, bf16[64,256]{1,0:T(8,128)(2,1)S(1)}, u32[]{:S(2)}, u32[]{:S(2)}) collective-permute-start(bf16[64,256]{1,0:T(8,128)(2,1)S(1)} %pad_maximum_fusion.3), channel_id=1, source_target_pairs={{0,96},{32,64},{64,32},{96,0},{1,97},{33,65},{65,33},{97,1},{2,98}... | collective-permute-start | bytes 98312 | tf_op jit(solution)/shard_map/ppermute | solution.py:34
  120.9 6.1 %collective-permute-start.2 = (bf16[128,256]{1,0:T(8,128)(2,1)S(1)}, bf16[128,256]{1,0:T(8,128)(2,1)S(1)}, u32[]{:S(2)}, u32[]{:S(2)}) collective-permute-start(bf16[128,256]{1,0:T(8,128)(2,1)S(1)} %pad_maximum_fusion.2), channel_id=1, source_target_pairs={{0,128},{128,0},{256,384},{384,256},{1,129},{129,1},{257,385},{385... | collective-permute-start | bytes 196616 | tf_op jit(solution)/shard_map/ppermute | solution.py:34
  127.0 8.1 %collective-permute-start.3 = (bf16[256,256]{1,0:T(8,128)(2,1)S(1)}, bf16[256,256]{1,0:T(8,128)(2,1)S(1)}, u32[]{:S(2)}, u32[]{:S(2)}) collective-permute-start(bf16[256,256]{1,0:T(8,128)(2,1)S(1)} %pad_maximum_fusion.1), channel_id=1, source_target_pairs={{0,384},{128,256},{256,128},{384,0},{1,385},{129,257},{257,129},{3... | collective-permute-start | bytes 393224 | tf_op jit(solution)/shard_map/ppermute | solution.py:34
  129.2 9.4 %copy-start.6 = (bf16[2048,128]{1,0:T(8,128)(2,1)S(1)}, bf16[2048,128]{1,0:T(8,128)(2,1)}, u32[]{:S(2)}) copy-start(bf16[2048,128]{1,0:T(8,128)(2,1)} %param.22) | copy-start | bytes 1572868
  135.1 3.4 %collective-permute-start.4 = (bf16[512,256]{1,0:T(8,128)(2,1)S(1)}, bf16[512,256]{1,0:T(8,128)(2,1)S(1)}, u32[]{:S(2)}, u32[]{:S(2)}) collective-permute-start(bf16[512,256]{1,0:T(8,128)(2,1)S(1)} %get-tuple-element.9), channel_id=1, source_target_pairs={{0,16},{16,0},{1,17},{17,1},{2,18},{18,2},{3,19},{19,3},{4,20},{20... | collective-permute-start | bytes 786440 | tf_op jit(solution)/shard_map/ppermute | solution.py:34

commit v5 on v4

--- a/solution.py
+++ b/solution.py
@@ -47,30 +47,39 @@
     return pl.CostEstimate(flops=flops, bytes_accessed=size, transcendentals=0)
 
 
-def key_kernel(slot_ref, group_ref, embed_ref, out_ref):
+def prepare_kernel(
+    slot_ref, group_ref, embed_ref, merge_ref, query_ref, key_ref, value_ref, keyed_ref, pack_ref
+):
     lines = lax.broadcasted_iota(jnp.int32, embed_ref.shape, 0)
     chosen = jnp.where(lines == slot_ref[0, 0], embed_ref[...].astype(F32), 0.0)
     keyed = group_ref[...].astype(F32) + jnp.sum(chosen, axis=0, keepdims=True)
-    out_ref[...] = keyed.astype(BF16)
-
-
-def key_rows(slot_ids, group_latents, slot_embed):
-    return pl.pallas_call(
-        key_kernel,
-        out_shape=jax.ShapeDtypeStruct(group_latents.shape, BF16),
-        in_specs=[pl.BlockSpec(memory_space=pltpu.SMEM), VMEM, VMEM],
-        out_specs=VMEM,
+    keyed_ref[...] = keyed.astype(BF16)
+    query = dot(merge_ref[...], query_ref[...], ((1,), (0,))).astype(BF16)
+    length = query.shape[0]
+    pack_ref[:, :length] = dot(key_ref[...], query, ((1,), (1,))).astype(BF16)
+    pack_ref[:, length:] = value_ref[...]
+
+
+def prepare(slot_ids, group_latents, slot_embed, merge_latents, query, key, value):
+    depth, columns = key.shape
+    return pl.pallas_call(
+        prepare_kernel,
+        out_shape=[
+            jax.ShapeDtypeStruct(group_latents.shape, BF16),
+            jax.ShapeDtypeStruct((depth, merge_latents.shape[0] + columns), BF16),
+        ],
+        in_specs=[pl.BlockSpec(memory_space=pltpu.SMEM)] + [VMEM] * 6,
+        out_specs=[VMEM, VMEM],
         compiler_params=WIDE,
-        cost_estimate=cost(4 * group_latents.size, 2**20),
-        name="key_rows",
-    )(slot_ids, group_latents, slot_embed)
-
-
-def attend_one(blocks_ref, pack):
-    many = blocks_ref.shape[0]
-    both = [dot(blocks_ref[j], pack, ((1,), (0,))) for j in range(many)]
-    scores = jnp.concatenate([b[:, :-HEAD] for b in both], axis=0) * SCALE
-    values = jnp.concatenate([b[:, -HEAD:].astype(BF16) for b in both], axis=0)
+        cost_estimate=cost(2 * merge_latents.size * columns * 2, 2**20),
+        name="prepare",
+    )(slot_ids, group_latents, slot_embed, merge_latents, query, key, value)
+
+
+def attend_one(blocks, pack):
+    both = dot(blocks, pack, ((1,), (0,)))
+    scores = both[:, :-HEAD] * SCALE
+    values = both[:, -HEAD:].astype(BF16)
     top = jnp.max(scores, axis=0, keepdims=True)
     weights = jnp.exp(scores - top)
     total = jnp.sum(weights, axis=0, keepdims=True)
@@ -86,9 +95,10 @@
 
 def attend_kernel(count, *refs):
     given, (out_ref, blocks_ref, packs_ref, sems) = refs[:-4], refs[-4:]
+    size = given[0].shape[0]
     copies = []
     for k, ref in enumerate(given):
-        target = blocks_ref.at[k] if k < count else packs_ref.at[k - count]
+        target = blocks_ref.at[pl.ds(k * size, size)] if k < count else packs_ref.at[k - count]
         copies.append(pltpu.make_async_copy(ref, target, sems.at[k]))
         copies[-1].start()
     for copy in copies[:count]:
@@ -96,7 +106,7 @@
     mine = lax.axis_index("x")
     for k, copy in enumerate(copies[count:]):
         copy.wait()
-        out_ref[mine ^ k] = attend_one(blocks_ref, packs_ref[k])
+        out_ref[mine ^ k] = attend_one(blocks_ref[...], packs_ref[k])
 
 
 def attend_part(blocks, packs):
@@ -110,7 +120,7 @@
         in_specs=[pl.BlockSpec(memory_space=pl.ANY)] * (count + many),
         out_specs=VMEM,
         scratch_shapes=[
-            pltpu.VMEM((count, *blocks[0].shape), BF16),
+            pltpu.VMEM((keys, blocks[0].shape[1]), BF16),
             pltpu.VMEM((many, *packs[0].shape), BF16),
             pltpu.SemaphoreType.DMA((count + many,)),
         ],
@@ -232,12 +242,11 @@
     length, width = merge_latents.shape
     rows = length // inner
 
-    query_two = dot(merge_latents, query_weight, ((1,), (0,))).astype(BF16)
-    folded = dot(key_weight, query_two, ((1,), (1,))).astype(BF16)
-    pack = jnp.concatenate([folded, value_weight], axis=1)
     own_rows = lax.dynamic_slice_in_dim(merge_latents, lax.axis_index(INNER) * rows, rows, 0)
 
-    keyed = key_rows(slot_ids, group_latents, slot_embed)
+    keyed, pack = prepare(
+        slot_ids, group_latents, slot_embed, merge_latents, query_weight, key_weight, value_weight
+    )
     pack_two = partner(pack, "x", 2)
     keyed_three = partner(keyed, "z", 3)
     outer_block = all_from(global_latents, INNER)

time: 167 us -> 167 us (level)
  Pallas kernels: 8.91 us -> 11.1 us
where the time goes in v5:
time: 167 us; the launch traced here: 166 us
  starting transfers between devices  55.8 us (33%)
  blocking collectives  55.7 us (33%)
  waiting for transfers between devices  38 us (23%)
  Pallas kernels  11.1 us (7%)
  local copies, waits for them, and re-layouts  3.16 us (2%)
    all_to_all x3, blocking collectives, exchange(): return lax.all_to_all(tiles, axis, split_axis=0, concat_axis=0, tiled=True)  55.7 us
    ppermute x11, starting transfers between devices, partner(): return lax.ppermute(value, axis, pairs)  47.7 us
    ppermute x11, waiting for transfers between devices, partner(): return lax.ppermute(value, axis, pairs)  30.9 us
    all_to_all x2, starting transfers between devices, exchange(): return lax.all_to_all(tiles, axis, split_axis=0, concat_axis=0, tiled=True)  8.15 us
    all_to_all x2, waiting for transfers between devices, exchange(): return lax.all_to_all(tiles, axis, split_axis=0, concat_axis=0, tiled=True)  7.11 us
    pallas_call x1, Pallas kernels, attend_part(): pl.pallas_call(functools.partial(attend_kernel, count), out_shape=jax.Sha...  5.81 us
  transfers between devices with their start and end apart: 13, of which 8 were waited for; matrix products, arithmetic and copies ran while one was open for 1% of the time, Pallas kernels for 1%

profile of v5, /device:TPU:24, one launch (start us, length us, event | category | flops | bytes accessed | tf_op | source)
XLA Modules:
  0.0 166.1 jit_solution(11195482050254548809)
XLA Ops:
  0.7 2.9 %prepare.1 = (bf16[128,1024]{1,0:T(8,128)(2,1)}, bf16[1024,256]{1,0:T(8,128)(2,1)}) custom-call(s32[1,1]{1,0:T(1,128)S(6)} %copy.23.slot_ref, bf16[128,1024]{1,0:T(8,128)(2,1)} %group_ref.1, bf16[16,1024]{1,0:T(8,128)(2,1)} %embed_ref.1, bf16[128,2048]{1,0:T(8,128)(2,1)} %merge_ref.1, bf16[2048,128]{1,0:T(8,128)(2,1)} %query_ref.1, ...), custom_call_target="tpu_custom_call" | custom-call | flops 134217728 | bytes 1048576 | tf_op jit(solution)/shard_map/prepare/pallas_call | solution.py:65
  3.6 3.8 %collective-permute-start.5 = (bf16[128,1024]{1,0:T(8,128)(2,1)}, bf16[128,1024]{1,0:T(8,128)(2,1)S(1)}, u32[]{:S(2)}, u32[]{:S(2)}) collective-permute-start(bf16[128,1024]{1,0:T(8,128)(2,1)} %get-tuple-element.9.refs_0_), channel_id=1, source_target_pairs={{0,4},{4,0},{8,12},{12,8},{1,5},{5,1},{9,13},{13,9},{2,6},{6,2},{1... | collective-permute-start | bytes 786440 | tf_op jit(solution)/shard_map/ppermute | solution.py:34
  7.4 3.4 %collective-permute-start.8 = (bf16[1024,256]{1,0:T(8,128)(2,1)}, bf16[1024,256]{1,0:T(8,128)(2,1)S(1)}, u32[]{:S(2)}, u32[]{:S(2)}) collective-permute-start(bf16[1024,256]{1,0:T(8,128)(2,1)} %get-tuple-element.10.refs_4_), channel_id=1, source_target_pairs={{0,1},{1,0},{2,3},{3,2},{4,5},{5,4},{6,7},{7,6},{8,9},{9,8},{10,11... | collective-permute-start | bytes 1572872 | tf_op jit(solution)/shard_map/ppermute | solution.py:34
  10.9 4.6 %collective-permute-start.9 = (bf16[1024,256]{1,0:T(8,128)(2,1)}, bf16[1024,256]{1,0:T(8,128)(2,1)S(1)}, u32[]{:S(2)}, u32[]{:S(2)}) collective-permute-start(bf16[1024,256]{1,0:T(8,128)(2,1)} %get-tuple-element.10.refs_4_), channel_id=1, source_target_pairs={{0,2},{1,3},{2,0},{3,1},{4,6},{5,7},{6,4},{7,5},{8,10},{9,11},{10,... | collective-permute-start | bytes 1572872 | tf_op jit(solution)/shard_map/ppermute | solution.py:34
  15.5 2.4 %collective-permute-start.10 = (bf16[1024,256]{1,0:T(8,128)(2,1)}, bf16[1024,256]{1,0:T(8,128)(2,1)}, u32[]{:S(2)}, u32[]{:S(2)}) collective-permute-start(bf16[1024,256]{1,0:T(8,128)(2,1)} %get-tuple-element.10.refs_4_), channel_id=1, source_target_pairs={{0,3},{1,2},{2,1},{3,0},{4,7},{5,6},{6,5},{7,4},{8,11},{9,10},{10,... | collective-permute-start | bytes 1572872 | tf_op jit(solution)/shard_map/ppermute | solution.py:34
  17.9 5.2 %collective-permute-start.6 = (bf16[128,1024]{1,0:T(8,128)(2,1)}, bf16[128,1024]{1,0:T(8,128)(2,1)S(1)}, u32[]{:S(2)}, u32[]{:S(2)}) collective-permute-start(bf16[128,1024]{1,0:T(8,128)(2,1)} %get-tuple-element.9.refs_0_), channel_id=1, source_target_pairs={{0,8},{4,12},{8,0},{12,4},{1,9},{5,13},{9,1},{13,5},{2,10},{6,14},... | collective-permute-start | bytes 786440 | tf_op jit(solution)/shard_map/ppermute | solution.py:34
  23.1 1.9 %collective-permute-start.7 = (bf16[128,1024]{1,0:T(8,128)(2,1)}, bf16[128,1024]{1,0:T(8,128)(2,1)S(1)}, u32[]{:S(2)}, u32[]{:S(2)}) collective-permute-start(bf16[128,1024]{1,0:T(8,128)(2,1)} %get-tuple-element.9.refs_0_), channel_id=1, source_target_pairs={{0,12},{4,8},{8,4},{12,0},{1,13},{5,9},{9,5},{13,1},{2,14},{6,10},... | collective-permute-start | bytes 786440 | tf_op jit(solution)/shard_map/ppermute | solution.py:34
  25.0 14.5 %collective-permute-done.6.refs_2_ = bf16[128,1024]{1,0:T(8,128)(2,1)S(1)} collective-permute-done((bf16[128,1024]{1,0:T(8,128)(2,1)}, bf16[128,1024]{1,0:T(8,128)(2,1)S(1)}, u32[]{:S(2)}, u32[]{:S(2)}) %collective-permute-start.6) | collective-permute-done | bytes 262176 | tf_op jit(solution)/shard_map/ppermute | solution.py:34
  39.5 0.7 copy-done.9
  40.3 0.8 copy-done.7
  41.1 1.9 %collective-permute-done.10.refs_7_ = bf16[1024,256]{1,0:T(8,128)(2,1)} collective-permute-done((bf16[1024,256]{1,0:T(8,128)(2,1)}, bf16[1024,256]{1,0:T(8,128)(2,1)}, u32[]{:S(2)}, u32[]{:S(2)}) %collective-permute-start.10) | collective-permute-done | bytes 524320 | tf_op jit(solution)/shard_map/ppermute | solution.py:34
  43.0 5.8 %attend_part.1 = bf16[4,144,128]{2,1,0:T(8,128)(2,1)} custom-call(bf16[128,1024]{1,0:T(8,128)(2,1)} %get-tuple-element.9.refs_0_, bf16[128,1024]{1,0:T(8,128)(2,1)} %copy-done.8, bf16[128,1024]{1,0:T(8,128)(2,1)} %copy-done.9, bf16[128,1024]{1,0:T(8,128)(2,1)} %copy-done.10, bf16[1024,256]{1,0:T(8,128)(2,1)} %get-tuple-element.10.refs_4_, ...), custom_call_target="tpu_custom_call" | custom-call | flops 1140850688 | bytes 3145728 | tf_op jit(solution)/shard_map/attend_part/pallas_call | solution.py:117
  48.8 9.4 %all_to_all.25.parts_ref = bf16[4,144,128]{2,1,0:T(8,128)(2,1)S(1)} all-to-all(bf16[4,144,128]{2,1,0:T(8,128)(2,1)} %attend_part.1), channel_id=1, replica_groups=mesh['y'=4,'h'=4,'c'=2,'z'=4,'x'=4] {'x'}, dimensions={0} | all-to-all | bytes 294912 | tf_op jit(solution)/shard_map/all_to_all | solution.py:38
  58.6 21.2 %all_to_all.26.parts_ref = bf16[16,8,2048]{2,1,0:T(8,128)(2,1)S(1)} all-to-all(bf16[16,8,2048]{2,1,0:T(8,128)(2,1)S(1)} %bitcast.11), channel_id=1, replica_groups=mesh['y'=4,'h'=4,'c'=2,'z'=4,'x'=4] {'z','x'}, dimensions={0} | all-to-all | bytes 1048576 | tf_op jit(solution)/shard_map/all_to_all | solution.py:38
  79.7 0.7 broadcast_in_dim.2
  80.4 4.4 %all-to-all-start = ((bf16[16,2,2048]{2,1,0:T(2,128)(2,1)}), bf16[16,2,2048]{2,1,0:T(2,128)(2,1)S(1)}, u32[]{:S(2)}, u32[]{:S(2)}) async-start(bf16[16,2,2048]{2,1,0:T(2,128)(2,1)} %broadcast_in_dim.2), calls=%async_computation | async-start | bytes 262144 | tf_op jit(solution)/shard_map/all_to_all | solution.py:38
  84.9 0.8 constant_dynamic-slice_fusion.own_ref
  85.7 1.0 sum_and_norm.1
  86.7 7.1 %all-to-all-done.parts_ref = bf16[16,2,2048]{2,1,0:T(2,128)(2,1)S(1)} async-done(((bf16[16,2,2048]{2,1,0:T(2,128)(2,1)}), bf16[16,2,2048]{2,1,0:T(2,128)(2,1)S(1)}, u32[]{:S(2)}, u32[]{:S(2)}) %all-to-all-start) | async-done | bytes 131104 | tf_op jit(solution)/shard_map/all_to_all | solution.py:38
  93.8 3.7 %all-to-all-start.3 = ((bf16[16,8,2048]{2,1,0:T(8,128)(2,1)}), bf16[16,8,2048]{2,1,0:T(8,128)(2,1)S(1)}, u32[]{:S(2)}, u32[]{:S(2)}) async-start(bf16[16,8,2048]{2,1,0:T(8,128)(2,1)} %get-tuple-element.11), calls=%async_computation.3 | async-start | bytes 1048576 | tf_op jit(solution)/shard_map/all_to_all | solution.py:38
  97.8 9.1 %collective-permute-start = (bf16[32,256]{1,0:T(8,128)(2,1)S(1)}, bf16[32,256]{1,0:T(8,128)(2,1)S(1)}, u32[]{:S(2)}, u32[]{:S(2)}) collective-permute-start(bf16[32,256]{1,0:T(8,128)(2,1)S(1)} %decode_pairs.1), channel_id=1, source_target_pairs={{0,32},{32,0},{64,96},{96,64},{1,33},{33,1},{65,97},{97,65},{2,34}... | collective-permute-start | bytes 49160 | tf_op jit(solution)/shard_map/ppermute | solution.py:34
  106.9 1.8 %collective-permute-done = bf16[32,256]{1,0:T(8,128)(2,1)S(1)} collective-permute-done((bf16[32,256]{1,0:T(8,128)(2,1)S(1)}, bf16[32,256]{1,0:T(8,128)(2,1)S(1)}, u32[]{:S(2)}, u32[]{:S(2)}) %collective-permute-start) | collective-permute-done | bytes 16416 | tf_op jit(solution)/shard_map/ppermute | solution.py:34
  108.7 10.5 %collective-permute-start.1 = (bf16[64,256]{1,0:T(8,128)(2,1)S(1)}, bf16[64,256]{1,0:T(8,128)(2,1)S(1)}, u32[]{:S(2)}, u32[]{:S(2)}) collective-permute-start(bf16[64,256]{1,0:T(8,128)(2,1)S(1)} %pad_maximum_fusion.2), channel_id=1, source_target_pairs={{0,96},{32,64},{64,32},{96,0},{1,97},{33,65},{65,33},{97,1},{2,98}... | collective-permute-start | bytes 98312 | tf_op jit(solution)/shard_map/ppermute | solution.py:34
  119.3 1.9 %collective-permute-done.1 = bf16[64,256]{1,0:T(8,128)(2,1)S(1)} collective-permute-done((bf16[64,256]{1,0:T(8,128)(2,1)S(1)}, bf16[64,256]{1,0:T(8,128)(2,1)S(1)}, u32[]{:S(2)}, u32[]{:S(2)}) %collective-permute-start.1) | collective-permute-done | bytes 32800 | tf_op jit(solution)/shard_map/ppermute | solution.py:34
  121.2 2.6 %collective-permute-start.2 = (bf16[128,256]{1,0:T(8,128)(2,1)S(1)}, bf16[128,256]{1,0:T(8,128)(2,1)S(1)}, u32[]{:S(2)}, u32[]{:S(2)}) collective-permute-start(bf16[128,256]{1,0:T(8,128)(2,1)S(1)} %pad_maximum_fusion.1), channel_id=1, source_target_pairs={{0,128},{128,0},{256,384},{384,256},{1,129},{129,1},{257,385},{385... | collective-permute-start | bytes 196616 | tf_op jit(solution)/shard_map/ppermute | solution.py:34
  123.8 3.5 %collective-permute-done.2 = bf16[128,256]{1,0:T(8,128)(2,1)S(1)} collective-permute-done((bf16[128,256]{1,0:T(8,128)(2,1)S(1)}, bf16[128,256]{1,0:T(8,128)(2,1)S(1)}, u32[]{:S(2)}, u32[]{:S(2)}) %collective-permute-start.2) | collective-permute-done | bytes 65568 | tf_op jit(solution)/shard_map/ppermute | solution.py:34
  127.3 2.1 %collective-permute-start.3 = (bf16[256,256]{1,0:T(8,128)(2,1)S(1)}, bf16[256,256]{1,0:T(8,128)(2,1)S(1)}, u32[]{:S(2)}, u32[]{:S(2)}) collective-permute-start(bf16[256,256]{1,0:T(8,128)(2,1)S(1)} %pad_maximum_fusion), channel_id=1, source_target_pairs={{0,384},{128,256},{256,128},{384,0},{1,385},{129,257},{257,129},{3... | collective-permute-start | bytes 393224 | tf_op jit(solution)/shard_map/ppermute | solution.py:34
  129.5 5.9 %collective-permute-done.3 = bf16[256,256]{1,0:T(8,128)(2,1)S(1)} collective-permute-done((bf16[256,256]{1,0:T(8,128)(2,1)S(1)}, bf16[256,256]{1,0:T(8,128)(2,1)S(1)}, u32[]{:S(2)}, u32[]{:S(2)}) %collective-permute-start.3) | collective-permute-done | bytes 131104 | tf_op jit(solution)/shard_map/ppermute | solution.py:34
  135.4 1.9 %collective-permute-start.4 = (bf16[512,256]{1,0:T(8,128)(2,1)S(1)}, bf16[512,256]{1,0:T(8,128)(2,1)S(1)}, u32[]{:S(2)}, u32[]{:S(2)}) collective-permute-start(bf16[512,256]{1,0:T(8,128)(2,1)S(1)} %get-tuple-element.13), channel_id=1, source_target_pairs={{0,16},{16,0},{1,17},{17,1},{2,18},{18,2},{3,19},{19,3},{4,20},{20... | collective-permute-start | bytes 786440 | tf_op jit(solution)/shard_map/ppermute | solution.py:34
  137.4 1.5 collective-permute-done.4
  140.2 25.2 %all_to_all.27.parts_ref = bf16[16,8,2048]{2,1,0:T(8,128)(2,1)S(1)} all-to-all(bf16[16,8,2048]{2,1,0:T(8,128)(2,1)S(1)} %fusion), channel_id=1, replica_groups=mesh['y'=4,'h'=4,'c'=2,'z'=4,'x'=4] {'z','x'}, dimensions={0} | all-to-all | bytes 1048576 | tf_op jit(solution)/shard_map/all_to_all | solution.py:38
  165.4 0.7 last_sum.1
  (39 shorter events, 2.1 us)
Async XLA Ops:
  0.0 139.7 %copy-start = (bf16[128,2048]{1,0:T(8,128)(2,1)S(1)}, bf16[128,2048]{1,0:T(8,128)(2,1)}, u32[]{:S(2)}) copy-start(bf16[128,2048]{1,0:T(8,128)(2,1)} %param.25) | copy-start | bytes 1572868
  3.6 19.5 %collective-permute-start.5 = (bf16[128,1024]{1,0:T(8,128)(2,1)}, bf16[128,1024]{1,0:T(8,128)(2,1)S(1)}, u32[]{:S(2)}, u32[]{:S(2)}) collective-permute-start(bf16[128,1024]{1,0:T(8,128)(2,1)} %get-tuple-element.9.refs_0_), channel_id=1, source_target_pairs={{0,4},{4,0},{8,12},{12,8},{1,5},{5,1},{9,13},{13,9},{2,6},{6,2},{1... | collective-permute-start | bytes 786440 | tf_op jit(solution)/shard_map/ppermute | solution.py:34
  7.4 32.1 %collective-permute-start.8 = (bf16[1024,256]{1,0:T(8,128)(2,1)}, bf16[1024,256]{1,0:T(8,128)(2,1)S(1)}, u32[]{:S(2)}, u32[]{:S(2)}) collective-permute-start(bf16[1024,256]{1,0:T(8,128)(2,1)} %get-tuple-element.10.refs_4_), channel_id=1, source_target_pairs={{0,1},{1,0},{2,3},{3,2},{4,5},{5,4},{6,7},{7,6},{8,9},{9,8},{10,11... | collective-permute-start | bytes 1572872 | tf_op jit(solution)/shard_map/ppermute | solution.py:34
  10.9 28.7 %collective-permute-start.9 = (bf16[1024,256]{1,0:T(8,128)(2,1)}, bf16[1024,256]{1,0:T(8,128)(2,1)S(1)}, u32[]{:S(2)}, u32[]{:S(2)}) collective-permute-start(bf16[1024,256]{1,0:T(8,128)(2,1)} %get-tuple-element.10.refs_4_), channel_id=1, source_target_pairs={{0,2},{1,3},{2,0},{3,1},{4,6},{5,7},{6,4},{7,5},{8,10},{9,11},{10,... | collective-permute-start | bytes 1572872 | tf_op jit(solution)/shard_map/ppermute | solution.py:34
  15.5 27.5 %collective-permute-start.10 = (bf16[1024,256]{1,0:T(8,128)(2,1)}, bf16[1024,256]{1,0:T(8,128)(2,1)}, u32[]{:S(2)}, u32[]{:S(2)}) collective-permute-start(bf16[1024,256]{1,0:T(8,128)(2,1)} %get-tuple-element.10.refs_4_), channel_id=1, source_target_pairs={{0,3},{1,2},{2,1},{3,0},{4,7},{5,6},{6,5},{7,4},{8,11},{9,10},{10,... | collective-permute-start | bytes 1572872 | tf_op jit(solution)/shard_map/ppermute | solution.py:34
  17.9 21.6 %collective-permute-start.6 = (bf16[128,1024]{1,0:T(8,128)(2,1)}, bf16[128,1024]{1,0:T(8,128)(2,1)S(1)}, u32[]{:S(2)}, u32[]{:S(2)}) collective-permute-start(bf16[128,1024]{1,0:T(8,128)(2,1)} %get-tuple-element.9.refs_0_), channel_id=1, source_target_pairs={{0,8},{4,12},{8,0},{12,4},{1,9},{5,13},{9,1},{13,5},{2,10},{6,14},... | collective-permute-start | bytes 786440 | tf_op jit(solution)/shard_map/ppermute | solution.py:34
  23.1 19.9 %copy-start.8 = (bf16[128,1024]{1,0:T(8,128)(2,1)}, bf16[128,1024]{1,0:T(8,128)(2,1)S(1)}, u32[]{:S(2)}) copy-start(bf16[128,1024]{1,0:T(8,128)(2,1)S(1)} %collective-permute-done.5.refs_1_) | copy-start | bytes 786436
  23.1 16.4 %collective-permute-start.7 = (bf16[128,1024]{1,0:T(8,128)(2,1)}, bf16[128,1024]{1,0:T(8,128)(2,1)S(1)}, u32[]{:S(2)}, u32[]{:S(2)}) collective-permute-start(bf16[128,1024]{1,0:T(8,128)(2,1)} %get-tuple-element.9.refs_0_), channel_id=1, source_target_pairs={{0,12},{4,8},{8,4},{12,0},{1,13},{5,9},{9,5},{13,1},{2,14},{6,10},... | collective-permute-start | bytes 786440 | tf_op jit(solution)/shard_map/ppermute | solution.py:34
  39.5 0.7 copy-start.9
  39.5 0.8 copy-start.10
  39.5 3.5 %copy-start.6 = (bf16[1024,256]{1,0:T(8,128)(2,1)}, bf16[1024,256]{1,0:T(8,128)(2,1)S(1)}, u32[]{:S(2)}) copy-start(bf16[1024,256]{1,0:T(8,128)(2,1)S(1)} %collective-permute-done.8.refs_5_) | copy-start | bytes 1572868
  40.3 0.8 copy-start.7
  43.0 15.2 %copy-start.1 = (bf16[128,2048]{1,0:T(8,128)(2,1)S(1)}, bf16[128,2048]{1,0:T(8,128)(2,1)}, u32[]{:S(2)}) copy-start(bf16[128,2048]{1,0:T(8,128)(2,1)} %weight_ref.1) | copy-start | bytes 1572868
  58.5 21.2 %copy-start.5 = (bf16[2,2048]{1,0:T(2,128)(2,1)S(1)}, bf16[2,2048]{1,0:T(2,128)(2,1)}, u32[]{:S(2)}) copy-start(bf16[2,2048]{1,0:T(2,128)(2,1)} %param.21) | copy-start | bytes 24580
  80.4 13.4 %all-to-all-start = ((bf16[16,2,2048]{2,1,0:T(2,128)(2,1)}), bf16[16,2,2048]{2,1,0:T(2,128)(2,1)S(1)}, u32[]{:S(2)}, u32[]{:S(2)}) async-start(bf16[16,2,2048]{2,1,0:T(2,128)(2,1)} %broadcast_in_dim.2), calls=%async_computation | async-start | bytes 262144 | tf_op jit(solution)/shard_map/all_to_all | solution.py:38
  93.8 3.7 %copy-start.2 = (bf16[2048,128]{1,0:T(8,128)(2,1)S(1)}, bf16[2048,128]{1,0:T(8,128)(2,1)}, u32[]{:S(2)}) copy-start(bf16[2048,128]{1,0:T(8,128)(2,1)} %key_ref.2) | copy-start | bytes 1572868
  93.8 3.7 %copy-start.3 = (bf16[2048,128]{1,0:T(8,128)(2,1)S(1)}, bf16[2048,128]{1,0:T(8,128)(2,1)}, u32[]{:S(2)}) copy-start(bf16[2048,128]{1,0:T(8,128)(2,1)} %value_ref.2) | copy-start | bytes 1572868
  93.8 45.1 %all-to-all-start.3 = ((bf16[16,8,2048]{2,1,0:T(8,128)(2,1)}), bf16[16,8,2048]{2,1,0:T(8,128)(2,1)S(1)}, u32[]{:S(2)}, u32[]{:S(2)}) async-start(bf16[16,8,2048]{2,1,0:T(8,128)(2,1)} %get-tuple-element.11), calls=%async_computation.3 | async-start | bytes 1048576 | tf_op jit(solution)/shard_map/all_to_all | solution.py:38
  97.8 10.9 %collective-permute-start = (bf16[32,256]{1,0:T(8,128)(2,1)S(1)}, bf16[32,256]{1,0:T(8,128)(2,1)S(1)}, u32[]{:S(2)}, u32[]{:S(2)}) collective-permute-start(bf16[32,256]{1,0:T(8,128)(2,1)S(1)} %decode_pairs.1), channel_id=1, source_target_pairs={{0,32},{32,0},{64,96},{96,64},{1,33},{33,1},{65,97},{97,65},{2,34}... | collective-permute-start | bytes 49160 | tf_op jit(solution)/shard_map/ppermute | solution.py:34
  108.7 12.4 %collective-permute-start.1 = (bf16[64,256]{1,0:T(8,128)(2,1)S(1)}, bf16[64,256]{1,0:T(8,128)(2,1)S(1)}, u32[]{:S(2)}, u32[]{:S(2)}) collective-permute-start(bf16[64,256]{1,0:T(8,128)(2,1)S(1)} %pad_maximum_fusion.2), channel_id=1, source_target_pairs={{0,96},{32,64},{64,32},{96,0},{1,97},{33,65},{65,33},{97,1},{2,98}... | collective-permute-start | bytes 98312 | tf_op jit(solution)/shard_map/ppermute | solution.py:34
  121.2 6.1 %collective-permute-start.2 = (bf16[128,256]{1,0:T(8,128)(2,1)S(1)}, bf16[128,256]{1,0:T(8,128)(2,1)S(1)}, u32[]{:S(2)}, u32[]{:S(2)}) collective-permute-start(bf16[128,256]{1,0:T(8,128)(2,1)S(1)} %pad_maximum_fusion.1), channel_id=1, source_target_pairs={{0,128},{128,0},{256,384},{384,256},{1,129},{129,1},{257,385},{385... | collective-permute-start | bytes 196616 | tf_op jit(solution)/shard_map/ppermute | solution.py:34
  127.3 8.1 %collective-permute-start.3 = (bf16[256,256]{1,0:T(8,128)(2,1)S(1)}, bf16[256,256]{1,0:T(8,128)(2,1)S(1)}, u32[]{:S(2)}, u32[]{:S(2)}) collective-permute-start(bf16[256,256]{1,0:T(8,128)(2,1)S(1)} %pad_maximum_fusion), channel_id=1, source_target_pairs={{0,384},{128,256},{256,128},{384,0},{1,385},{129,257},{257,129},{3... | collective-permute-start | bytes 393224 | tf_op jit(solution)/shard_map/ppermute | solution.py:34
  129.5 9.4 %copy-start.4 = (bf16[2048,128]{1,0:T(8,128)(2,1)S(1)}, bf16[2048,128]{1,0:T(8,128)(2,1)}, u32[]{:S(2)}) copy-start(bf16[2048,128]{1,0:T(8,128)(2,1)} %param.22) | copy-start | bytes 1572868
  135.4 3.4 %collective-permute-start.4 = (bf16[512,256]{1,0:T(8,128)(2,1)S(1)}, bf16[512,256]{1,0:T(8,128)(2,1)S(1)}, u32[]{:S(2)}, u32[]{:S(2)}) collective-permute-start(bf16[512,256]{1,0:T(8,128)(2,1)S(1)} %get-tuple-element.13), channel_id=1, source_target_pairs={{0,16},{16,0},{1,17},{17,1},{2,18},{18,2},{3,19},{19,3},{4,20},{20... | collective-permute-start | bytes 786440 | tf_op jit(solution)/shard_map/ppermute | solution.py:34

commit v6 on v5

--- a/solution.py
+++ b/solution.py
@@ -76,58 +76,83 @@
     )(slot_ids, group_latents, slot_embed, merge_latents, query, key, value)
 
 
-def attend_one(blocks, pack):
-    both = dot(blocks, pack, ((1,), (0,)))
-    scores = both[:, :-HEAD] * SCALE
-    values = both[:, -HEAD:].astype(BF16)
-    top = jnp.max(scores, axis=0, keepdims=True)
-    weights = jnp.exp(scores - top)
-    total = jnp.sum(weights, axis=0, keepdims=True)
-    mixed = dot(values, weights.astype(BF16), ((0,), (0,))) / total
-    level = top + jnp.log(total)
-    high = level.astype(BF16).astype(F32)
-    middle = (level - high).astype(BF16).astype(F32)
-    low = level - high - middle
-    line = lax.broadcasted_iota(jnp.int32, (TAIL, mixed.shape[1]), 0)
-    tail = jnp.where(line == 0, high, jnp.where(line == 1, middle, jnp.where(line == 2, low, 0.0)))
-    return jnp.concatenate([mixed, tail], axis=0).astype(BF16)
-
-
-def attend_kernel(count, *refs):
-    given, (out_ref, blocks_ref, packs_ref, sems) = refs[:-4], refs[-4:]
-    size = given[0].shape[0]
-    copies = []
-    for k, ref in enumerate(given):
-        target = blocks_ref.at[pl.ds(k * size, size)] if k < count else packs_ref.at[k - count]
-        copies.append(pltpu.make_async_copy(ref, target, sems.at[k]))
-        copies[-1].start()
-    for copy in copies[:count]:
-        copy.wait()
+def attend_blocks(blocks, pack):
+    both = [dot(block[...], pack, ((1,), (0,))) for block in blocks]
+    scores = jnp.concatenate([b[:, :-HEAD] for b in both], axis=0) * SCALE
+    values = jnp.concatenate([b[:, -HEAD:].astype(BF16) for b in both], axis=0)
+    return scores, values
+
+
+def early_kernel(count, *refs):
+    blocks, packs, (mixed_ref, state_ref) = refs[:count], refs[count:-2], refs[-2:]
+    for k, pack_ref in enumerate(packs):
+        scores, values = attend_blocks(blocks, pack_ref[...])
+        top = jnp.max(scores, axis=0, keepdims=True)
+        weights = jnp.exp(scores - top)
+        state_ref[k, :8, :] = jnp.broadcast_to(top, (8, top.shape[1]))
+        state_ref[k, 8:, :] = jnp.broadcast_to(
+            jnp.sum(weights, axis=0, keepdims=True), (8, top.shape[1])
+        )
+        mixed_ref[k] = dot(values, weights.astype(BF16), ((0,), (0,)))
+
+
+def late_kernel(count, *refs):
+    blocks, packs = refs[:count], refs[count:-3]
+    mixed_ref, state_ref, out_ref = refs[-3:]
     mine = lax.axis_index("x")
-    for k, copy in enumerate(copies[count:]):
-        copy.wait()
-        out_ref[mine ^ k] = attend_one(blocks_ref[...], packs_ref[k])
-
-
-def attend_part(blocks, packs):
+    for k, pack_ref in enumerate(packs):
+        scores, values = attend_blocks(blocks, pack_ref[...])
+        before = state_ref[k, :1, :]
+        top = jnp.maximum(jnp.max(scores, axis=0, keepdims=True), before)
+        weights = jnp.exp(scores - top)
+        kept = jnp.exp(before - top)
+        total = jnp.sum(weights, axis=0, keepdims=True) + state_ref[k, 8:9, :] * kept
+        mixed = dot(values, weights.astype(BF16), ((0,), (0,))) + mixed_ref[k] * kept
+        mixed = mixed / total
+        level = top + jnp.log(total)
+        high = level.astype(BF16).astype(F32)
+        middle = (level - high).astype(BF16).astype(F32)
+        low = level - high - middle
+        line = lax.broadcasted_iota(jnp.int32, (TAIL, mixed.shape[1]), 0)
+        tail = jnp.where(
+            line == 0, high, jnp.where(line == 1, middle, jnp.where(line == 2, low, 0.0))
+        )
+        out_ref[mine ^ k] = jnp.concatenate([mixed, tail], axis=0).astype(BF16)
+
+
+def attend_cost(blocks, packs):
+    keys = len(blocks) * blocks[0].shape[0]
+    flops = 2 * len(packs) * keys * packs[0].size + 2 * len(packs) * keys * HEAD * HEAD
+    return cost(flops, 3 * 2**20)
+
+
+def attend_early(blocks, packs):
     many, length = len(packs), packs[0].shape[1] - HEAD
-    count = len(blocks)
-    keys = count * blocks[0].shape[0]
-    flops = 2 * many * keys * (blocks[0].shape[1] * 2 * HEAD + HEAD * length)
-    return pl.pallas_call(
-        functools.partial(attend_kernel, count),
+    return pl.pallas_call(
+        functools.partial(early_kernel, len(blocks)),
+        out_shape=[
+            jax.ShapeDtypeStruct((many, HEAD, length), F32),
+            jax.ShapeDtypeStruct((many, 16, length), F32),
+        ],
+        in_specs=[VMEM] * (len(blocks) + many),
+        out_specs=[VMEM, VMEM],
+        compiler_params=WIDE,
+        cost_estimate=attend_cost(blocks, packs),
+        name="attend_early",
+    )(*blocks, *packs)
+
+
+def attend_late(blocks, packs, mixed, state):
+    many, length = len(packs), packs[0].shape[1] - HEAD
+    return pl.pallas_call(
+        functools.partial(late_kernel, len(blocks)),
         out_shape=jax.ShapeDtypeStruct((many, HEAD + TAIL, length), BF16),
-        in_specs=[pl.BlockSpec(memory_space=pl.ANY)] * (count + many),
+        in_specs=[VMEM] * (len(blocks) + many + 2),
         out_specs=VMEM,
-        scratch_shapes=[
-            pltpu.VMEM((keys, blocks[0].shape[1]), BF16),
-            pltpu.VMEM((many, *packs[0].shape), BF16),
-            pltpu.SemaphoreType.DMA((count + many,)),
-        ],
         compiler_params=WIDE,
-        cost_estimate=cost(flops, 3 * 2**20),
-        name="attend_part",
-    )(*blocks, *packs)
+        cost_estimate=attend_cost(blocks, packs),
+        name="attend_late",
+    )(*blocks, *packs, mixed, state)
 
 
 def pair_kernel(parts_ref, key_ref, value_ref, out_ref):
@@ -249,22 +274,20 @@
     )
     pack_two = partner(pack, "x", 2)
     keyed_three = partner(keyed, "z", 3)
-    outer_block = all_from(global_latents, INNER)
+    outer_block = all_from(global_latents, ("c", *INNER))
     pack_three = partner(pack, "x", 3)
     keyed_two = partner(keyed, "z", 2)
     pack_one = partner(pack, "x", 1)
     keyed_one = partner(keyed, "z", 1)
-    parts = attend_part(
-        [keyed, keyed_one, keyed_two, keyed_three],
-        [pack, pack_one, pack_two, pack_three],
-    )
+    packs = [pack, pack_one, pack_two, pack_three]
+    mixed, state = attend_early([keyed, keyed_three], packs)
+    parts = attend_late([keyed_two, keyed_one], packs, mixed, state)
     parts = exchange(parts, "x")
 
     pairs = decode_pairs(outer_block, decode_key, decode_value)
     for axis, step_size in (("h", 1), ("h", 3), ("y", 1), ("y", 3)):
         if lax.axis_size(axis) > step_size:
             pairs = jnp.concatenate([pairs, partner(pairs, axis, step_size)], axis=0)
-    other = partner(pairs, "c", 1)
 
     partial = join_and_project(parts, output_weight)
     arrived = exchange(partial.reshape(inner, rows, width), INNER)
@@ -272,7 +295,6 @@
     normed = exchange(copies, INNER).reshape(length, width)
 
     query_five = dot(normed, decode_query, ((1,), (0,))).astype(BF16)
-    pairs = jnp.concatenate([pairs, other], axis=0)
     scores = dot(pairs[:, :HEAD], query_five, ((1,), (1,))) * SCALE
     top = jnp.max(scores, axis=0, keepdims=True)
     weights = jnp.exp(scores - top)

time: 167 us -> 170 us (1.018)
  starting transfers between devices: 55.8 us -> 66.9 us
  blocking collectives: 55.7 us -> 49 us
  waiting for transfers between devices: 38 us -> 34.8 us
  Pallas kernels: 11.1 us -> 13.2 us
    ppermute x11 -> x10, starting transfers between devices: 47.7 us -> 58.5 us  [partner(): return lax.ppermute(value, axis, pairs)]
    all_to_all x3, blocking collectives: 55.7 us -> 49 us  [exchange(): return lax.all_to_all(tiles, axis, split_axis=0, concat_axis=0, tiled=True)]
    ppermute x11 -> x10, waiting for transfers between devices: 30.9 us -> 25 us  [partner(): return lax.ppermute(value, axis, pairs)]
    all_to_all x2, waiting for transfers between devices: 7.11 us -> 9.73 us  [exchange(): return lax.all_to_all(tiles, axis, split_axis=0, concat_axis=0, tiled=True)]
    pallas_call x1 -> x2, Pallas kernels: 5.81 us -> 7.85 us  [the longest x1 3.95 us: attend_late(): pl.pallas_call(functools.partial(late_kernel, len(blocks)), out_shape=jax...]
  transfers between devices with their start and end apart: 13 -> 12, of which waited for: 8 -> 7; matrix products, arithmetic and copies ran while one was open for 1% -> 0% of each run, Pallas kernels for 1% -> 3%
where the time goes in v6:
time: 170 us; the launch traced here: 169 us
  starting transfers between devices  66.9 us (39%)
  blocking collectives  49 us (29%)
  waiting for transfers between devices  34.8 us (20%)
  Pallas kernels  13.2 us (8%)
  local copies, waits for them, and re-layouts  2.6 us (2%)
    ppermute x10, starting transfers between devices, partner(): return lax.ppermute(value, axis, pairs)  58.5 us
    all_to_all x3, blocking collectives, exchange(): return lax.all_to_all(tiles, axis, split_axis=0, concat_axis=0, tiled=True)  49 us
    ppermute x10, waiting for transfers between devices, partner(): return lax.ppermute(value, axis, pairs)  25 us
    all_to_all x2, waiting for transfers between devices, exchange(): return lax.all_to_all(tiles, axis, split_axis=0, concat_axis=0, tiled=True)  9.73 us
    all_to_all x2, starting transfers between devices, exchange(): return lax.all_to_all(tiles, axis, split_axis=0, concat_axis=0, tiled=True)  8.43 us
    pallas_call x1, Pallas kernels, attend_late(): pl.pallas_call(functools.partial(late_kernel, len(blocks)), out_shape=jax...  3.95 us
    pallas_call x1, Pallas kernels, attend_early(): pl.pallas_call(functools.partial(early_kernel, len(blocks)), out_shape=[j...  3.9 us
  transfers between devices with their start and end apart: 12, of which 7 were waited for; matrix products, arithmetic and copies ran while one was open for 0% of the time, Pallas kernels for 3%

profile of v6, /device:TPU:24, one launch (start us, length us, event | category | flops | bytes accessed | tf_op | source)
XLA Modules:
  0.0 168.8 jit_solution(7622693527147970326)
XLA Ops:
  0.7 2.9 %prepare.1 = (bf16[128,1024]{1,0:T(8,128)(2,1)}, bf16[1024,256]{1,0:T(8,128)(2,1)}) custom-call(s32[1,1]{1,0:T(1,128)S(6)} %copy.18.slot_ref, bf16[128,1024]{1,0:T(8,128)(2,1)} %group_ref.1, bf16[16,1024]{1,0:T(8,128)(2,1)} %embed_ref.1, bf16[128,2048]{1,0:T(8,128)(2,1)} %merge_ref.1, bf16[2048,128]{1,0:T(8,128)(2,1)} %query_ref.1, ...), custom_call_target="tpu_custom_call" | custom-call | flops 134217728 | bytes 1048576 | tf_op jit(solution)/shard_map/prepare/pallas_call | solution.py:65
  3.6 3.4 %collective-permute-start.6 = (bf16[1024,256]{1,0:T(8,128)(2,1)}, bf16[1024,256]{1,0:T(8,128)(2,1)S(1)}, u32[]{:S(2)}, u32[]{:S(2)}) collective-permute-start(bf16[1024,256]{1,0:T(8,128)(2,1)} %get-tuple-element.12.refs_2_), channel_id=1, source_target_pairs={{0,1},{1,0},{2,3},{3,2},{4,5},{5,4},{6,7},{7,6},{8,9},{9,8},{10,11... | collective-permute-start | bytes 1572872 | tf_op jit(solution)/shard_map/ppermute | solution.py:34
  7.0 4.6 %collective-permute-start.7 = (bf16[1024,256]{1,0:T(8,128)(2,1)}, bf16[1024,256]{1,0:T(8,128)(2,1)S(1)}, u32[]{:S(2)}, u32[]{:S(2)}) collective-permute-start(bf16[1024,256]{1,0:T(8,128)(2,1)} %get-tuple-element.12.refs_2_), channel_id=1, source_target_pairs={{0,2},{1,3},{2,0},{3,1},{4,6},{5,7},{6,4},{7,5},{8,10},{9,11},{10,... | collective-permute-start | bytes 1572872 | tf_op jit(solution)/shard_map/ppermute | solution.py:34
  11.6 2.4 %collective-permute-start.8 = (bf16[1024,256]{1,0:T(8,128)(2,1)}, bf16[1024,256]{1,0:T(8,128)(2,1)}, u32[]{:S(2)}, u32[]{:S(2)}) collective-permute-start(bf16[1024,256]{1,0:T(8,128)(2,1)} %get-tuple-element.12.refs_2_), channel_id=1, source_target_pairs={{0,3},{1,2},{2,1},{3,0},{4,7},{5,6},{6,5},{7,4},{8,11},{9,10},{10,... | collective-permute-start | bytes 1572872 | tf_op jit(solution)/shard_map/ppermute | solution.py:34
  14.0 6.5 %collective-permute-start.9 = (bf16[128,1024]{1,0:T(8,128)(2,1)}, bf16[128,1024]{1,0:T(8,128)(2,1)S(1)}, u32[]{:S(2)}, u32[]{:S(2)}) collective-permute-start(bf16[128,1024]{1,0:T(8,128)(2,1)} %get-tuple-element.11.refs_0_), channel_id=1, source_target_pairs={{0,12},{4,8},{8,4},{12,0},{1,13},{5,9},{9,5},{13,1},{2,14},{6,10},... | collective-permute-start | bytes 786440 | tf_op jit(solution)/shard_map/ppermute | solution.py:34
  20.5 1.9 %collective-permute-start.4 = (bf16[128,1024]{1,0:T(8,128)(2,1)}, bf16[128,1024]{1,0:T(8,128)(2,1)S(1)}, u32[]{:S(2)}, u32[]{:S(2)}) collective-permute-start(bf16[128,1024]{1,0:T(8,128)(2,1)} %get-tuple-element.11.refs_0_), channel_id=1, source_target_pairs={{0,8},{4,12},{8,0},{12,4},{1,9},{5,13},{9,1},{13,5},{2,10},{6,14},... | collective-permute-start | bytes 786440 | tf_op jit(solution)/shard_map/ppermute | solution.py:34
  22.5 5.5 %collective-permute-done.9.refs_1_ = bf16[128,1024]{1,0:T(8,128)(2,1)S(1)} collective-permute-done((bf16[128,1024]{1,0:T(8,128)(2,1)}, bf16[128,1024]{1,0:T(8,128)(2,1)S(1)}, u32[]{:S(2)}, u32[]{:S(2)}) %collective-permute-start.9) | collective-permute-done | bytes 262176 | tf_op jit(solution)/shard_map/ppermute | solution.py:34
  28.0 12.0 %collective-permute-start.5 = (bf16[128,1024]{1,0:T(8,128)(2,1)}, bf16[128,1024]{1,0:T(8,128)(2,1)}, u32[]{:S(2)}, u32[]{:S(2)}) collective-permute-start(bf16[128,1024]{1,0:T(8,128)(2,1)} %get-tuple-element.11.refs_0_), channel_id=1, source_target_pairs={{0,4},{4,0},{8,12},{12,8},{1,5},{5,1},{9,13},{13,9},{2,6},{6,2},{1... | collective-permute-start | bytes 786440 | tf_op jit(solution)/shard_map/ppermute | solution.py:34
  40.1 0.7 copy-done.4
  41.0 3.9 %attend_early.1 = (f32[4,128,128]{2,1,0:T(8,128)}, f32[4,16,128]{2,1,0:T(8,128)}) custom-call(bf16[128,1024]{1,0:T(8,128)(2,1)} %get-tuple-element.11.refs_0_, bf16[128,1024]{1,0:T(8,128)(2,1)} %copy-done.8, bf16[1024,256]{1,0:T(8,128)(2,1)} %get-tuple-element.12.refs_2_, bf16[1024,256]{1,0:T(8,128)(2,1)} %copy-done.4, bf16[1024,256]{1,0:T(8,128)(2,1)} %copy-done.5, ...), custom_call_target="tpu_custom_call" | custom-call | flops 570425344 | bytes 3145728 | tf_op jit(solution)/shard_map/attend_early/pallas_call | solution.py:131
  44.9 2.5 %collective-permute-done.5.refs_1_ = bf16[128,1024]{1,0:T(8,128)(2,1)} collective-permute-done((bf16[128,1024]{1,0:T(8,128)(2,1)}, bf16[128,1024]{1,0:T(8,128)(2,1)}, u32[]{:S(2)}, u32[]{:S(2)}) %collective-permute-start.5) | collective-permute-done | bytes 262176 | tf_op jit(solution)/shard_map/ppermute | solution.py:34
  47.4 4.0 %attend_late.1 = bf16[4,144,128]{2,1,0:T(8,128)(2,1)} custom-call(bf16[128,1024]{1,0:T(8,128)(2,1)} %copy-done.7, bf16[128,1024]{1,0:T(8,128)(2,1)} %collective-permute-done.5.refs_1_, bf16[1024,256]{1,0:T(8,128)(2,1)} %get-tuple-element.12.refs_2_, bf16[1024,256]{1,0:T(8,128)(2,1)} %copy-done.4, bf16[1024,256]{1,0:T(8,128)(2,1)} %copy-done.5, ...), custom_call_target="tpu_custom_call" | custom-call | flops 570425344 | bytes 3145728 | tf_op jit(solution)/shard_map/attend_late/pallas_call | solution.py:147
  51.4 10.1 %all_to_all.25.parts_ref = bf16[4,144,128]{2,1,0:T(8,128)(2,1)S(1)} all-to-all(bf16[4,144,128]{2,1,0:T(8,128)(2,1)} %attend_late.1), channel_id=1, replica_groups=mesh['y'=4,'h'=4,'c'=2,'z'=4,'x'=4] {'x'}, dimensions={0} | all-to-all | bytes 294912 | tf_op jit(solution)/shard_map/all_to_all | solution.py:38
  61.9 18.0 %all_to_all.26.parts_ref = bf16[16,8,2048]{2,1,0:T(8,128)(2,1)S(1)} all-to-all(bf16[16,8,2048]{2,1,0:T(8,128)(2,1)S(1)} %bitcast.11), channel_id=1, replica_groups=mesh['y'=4,'h'=4,'c'=2,'z'=4,'x'=4] {'z','x'}, dimensions={0} | all-to-all | bytes 1048576 | tf_op jit(solution)/shard_map/all_to_all | solution.py:38
  79.9 0.8 broadcast_in_dim.2
  80.7 4.7 %all-to-all-start = ((bf16[32,2,2048]{2,1,0:T(2,128)(2,1)}), bf16[32,2,2048]{2,1,0:T(2,128)(2,1)S(1)}, u32[]{:S(2)}, u32[]{:S(2)}) async-start(bf16[32,2,2048]{2,1,0:T(2,128)(2,1)} %broadcast_in_dim.2), calls=%async_computation | async-start | bytes 524288 | tf_op jit(solution)/shard_map/all_to_all | solution.py:38
  85.4 0.8 constant_dynamic-slice_fusion.own_ref
  86.2 1.0 sum_and_norm.1
  87.2 9.7 %all-to-all-done.parts_ref = bf16[32,2,2048]{2,1,0:T(2,128)(2,1)S(1)} async-done(((bf16[32,2,2048]{2,1,0:T(2,128)(2,1)}), bf16[32,2,2048]{2,1,0:T(2,128)(2,1)S(1)}, u32[]{:S(2)}, u32[]{:S(2)}) %all-to-all-start) | async-done | bytes 262176 | tf_op jit(solution)/shard_map/all_to_all | solution.py:38
  97.0 3.7 %all-to-all-start.3 = ((bf16[16,8,2048]{2,1,0:T(8,128)(2,1)}), bf16[16,8,2048]{2,1,0:T(8,128)(2,1)S(1)}, u32[]{:S(2)}, u32[]{:S(2)}) async-start(bf16[16,8,2048]{2,1,0:T(8,128)(2,1)} %get-tuple-element.15), calls=%async_computation.3 | async-start | bytes 1048576 | tf_op jit(solution)/shard_map/all_to_all | solution.py:38
  101.1 9.1 %collective-permute-start = (bf16[64,256]{1,0:T(8,128)(2,1)S(1)}, bf16[64,256]{1,0:T(8,128)(2,1)S(1)}, u32[]{:S(2)}, u32[]{:S(2)}) collective-permute-start(bf16[64,256]{1,0:T(8,128)(2,1)S(1)} %decode_pairs.1), channel_id=1, source_target_pairs={{0,32},{32,0},{64,96},{96,64},{1,33},{33,1},{65,97},{97,65},{2,34}... | collective-permute-start | bytes 98312 | tf_op jit(solution)/shard_map/ppermute | solution.py:34
  110.2 2.0 %collective-permute-done = bf16[64,256]{1,0:T(8,128)(2,1)S(1)} collective-permute-done((bf16[64,256]{1,0:T(8,128)(2,1)S(1)}, bf16[64,256]{1,0:T(8,128)(2,1)S(1)}, u32[]{:S(2)}, u32[]{:S(2)}) %collective-permute-start) | collective-permute-done | bytes 32800 | tf_op jit(solution)/shard_map/ppermute | solution.py:34
  112.2 13.5 %collective-permute-start.1 = (bf16[128,256]{1,0:T(8,128)(2,1)S(1)}, bf16[128,256]{1,0:T(8,128)(2,1)S(1)}, u32[]{:S(2)}, u32[]{:S(2)}) collective-permute-start(bf16[128,256]{1,0:T(8,128)(2,1)S(1)} %pad_maximum_fusion.2), channel_id=1, source_target_pairs={{0,96},{32,64},{64,32},{96,0},{1,97},{33,65},{65,33},{97,1},{2,98}... | collective-permute-start | bytes 196616 | tf_op jit(solution)/shard_map/ppermute | solution.py:34
  125.7 3.5 %collective-permute-done.1 = bf16[128,256]{1,0:T(8,128)(2,1)S(1)} collective-permute-done((bf16[128,256]{1,0:T(8,128)(2,1)S(1)}, bf16[128,256]{1,0:T(8,128)(2,1)S(1)}, u32[]{:S(2)}, u32[]{:S(2)}) %collective-permute-start.1) | collective-permute-done | bytes 65568 | tf_op jit(solution)/shard_map/ppermute | solution.py:34
  129.3 2.7 %collective-permute-start.2 = (bf16[256,256]{1,0:T(8,128)(2,1)S(1)}, bf16[256,256]{1,0:T(8,128)(2,1)S(1)}, u32[]{:S(2)}, u32[]{:S(2)}) collective-permute-start(bf16[256,256]{1,0:T(8,128)(2,1)S(1)} %pad_maximum_fusion.1), channel_id=1, source_target_pairs={{0,128},{128,0},{256,384},{384,256},{1,129},{129,1},{257,385},{385... | collective-permute-start | bytes 393224 | tf_op jit(solution)/shard_map/ppermute | solution.py:34
  132.0 4.2 %collective-permute-done.2 = bf16[256,256]{1,0:T(8,128)(2,1)S(1)} collective-permute-done((bf16[256,256]{1,0:T(8,128)(2,1)S(1)}, bf16[256,256]{1,0:T(8,128)(2,1)S(1)}, u32[]{:S(2)}, u32[]{:S(2)}) %collective-permute-start.2) | collective-permute-done | bytes 131104 | tf_op jit(solution)/shard_map/ppermute | solution.py:34
  136.2 2.3 %collective-permute-start.3 = (bf16[512,256]{1,0:T(8,128)(2,1)S(1)}, bf16[512,256]{1,0:T(8,128)(2,1)S(1)}, u32[]{:S(2)}, u32[]{:S(2)}) collective-permute-start(bf16[512,256]{1,0:T(8,128)(2,1)S(1)} %pad_maximum_fusion), channel_id=1, source_target_pairs={{0,384},{128,256},{256,128},{384,0},{1,385},{129,257},{257,129},{3... | collective-permute-start | bytes 786440 | tf_op jit(solution)/shard_map/ppermute | solution.py:34
  138.5 7.3 %collective-permute-done.3 = bf16[512,256]{1,0:T(8,128)(2,1)S(1)} collective-permute-done((bf16[512,256]{1,0:T(8,128)(2,1)S(1)}, bf16[512,256]{1,0:T(8,128)(2,1)S(1)}, u32[]{:S(2)}, u32[]{:S(2)}) %collective-permute-start.3) | collective-permute-done | bytes 262176 | tf_op jit(solution)/shard_map/ppermute | solution.py:34
  145.8 0.6 fusion.14
  146.6 0.6 fusion
  147.2 21.0 %all_to_all.27.parts_ref = bf16[16,8,2048]{2,1,0:T(8,128)(2,1)S(1)} all-to-all(bf16[16,8,2048]{2,1,0:T(8,128)(2,1)S(1)} %fusion), channel_id=1, replica_groups=mesh['y'=4,'h'=4,'c'=2,'z'=4,'x'=4] {'z','x'}, dimensions={0} | all-to-all | bytes 1048576 | tf_op jit(solution)/shard_map/all_to_all | solution.py:38
  168.1 0.7 last_sum.1
  (35 shorter events, 1.2 us)
Async XLA Ops:
  0.0 146.6 %copy-start = (bf16[128,2048]{1,0:T(8,128)(2,1)S(1)}, bf16[128,2048]{1,0:T(8,128)(2,1)}, u32[]{:S(2)}) copy-start(bf16[128,2048]{1,0:T(8,128)(2,1)} %param.25) | copy-start | bytes 1572868
  3.6 36.4 %collective-permute-start.6 = (bf16[1024,256]{1,0:T(8,128)(2,1)}, bf16[1024,256]{1,0:T(8,128)(2,1)S(1)}, u32[]{:S(2)}, u32[]{:S(2)}) collective-permute-start(bf16[1024,256]{1,0:T(8,128)(2,1)} %get-tuple-element.12.refs_2_), channel_id=1, source_target_pairs={{0,1},{1,0},{2,3},{3,2},{4,5},{5,4},{6,7},{7,6},{8,9},{9,8},{10,11... | collective-permute-start | bytes 1572872 | tf_op jit(solution)/shard_map/ppermute | solution.py:34
  7.0 33.1 %collective-permute-start.7 = (bf16[1024,256]{1,0:T(8,128)(2,1)}, bf16[1024,256]{1,0:T(8,128)(2,1)S(1)}, u32[]{:S(2)}, u32[]{:S(2)}) collective-permute-start(bf16[1024,256]{1,0:T(8,128)(2,1)} %get-tuple-element.12.refs_2_), channel_id=1, source_target_pairs={{0,2},{1,3},{2,0},{3,1},{4,6},{5,7},{6,4},{7,5},{8,10},{9,11},{10,... | collective-permute-start | bytes 1572872 | tf_op jit(solution)/shard_map/ppermute | solution.py:34
  11.6 28.5 %collective-permute-start.8 = (bf16[1024,256]{1,0:T(8,128)(2,1)}, bf16[1024,256]{1,0:T(8,128)(2,1)}, u32[]{:S(2)}, u32[]{:S(2)}) collective-permute-start(bf16[1024,256]{1,0:T(8,128)(2,1)} %get-tuple-element.12.refs_2_), channel_id=1, source_target_pairs={{0,3},{1,2},{2,1},{3,0},{4,7},{5,6},{6,5},{7,4},{8,11},{9,10},{10,... | collective-permute-start | bytes 1572872 | tf_op jit(solution)/shard_map/ppermute | solution.py:34
  14.0 13.9 %collective-permute-start.9 = (bf16[128,1024]{1,0:T(8,128)(2,1)}, bf16[128,1024]{1,0:T(8,128)(2,1)S(1)}, u32[]{:S(2)}, u32[]{:S(2)}) collective-permute-start(bf16[128,1024]{1,0:T(8,128)(2,1)} %get-tuple-element.11.refs_0_), channel_id=1, source_target_pairs={{0,12},{4,8},{8,4},{12,0},{1,13},{5,9},{9,5},{13,1},{2,14},{6,10},... | collective-permute-start | bytes 786440 | tf_op jit(solution)/shard_map/ppermute | solution.py:34
  20.5 24.4 %collective-permute-start.4 = (bf16[128,1024]{1,0:T(8,128)(2,1)}, bf16[128,1024]{1,0:T(8,128)(2,1)S(1)}, u32[]{:S(2)}, u32[]{:S(2)}) collective-permute-start(bf16[128,1024]{1,0:T(8,128)(2,1)} %get-tuple-element.11.refs_0_), channel_id=1, source_target_pairs={{0,8},{4,12},{8,0},{12,4},{1,9},{5,13},{9,1},{13,5},{2,10},{6,14},... | collective-permute-start | bytes 786440 | tf_op jit(solution)/shard_map/ppermute | solution.py:34
  28.0 12.1 %copy-start.8 = (bf16[128,1024]{1,0:T(8,128)(2,1)}, bf16[128,1024]{1,0:T(8,128)(2,1)S(1)}, u32[]{:S(2)}) copy-start(bf16[128,1024]{1,0:T(8,128)(2,1)S(1)} %collective-permute-done.9.refs_1_) | copy-start | bytes 786436
  28.0 19.5 %collective-permute-start.5 = (bf16[128,1024]{1,0:T(8,128)(2,1)}, bf16[128,1024]{1,0:T(8,128)(2,1)}, u32[]{:S(2)}, u32[]{:S(2)}) collective-permute-start(bf16[128,1024]{1,0:T(8,128)(2,1)} %get-tuple-element.11.refs_0_), channel_id=1, source_target_pairs={{0,4},{4,0},{8,12},{12,8},{1,5},{5,1},{9,13},{13,9},{2,6},{6,2},{1... | collective-permute-start | bytes 786440 | tf_op jit(solution)/shard_map/ppermute | solution.py:34
  40.0 0.8 copy-start.4
  40.0 0.9 copy-start.5
  44.9 2.5 %copy-start.7 = (bf16[128,1024]{1,0:T(8,128)(2,1)}, bf16[128,1024]{1,0:T(8,128)(2,1)S(1)}, u32[]{:S(2)}) copy-start(bf16[128,1024]{1,0:T(8,128)(2,1)S(1)} %collective-permute-done.4.refs_0_) | copy-start | bytes 786436
  47.4 14.1 %copy-start.1 = (bf16[128,2048]{1,0:T(8,128)(2,1)S(1)}, bf16[128,2048]{1,0:T(8,128)(2,1)}, u32[]{:S(2)}) copy-start(bf16[128,2048]{1,0:T(8,128)(2,1)} %weight_ref.1) | copy-start | bytes 1572868
  61.8 18.0 %copy-start.9 = (bf16[2,2048]{1,0:T(2,128)(2,1)S(1)}, bf16[2,2048]{1,0:T(2,128)(2,1)}, u32[]{:S(2)}) copy-start(bf16[2,2048]{1,0:T(2,128)(2,1)} %param.21) | copy-start | bytes 24580
  80.7 16.3 %all-to-all-start = ((bf16[32,2,2048]{2,1,0:T(2,128)(2,1)}), bf16[32,2,2048]{2,1,0:T(2,128)(2,1)S(1)}, u32[]{:S(2)}, u32[]{:S(2)}) async-start(bf16[32,2,2048]{2,1,0:T(2,128)(2,1)} %broadcast_in_dim.2), calls=%async_computation | async-start | bytes 524288 | tf_op jit(solution)/shard_map/all_to_all | solution.py:38
  97.0 3.7 %copy-start.2 = (bf16[2048,128]{1,0:T(8,128)(2,1)S(1)}, bf16[2048,128]{1,0:T(8,128)(2,1)}, u32[]{:S(2)}) copy-start(bf16[2048,128]{1,0:T(8,128)(2,1)} %key_ref.2) | copy-start | bytes 1572868
  97.0 3.7 %copy-start.3 = (bf16[2048,128]{1,0:T(8,128)(2,1)S(1)}, bf16[2048,128]{1,0:T(8,128)(2,1)}, u32[]{:S(2)}) copy-start(bf16[2048,128]{1,0:T(8,128)(2,1)} %value_ref.2) | copy-start | bytes 1572868
  97.0 48.8 %all-to-all-start.3 = ((bf16[16,8,2048]{2,1,0:T(8,128)(2,1)}), bf16[16,8,2048]{2,1,0:T(8,128)(2,1)S(1)}, u32[]{:S(2)}, u32[]{:S(2)}) async-start(bf16[16,8,2048]{2,1,0:T(8,128)(2,1)} %get-tuple-element.15), calls=%async_computation.3 | async-start | bytes 1048576 | tf_op jit(solution)/shard_map/all_to_all | solution.py:38
  101.1 11.1 %collective-permute-start = (bf16[64,256]{1,0:T(8,128)(2,1)S(1)}, bf16[64,256]{1,0:T(8,128)(2,1)S(1)}, u32[]{:S(2)}, u32[]{:S(2)}) collective-permute-start(bf16[64,256]{1,0:T(8,128)(2,1)S(1)} %decode_pairs.1), channel_id=1, source_target_pairs={{0,32},{32,0},{64,96},{96,64},{1,33},{33,1},{65,97},{97,65},{2,34}... | collective-permute-start | bytes 98312 | tf_op jit(solution)/shard_map/ppermute | solution.py:34
  112.2 17.1 %collective-permute-start.1 = (bf16[128,256]{1,0:T(8,128)(2,1)S(1)}, bf16[128,256]{1,0:T(8,128)(2,1)S(1)}, u32[]{:S(2)}, u32[]{:S(2)}) collective-permute-start(bf16[128,256]{1,0:T(8,128)(2,1)S(1)} %pad_maximum_fusion.2), channel_id=1, source_target_pairs={{0,96},{32,64},{64,32},{96,0},{1,97},{33,65},{65,33},{97,1},{2,98}... | collective-permute-start | bytes 196616 | tf_op jit(solution)/shard_map/ppermute | solution.py:34
  129.3 6.9 %collective-permute-start.2 = (bf16[256,256]{1,0:T(8,128)(2,1)S(1)}, bf16[256,256]{1,0:T(8,128)(2,1)S(1)}, u32[]{:S(2)}, u32[]{:S(2)}) collective-permute-start(bf16[256,256]{1,0:T(8,128)(2,1)S(1)} %pad_maximum_fusion.1), channel_id=1, source_target_pairs={{0,128},{128,0},{256,384},{384,256},{1,129},{129,1},{257,385},{385... | collective-permute-start | bytes 393224 | tf_op jit(solution)/shard_map/ppermute | solution.py:34
  136.2 9.7 %copy-start.6 = (bf16[2048,128]{1,0:T(8,128)(2,1)S(1)}, bf16[2048,128]{1,0:T(8,128)(2,1)}, u32[]{:S(2)}) copy-start(bf16[2048,128]{1,0:T(8,128)(2,1)} %param.22) | copy-start | bytes 1572868
  136.2 9.6 %collective-permute-start.3 = (bf16[512,256]{1,0:T(8,128)(2,1)S(1)}, bf16[512,256]{1,0:T(8,128)(2,1)S(1)}, u32[]{:S(2)}, u32[]{:S(2)}) collective-permute-start(bf16[512,256]{1,0:T(8,128)(2,1)S(1)} %pad_maximum_fusion), channel_id=1, source_target_pairs={{0,384},{128,256},{256,128},{384,0},{1,385},{129,257},{257,129},{3... | collective-permute-start | bytes 786440 | tf_op jit(solution)/shard_map/ppermute | solution.py:34

commit v7 on v5

--- a/solution.py
+++ b/solution.py
@@ -18,6 +18,7 @@
 F32 = jnp.float32
 SCALE = HEAD ** (-0.5)
 TAIL = 16
+ROWS = 256
 PARAMS = pltpu.CompilerParams(vmem_limit_bytes=20 * 2**20)
 WIDE = pltpu.CompilerParams(vmem_limit_bytes=62 * 2**20)
 
@@ -76,10 +77,13 @@
     )(slot_ids, group_latents, slot_embed, merge_latents, query, key, value)
 
 
-def attend_one(blocks, pack):
-    both = dot(blocks, pack, ((1,), (0,)))
-    scores = both[:, :-HEAD] * SCALE
-    values = both[:, -HEAD:].astype(BF16)
+def attend_one(blocks_ref, pack):
+    both = [
+        dot(blocks_ref[pl.ds(k, ROWS)], pack, ((1,), (0,)))
+        for k in range(0, blocks_ref.shape[0], ROWS)
+    ]
+    scores = jnp.concatenate([b[:, :-HEAD] for b in both], axis=0) * SCALE
+    values = jnp.concatenate([b[:, -HEAD:].astype(BF16) for b in both], axis=0)
     top = jnp.max(scores, axis=0, keepdims=True)
     weights = jnp.exp(scores - top)
     total = jnp.sum(weights, axis=0, keepdims=True)
@@ -106,7 +110,7 @@
     mine = lax.axis_index("x")
     for k, copy in enumerate(copies[count:]):
         copy.wait()
-        out_ref[mine ^ k] = attend_one(blocks_ref[...], packs_ref[k])
+        out_ref[mine ^ k] = attend_one(blocks_ref, packs_ref[k])
 
 
 def attend_part(blocks, packs):
@@ -124,7 +128,7 @@
             pltpu.VMEM((many, *packs[0].shape), BF16),
             pltpu.SemaphoreType.DMA((count + many,)),
         ],
-        compiler_params=WIDE,
+        compiler_params=PARAMS,
         cost_estimate=cost(flops, 3 * 2**20),
         name="attend_part",
     )(*blocks, *packs)

time: 167 us -> 164 us (0.982)
  Pallas kernels: 11.1 us -> 8.17 us
    pallas_call x1, Pallas kernels: 5.81 us -> 2.96 us  [attend_part(): pl.pallas_call(functools.partial(attend_kernel, count), out_shape=jax.Sha...]
where the time goes in v7:
time: 164 us
  starting transfers between devices  55.8 us (34%)
  blocking collectives  54.1 us (33%)
  waiting for transfers between devices  39.5 us (24%)
  Pallas kernels  8.17 us (5%)
  local copies, waits for them, and re-layouts  3.57 us (2%)
    all_to_all x3, blocking collectives, exchange(): return lax.all_to_all(tiles, axis, split_axis=0, concat_axis=0, tiled=True)  54.1 us
    ppermute x11, starting transfers between devices, partner(): return lax.ppermute(value, axis, pairs)  47.7 us
    ppermute x11, waiting for transfers between devices, partner(): return lax.ppermute(value, axis, pairs)  32.4 us
    all_to_all x2, starting transfers between devices, exchange(): return lax.all_to_all(tiles, axis, split_axis=0, concat_axis=0, tiled=True)  8.15 us
    all_to_all x2, waiting for transfers between devices, exchange(): return lax.all_to_all(tiles, axis, split_axis=0, concat_axis=0, tiled=True)  7.12 us
  transfers between devices with their start and end apart: 13, of which 8 were waited for; matrix products, arithmetic and copies ran while one was open for 1% of the time, Pallas kernels for 1%

profile of v7, /device:TPU:24, one launch (start us, length us, event | category | flops | bytes accessed | tf_op | source)
XLA Modules:
  0.0 163.5 jit_solution(2646785563434514729)
XLA Ops:
  0.7 2.9 %prepare.1 = (bf16[128,1024]{1,0:T(8,128)(2,1)}, bf16[1024,256]{1,0:T(8,128)(2,1)}) custom-call(s32[1,1]{1,0:T(1,128)S(6)} %copy.23.slot_ref, bf16[128,1024]{1,0:T(8,128)(2,1)} %group_ref.1, bf16[16,1024]{1,0:T(8,128)(2,1)} %embed_ref.1, bf16[128,2048]{1,0:T(8,128)(2,1)} %merge_ref.1, bf16[2048,128]{1,0:T(8,128)(2,1)} %query_ref.1, ...), custom_call_target="tpu_custom_call" | custom-call | flops 134217728 | bytes 1048576 | tf_op jit(solution)/shard_map/prepare/pallas_call | solution.py:66
  3.6 3.8 %collective-permute-start.5 = (bf16[128,1024]{1,0:T(8,128)(2,1)}, bf16[128,1024]{1,0:T(8,128)(2,1)S(1)}, u32[]{:S(2)}, u32[]{:S(2)}) collective-permute-start(bf16[128,1024]{1,0:T(8,128)(2,1)} %get-tuple-element.9.refs_0_), channel_id=1, source_target_pairs={{0,4},{4,0},{8,12},{12,8},{1,5},{5,1},{9,13},{13,9},{2,6},{6,2},{1... | collective-permute-start | bytes 786440 | tf_op jit(solution)/shard_map/ppermute | solution.py:35
  7.4 3.4 %collective-permute-start.8 = (bf16[1024,256]{1,0:T(8,128)(2,1)}, bf16[1024,256]{1,0:T(8,128)(2,1)S(1)}, u32[]{:S(2)}, u32[]{:S(2)}) collective-permute-start(bf16[1024,256]{1,0:T(8,128)(2,1)} %get-tuple-element.10.refs_4_), channel_id=1, source_target_pairs={{0,1},{1,0},{2,3},{3,2},{4,5},{5,4},{6,7},{7,6},{8,9},{9,8},{10,11... | collective-permute-start | bytes 1572872 | tf_op jit(solution)/shard_map/ppermute | solution.py:35
  10.8 4.6 %collective-permute-start.9 = (bf16[1024,256]{1,0:T(8,128)(2,1)}, bf16[1024,256]{1,0:T(8,128)(2,1)S(1)}, u32[]{:S(2)}, u32[]{:S(2)}) collective-permute-start(bf16[1024,256]{1,0:T(8,128)(2,1)} %get-tuple-element.10.refs_4_), channel_id=1, source_target_pairs={{0,2},{1,3},{2,0},{3,1},{4,6},{5,7},{6,4},{7,5},{8,10},{9,11},{10,... | collective-permute-start | bytes 1572872 | tf_op jit(solution)/shard_map/ppermute | solution.py:35
  15.4 2.4 %collective-permute-start.10 = (bf16[1024,256]{1,0:T(8,128)(2,1)}, bf16[1024,256]{1,0:T(8,128)(2,1)S(1)}, u32[]{:S(2)}, u32[]{:S(2)}) collective-permute-start(bf16[1024,256]{1,0:T(8,128)(2,1)} %get-tuple-element.10.refs_4_), channel_id=1, source_target_pairs={{0,3},{1,2},{2,1},{3,0},{4,7},{5,6},{6,5},{7,4},{8,11},{9,10},{10,... | collective-permute-start | bytes 1572872 | tf_op jit(solution)/shard_map/ppermute | solution.py:35
  17.8 5.2 %collective-permute-start.6 = (bf16[128,1024]{1,0:T(8,128)(2,1)}, bf16[128,1024]{1,0:T(8,128)(2,1)S(1)}, u32[]{:S(2)}, u32[]{:S(2)}) collective-permute-start(bf16[128,1024]{1,0:T(8,128)(2,1)} %get-tuple-element.9.refs_0_), channel_id=1, source_target_pairs={{0,8},{4,12},{8,0},{12,4},{1,9},{5,13},{9,1},{13,5},{2,10},{6,14},... | collective-permute-start | bytes 786440 | tf_op jit(solution)/shard_map/ppermute | solution.py:35
  23.0 1.9 %collective-permute-start.7 = (bf16[128,1024]{1,0:T(8,128)(2,1)}, bf16[128,1024]{1,0:T(8,128)(2,1)S(1)}, u32[]{:S(2)}, u32[]{:S(2)}) collective-permute-start(bf16[128,1024]{1,0:T(8,128)(2,1)} %get-tuple-element.9.refs_0_), channel_id=1, source_target_pairs={{0,12},{4,8},{8,4},{12,0},{1,13},{5,9},{9,5},{13,1},{2,14},{6,10},... | collective-permute-start | bytes 786440 | tf_op jit(solution)/shard_map/ppermute | solution.py:35
  25.0 14.5 %collective-permute-done.6.refs_2_ = bf16[128,1024]{1,0:T(8,128)(2,1)S(1)} collective-permute-done((bf16[128,1024]{1,0:T(8,128)(2,1)}, bf16[128,1024]{1,0:T(8,128)(2,1)S(1)}, u32[]{:S(2)}, u32[]{:S(2)}) %collective-permute-start.6) | collective-permute-done | bytes 262176 | tf_op jit(solution)/shard_map/ppermute | solution.py:35
  39.5 3.3 %collective-permute-done.10.refs_7_ = bf16[1024,256]{1,0:T(8,128)(2,1)S(1)} collective-permute-done((bf16[1024,256]{1,0:T(8,128)(2,1)}, bf16[1024,256]{1,0:T(8,128)(2,1)S(1)}, u32[]{:S(2)}, u32[]{:S(2)}) %collective-permute-start.10) | collective-permute-done | bytes 524320 | tf_op jit(solution)/shard_map/ppermute | solution.py:35
  42.8 1.0 copy-done.4
  43.9 0.9 copy-done.5
  44.8 3.0 %attend_part.1 = bf16[4,144,128]{2,1,0:T(8,128)(2,1)S(1)} custom-call(bf16[128,1024]{1,0:T(8,128)(2,1)S(1)} %copy-done.5, bf16[128,1024]{1,0:T(8,128)(2,1)S(1)} %collective-permute-done.5.refs_1_, bf16[128,1024]{1,0:T(8,128)(2,1)S(1)} %collective-permute-done.6.refs_2_, bf16[128,1024]{1,0:T(8,128)(2,1)S(1)} %collective-permute-done.7.refs_3_, ...), custom_call_target="tpu_custom_call" | custom-call | flops 1140850688 | bytes 3145728 | tf_op jit(solution)/shard_map/attend_part/pallas_call | solution.py:121
  47.8 8.4 %all_to_all.25.parts_ref = bf16[4,144,128]{2,1,0:T(8,128)(2,1)S(1)} all-to-all(bf16[4,144,128]{2,1,0:T(8,128)(2,1)S(1)} %attend_part.1), channel_id=1, replica_groups=mesh['y'=4,'h'=4,'c'=2,'z'=4,'x'=4] {'x'}, dimensions={0} | all-to-all | bytes 294912 | tf_op jit(solution)/shard_map/all_to_all | solution.py:39
  56.6 20.5 %all_to_all.26.parts_ref = bf16[16,8,2048]{2,1,0:T(8,128)(2,1)S(1)} all-to-all(bf16[16,8,2048]{2,1,0:T(8,128)(2,1)S(1)} %bitcast.11), channel_id=1, replica_groups=mesh['y'=4,'h'=4,'c'=2,'z'=4,'x'=4] {'z','x'}, dimensions={0} | all-to-all | bytes 1048576 | tf_op jit(solution)/shard_map/all_to_all | solution.py:39
  77.1 0.7 broadcast_in_dim.2
  77.8 4.4 %all-to-all-start = ((bf16[16,2,2048]{2,1,0:T(2,128)(2,1)}), bf16[16,2,2048]{2,1,0:T(2,128)(2,1)S(1)}, u32[]{:S(2)}, u32[]{:S(2)}) async-start(bf16[16,2,2048]{2,1,0:T(2,128)(2,1)} %broadcast_in_dim.2), calls=%async_computation | async-start | bytes 262144 | tf_op jit(solution)/shard_map/all_to_all | solution.py:39
  82.3 0.8 constant_dynamic-slice_fusion.own_ref
  83.0 1.0 sum_and_norm.1
  84.1 7.1 %all-to-all-done.parts_ref = bf16[16,2,2048]{2,1,0:T(2,128)(2,1)S(1)} async-done(((bf16[16,2,2048]{2,1,0:T(2,128)(2,1)}), bf16[16,2,2048]{2,1,0:T(2,128)(2,1)S(1)}, u32[]{:S(2)}, u32[]{:S(2)}) %all-to-all-start) | async-done | bytes 131104 | tf_op jit(solution)/shard_map/all_to_all | solution.py:39
  91.2 3.7 %all-to-all-start.3 = ((bf16[16,8,2048]{2,1,0:T(8,128)(2,1)}), bf16[16,8,2048]{2,1,0:T(8,128)(2,1)S(1)}, u32[]{:S(2)}, u32[]{:S(2)}) async-start(bf16[16,8,2048]{2,1,0:T(8,128)(2,1)} %get-tuple-element.11), calls=%async_computation.3 | async-start | bytes 1048576 | tf_op jit(solution)/shard_map/all_to_all | solution.py:39
  95.2 9.1 %collective-permute-start = (bf16[32,256]{1,0:T(8,128)(2,1)S(1)}, bf16[32,256]{1,0:T(8,128)(2,1)S(1)}, u32[]{:S(2)}, u32[]{:S(2)}) collective-permute-start(bf16[32,256]{1,0:T(8,128)(2,1)S(1)} %decode_pairs.1), channel_id=1, source_target_pairs={{0,32},{32,0},{64,96},{96,64},{1,33},{33,1},{65,97},{97,65},{2,34}... | collective-permute-start | bytes 49160 | tf_op jit(solution)/shard_map/ppermute | solution.py:35
  104.3 1.8 %collective-permute-done = bf16[32,256]{1,0:T(8,128)(2,1)S(1)} collective-permute-done((bf16[32,256]{1,0:T(8,128)(2,1)S(1)}, bf16[32,256]{1,0:T(8,128)(2,1)S(1)}, u32[]{:S(2)}, u32[]{:S(2)}) %collective-permute-start) | collective-permute-done | bytes 16416 | tf_op jit(solution)/shard_map/ppermute | solution.py:35
  106.1 10.6 %collective-permute-start.1 = (bf16[64,256]{1,0:T(8,128)(2,1)S(1)}, bf16[64,256]{1,0:T(8,128)(2,1)S(1)}, u32[]{:S(2)}, u32[]{:S(2)}) collective-permute-start(bf16[64,256]{1,0:T(8,128)(2,1)S(1)} %pad_maximum_fusion.2), channel_id=1, source_target_pairs={{0,96},{32,64},{64,32},{96,0},{1,97},{33,65},{65,33},{97,1},{2,98}... | collective-permute-start | bytes 98312 | tf_op jit(solution)/shard_map/ppermute | solution.py:35
  116.7 1.9 %collective-permute-done.1 = bf16[64,256]{1,0:T(8,128)(2,1)S(1)} collective-permute-done((bf16[64,256]{1,0:T(8,128)(2,1)S(1)}, bf16[64,256]{1,0:T(8,128)(2,1)S(1)}, u32[]{:S(2)}, u32[]{:S(2)}) %collective-permute-start.1) | collective-permute-done | bytes 32800 | tf_op jit(solution)/shard_map/ppermute | solution.py:35
  118.5 2.6 %collective-permute-start.2 = (bf16[128,256]{1,0:T(8,128)(2,1)S(1)}, bf16[128,256]{1,0:T(8,128)(2,1)S(1)}, u32[]{:S(2)}, u32[]{:S(2)}) collective-permute-start(bf16[128,256]{1,0:T(8,128)(2,1)S(1)} %pad_maximum_fusion.1), channel_id=1, source_target_pairs={{0,128},{128,0},{256,384},{384,256},{1,129},{129,1},{257,385},{385... | collective-permute-start | bytes 196616 | tf_op jit(solution)/shard_map/ppermute | solution.py:35
  121.2 3.5 %collective-permute-done.2 = bf16[128,256]{1,0:T(8,128)(2,1)S(1)} collective-permute-done((bf16[128,256]{1,0:T(8,128)(2,1)S(1)}, bf16[128,256]{1,0:T(8,128)(2,1)S(1)}, u32[]{:S(2)}, u32[]{:S(2)}) %collective-permute-start.2) | collective-permute-done | bytes 65568 | tf_op jit(solution)/shard_map/ppermute | solution.py:35
  124.7 2.1 %collective-permute-start.3 = (bf16[256,256]{1,0:T(8,128)(2,1)S(1)}, bf16[256,256]{1,0:T(8,128)(2,1)S(1)}, u32[]{:S(2)}, u32[]{:S(2)}) collective-permute-start(bf16[256,256]{1,0:T(8,128)(2,1)S(1)} %pad_maximum_fusion), channel_id=1, source_target_pairs={{0,384},{128,256},{256,128},{384,0},{1,385},{129,257},{257,129},{3... | collective-permute-start | bytes 393224 | tf_op jit(solution)/shard_map/ppermute | solution.py:35
  126.9 5.9 %collective-permute-done.3 = bf16[256,256]{1,0:T(8,128)(2,1)S(1)} collective-permute-done((bf16[256,256]{1,0:T(8,128)(2,1)S(1)}, bf16[256,256]{1,0:T(8,128)(2,1)S(1)}, u32[]{:S(2)}, u32[]{:S(2)}) %collective-permute-start.3) | collective-permute-done | bytes 131104 | tf_op jit(solution)/shard_map/ppermute | solution.py:35
  132.8 1.9 %collective-permute-start.4 = (bf16[512,256]{1,0:T(8,128)(2,1)S(1)}, bf16[512,256]{1,0:T(8,128)(2,1)S(1)}, u32[]{:S(2)}, u32[]{:S(2)}) collective-permute-start(bf16[512,256]{1,0:T(8,128)(2,1)S(1)} %get-tuple-element.13), channel_id=1, source_target_pairs={{0,16},{16,0},{1,17},{17,1},{2,18},{18,2},{3,19},{19,3},{4,20},{20... | collective-permute-start | bytes 786440 | tf_op jit(solution)/shard_map/ppermute | solution.py:35
  134.7 1.5 collective-permute-done.4
  137.6 25.2 %all_to_all.27.parts_ref = bf16[16,8,2048]{2,1,0:T(8,128)(2,1)S(1)} all-to-all(bf16[16,8,2048]{2,1,0:T(8,128)(2,1)S(1)} %fusion), channel_id=1, replica_groups=mesh['y'=4,'h'=4,'c'=2,'z'=4,'x'=4] {'z','x'}, dimensions={0} | all-to-all | bytes 1048576 | tf_op jit(solution)/shard_map/all_to_all | solution.py:39
  162.8 0.7 last_sum.1
  (33 shorter events, 2.1 us)
Async XLA Ops:
  0.0 137.0 %copy-start = (bf16[128,2048]{1,0:T(8,128)(2,1)S(1)}, bf16[128,2048]{1,0:T(8,128)(2,1)}, u32[]{:S(2)}) copy-start(bf16[128,2048]{1,0:T(8,128)(2,1)} %param.25) | copy-start | bytes 1572868
  3.6 19.5 %collective-permute-start.5 = (bf16[128,1024]{1,0:T(8,128)(2,1)}, bf16[128,1024]{1,0:T(8,128)(2,1)S(1)}, u32[]{:S(2)}, u32[]{:S(2)}) collective-permute-start(bf16[128,1024]{1,0:T(8,128)(2,1)} %get-tuple-element.9.refs_0_), channel_id=1, source_target_pairs={{0,4},{4,0},{8,12},{12,8},{1,5},{5,1},{9,13},{13,9},{2,6},{6,2},{1... | collective-permute-start | bytes 786440 | tf_op jit(solution)/shard_map/ppermute | solution.py:35
  7.4 32.1 %collective-permute-start.8 = (bf16[1024,256]{1,0:T(8,128)(2,1)}, bf16[1024,256]{1,0:T(8,128)(2,1)S(1)}, u32[]{:S(2)}, u32[]{:S(2)}) collective-permute-start(bf16[1024,256]{1,0:T(8,128)(2,1)} %get-tuple-element.10.refs_4_), channel_id=1, source_target_pairs={{0,1},{1,0},{2,3},{3,2},{4,5},{5,4},{6,7},{7,6},{8,9},{9,8},{10,11... | collective-permute-start | bytes 1572872 | tf_op jit(solution)/shard_map/ppermute | solution.py:35
  10.8 28.7 %collective-permute-start.9 = (bf16[1024,256]{1,0:T(8,128)(2,1)}, bf16[1024,256]{1,0:T(8,128)(2,1)S(1)}, u32[]{:S(2)}, u32[]{:S(2)}) collective-permute-start(bf16[1024,256]{1,0:T(8,128)(2,1)} %get-tuple-element.10.refs_4_), channel_id=1, source_target_pairs={{0,2},{1,3},{2,0},{3,1},{4,6},{5,7},{6,4},{7,5},{8,10},{9,11},{10,... | collective-permute-start | bytes 1572872 | tf_op jit(solution)/shard_map/ppermute | solution.py:35
  15.4 27.4 %collective-permute-start.10 = (bf16[1024,256]{1,0:T(8,128)(2,1)}, bf16[1024,256]{1,0:T(8,128)(2,1)S(1)}, u32[]{:S(2)}, u32[]{:S(2)}) collective-permute-start(bf16[1024,256]{1,0:T(8,128)(2,1)} %get-tuple-element.10.refs_4_), channel_id=1, source_target_pairs={{0,3},{1,2},{2,1},{3,0},{4,7},{5,6},{6,5},{7,4},{8,11},{9,10},{10,... | collective-permute-start | bytes 1572872 | tf_op jit(solution)/shard_map/ppermute | solution.py:35
  17.8 21.6 %collective-permute-start.6 = (bf16[128,1024]{1,0:T(8,128)(2,1)}, bf16[128,1024]{1,0:T(8,128)(2,1)S(1)}, u32[]{:S(2)}, u32[]{:S(2)}) collective-permute-start(bf16[128,1024]{1,0:T(8,128)(2,1)} %get-tuple-element.9.refs_0_), channel_id=1, source_target_pairs={{0,8},{4,12},{8,0},{12,4},{1,9},{5,13},{9,1},{13,5},{2,10},{6,14},... | collective-permute-start | bytes 786440 | tf_op jit(solution)/shard_map/ppermute | solution.py:35
  23.0 16.4 %collective-permute-start.7 = (bf16[128,1024]{1,0:T(8,128)(2,1)}, bf16[128,1024]{1,0:T(8,128)(2,1)S(1)}, u32[]{:S(2)}, u32[]{:S(2)}) collective-permute-start(bf16[128,1024]{1,0:T(8,128)(2,1)} %get-tuple-element.9.refs_0_), channel_id=1, source_target_pairs={{0,12},{4,8},{8,4},{12,0},{1,13},{5,9},{9,5},{13,1},{2,14},{6,10},... | collective-permute-start | bytes 786440 | tf_op jit(solution)/shard_map/ppermute | solution.py:35
  42.8 1.0 copy-start.4
  43.9 0.9 copy-start.5
  44.8 11.4 %copy-start.1 = (bf16[128,2048]{1,0:T(8,128)(2,1)S(1)}, bf16[128,2048]{1,0:T(8,128)(2,1)}, u32[]{:S(2)}) copy-start(bf16[128,2048]{1,0:T(8,128)(2,1)} %weight_ref.1) | copy-start | bytes 1572868
  56.6 20.5 %copy-start.7 = (bf16[2,2048]{1,0:T(2,128)(2,1)S(1)}, bf16[2,2048]{1,0:T(2,128)(2,1)}, u32[]{:S(2)}) copy-start(bf16[2,2048]{1,0:T(2,128)(2,1)} %param.21) | copy-start | bytes 24580
  77.8 13.4 %all-to-all-start = ((bf16[16,2,2048]{2,1,0:T(2,128)(2,1)}), bf16[16,2,2048]{2,1,0:T(2,128)(2,1)S(1)}, u32[]{:S(2)}, u32[]{:S(2)}) async-start(bf16[16,2,2048]{2,1,0:T(2,128)(2,1)} %broadcast_in_dim.2), calls=%async_computation | async-start | bytes 262144 | tf_op jit(solution)/shard_map/all_to_all | solution.py:39
  91.2 3.7 %copy-start.2 = (bf16[2048,128]{1,0:T(8,128)(2,1)S(1)}, bf16[2048,128]{1,0:T(8,128)(2,1)}, u32[]{:S(2)}) copy-start(bf16[2048,128]{1,0:T(8,128)(2,1)} %key_ref.2) | copy-start | bytes 1572868
  91.2 3.7 %copy-start.3 = (bf16[2048,128]{1,0:T(8,128)(2,1)S(1)}, bf16[2048,128]{1,0:T(8,128)(2,1)}, u32[]{:S(2)}) copy-start(bf16[2048,128]{1,0:T(8,128)(2,1)} %value_ref.2) | copy-start | bytes 1572868
  91.2 45.1 %all-to-all-start.3 = ((bf16[16,8,2048]{2,1,0:T(8,128)(2,1)}), bf16[16,8,2048]{2,1,0:T(8,128)(2,1)S(1)}, u32[]{:S(2)}, u32[]{:S(2)}) async-start(bf16[16,8,2048]{2,1,0:T(8,128)(2,1)} %get-tuple-element.11), calls=%async_computation.3 | async-start | bytes 1048576 | tf_op jit(solution)/shard_map/all_to_all | solution.py:39
  95.2 10.9 %collective-permute-start = (bf16[32,256]{1,0:T(8,128)(2,1)S(1)}, bf16[32,256]{1,0:T(8,128)(2,1)S(1)}, u32[]{:S(2)}, u32[]{:S(2)}) collective-permute-start(bf16[32,256]{1,0:T(8,128)(2,1)S(1)} %decode_pairs.1), channel_id=1, source_target_pairs={{0,32},{32,0},{64,96},{96,64},{1,33},{33,1},{65,97},{97,65},{2,34}... | collective-permute-start | bytes 49160 | tf_op jit(solution)/shard_map/ppermute | solution.py:35
  106.1 12.4 %collective-permute-start.1 = (bf16[64,256]{1,0:T(8,128)(2,1)S(1)}, bf16[64,256]{1,0:T(8,128)(2,1)S(1)}, u32[]{:S(2)}, u32[]{:S(2)}) collective-permute-start(bf16[64,256]{1,0:T(8,128)(2,1)S(1)} %pad_maximum_fusion.2), channel_id=1, source_target_pairs={{0,96},{32,64},{64,32},{96,0},{1,97},{33,65},{65,33},{97,1},{2,98}... | collective-permute-start | bytes 98312 | tf_op jit(solution)/shard_map/ppermute | solution.py:35
  118.5 6.1 %collective-permute-start.2 = (bf16[128,256]{1,0:T(8,128)(2,1)S(1)}, bf16[128,256]{1,0:T(8,128)(2,1)S(1)}, u32[]{:S(2)}, u32[]{:S(2)}) collective-permute-start(bf16[128,256]{1,0:T(8,128)(2,1)S(1)} %pad_maximum_fusion.1), channel_id=1, source_target_pairs={{0,128},{128,0},{256,384},{384,256},{1,129},{129,1},{257,385},{385... | collective-permute-start | bytes 196616 | tf_op jit(solution)/shard_map/ppermute | solution.py:35
  124.7 8.1 %collective-permute-start.3 = (bf16[256,256]{1,0:T(8,128)(2,1)S(1)}, bf16[256,256]{1,0:T(8,128)(2,1)S(1)}, u32[]{:S(2)}, u32[]{:S(2)}) collective-permute-start(bf16[256,256]{1,0:T(8,128)(2,1)S(1)} %pad_maximum_fusion), channel_id=1, source_target_pairs={{0,384},{128,256},{256,128},{384,0},{1,385},{129,257},{257,129},{3... | collective-permute-start | bytes 393224 | tf_op jit(solution)/shard_map/ppermute | solution.py:35
  126.9 9.4 %copy-start.6 = (bf16[2048,128]{1,0:T(8,128)(2,1)S(1)}, bf16[2048,128]{1,0:T(8,128)(2,1)}, u32[]{:S(2)}) copy-start(bf16[2048,128]{1,0:T(8,128)(2,1)} %param.22) | copy-start | bytes 1572868
  132.8 3.4 %collective-permute-start.4 = (bf16[512,256]{1,0:T(8,128)(2,1)S(1)}, bf16[512,256]{1,0:T(8,128)(2,1)S(1)}, u32[]{:S(2)}, u32[]{:S(2)}) collective-permute-start(bf16[512,256]{1,0:T(8,128)(2,1)S(1)} %get-tuple-element.13), channel_id=1, source_target_pairs={{0,16},{16,0},{1,17},{17,1},{2,18},{18,2},{3,19},{19,3},{4,20},{20... | collective-permute-start | bytes 786440 | tf_op jit(solution)/shard_map/ppermute | solution.py:35
